TPU v7x, 32 devices: a whole 2x2x4 slice. The times are simulated.
32 devices in a mesh: cuts: 2 (over x), row: 16 (over z, y, core).
Axes of the slice: x: 2, y: 2, z: 4, core: 2. Of those that a mesh axis runs over, the one named last changes fastest.
Arguments:
- raw: bfloat16 [2, 3, 5, 1024, 1024], P('cuts', None, None, 'row'), may hold values from -6 to 6
- otf: float32 [2, 1024, 1024], P('cuts', 'row'), may hold values from 0.0135 to 121.5, as said below
- offsets: int32 [3, 2], replicated, may hold values from -256 to 255
- phase_order: int32 [3, 5], replicated, may hold values from 0 to 4, each once within a row
- unmix: float32 [2, 3, 5, 5], replicated, may hold values from -3 to 3
Outputs:
- recon: float32 [2, 1024, 1024], P('cuts', 'row')
Inputs may be any that keep to these rules, and one draw needn't show every extreme that they name: `otf`: positive.
All inputs are finite; a program needn't handle non-finite values.
Results may differ from a plain program's by a relative error of at most 0.0072.
Values may be sent and summed in bfloat16 or wider, within the bound.
No kernel may reach another device: no remote copies, remote signals or barrier semaphores. Data moves between devices by JAX's collectives and lax.ppermute only.
A program may use at most 128 MiB of HBM per device.

v0:
```python
import functools
import math

import jax
import jax.numpy as jnp
from jax import lax
from jax.experimental import pallas as pl
from jax.experimental.pallas import tpu as pltpu
from jax.sharding import PartitionSpec as P

MULTIPLES = (0, 1, -1, 2, -2)
WIENER = 0.1
LANES = 128
GROUP = 16


def tables(pixels):
    fine = 1 << (max(pixels.bit_length() - 1, 0) // 2)
    coarse = pixels // fine
    rows = jnp.arange(pixels, dtype=jnp.int32)[:, None]
    step = 2.0 * math.pi / pixels

    def angle(columns):
        return (rows * columns[None, :] % pixels).astype(jnp.float32) * step

    high = angle(jnp.arange(coarse, dtype=jnp.int32) * fine)
    low = angle(jnp.arange(fine, dtype=jnp.int32))
    factor = 1.0 / math.sqrt(pixels)
    high_cos, high_sin, low_cos, low_sin = lax.optimization_barrier(
        (jnp.cos(high) * factor, jnp.sin(high) * factor, jnp.cos(low), jnp.sin(low))
    )
    high_cos, high_sin = (high_cos[:, :, None], high_sin[:, :, None])
    low_cos, low_sin = (low_cos[:, None, :], low_sin[:, None, :])
    cosine = (high_cos * low_cos - high_sin * low_sin).reshape(pixels, pixels)
    sine = (high_sin * low_cos + high_cos * low_sin).reshape(pixels, pixels)
    return lax.optimization_barrier((cosine.astype(jnp.bfloat16), sine.astype(jnp.bfloat16)))


def mixing(unmix, phase_order):
    phases = unmix.shape[-1]
    onehot = (phase_order[:, :, None] == jnp.arange(phases, dtype=jnp.int32)[None, None, :]).astype(
        jnp.float32
    )
    mixed = jnp.sum(unmix[:, :, :, None, :] * onehot[None, :, None, :, :], axis=-1)
    return (mixed[0], mixed[1])


def band_kernel(angles, phases, shift_ref, raw_ref, cos_ref, sin_ref, coef_ref, out_ref, spec):
    frames = angles * phases
    slab = out_ref.shape[3] // 2
    pixels = raw_ref.shape[1]
    quarter = out_ref.shape[4]
    tile = 256

    @pl.loop(0, pixels // tile)
    def _(step):
        cut = pl.ds(pl.multiple_of(step * tile, tile), tile)
        spec[0, :, cut] = jnp.dot(raw_ref[...], cos_ref[:, cut], preferred_element_type=jnp.float32)
        spec[1, :, cut] = jnp.dot(raw_ref[...], sin_ref[:, cut], preferred_element_type=jnp.float32)

    def combine(rows, terms):
        real = imag = None
        for frame, column in terms:
            here = pl.ds(pl.multiple_of(frame * slab + rows, GROUP), GROUP)
            cosine_sum = spec[0, here, :]
            sine_sum = spec[1, here, :]
            weights = coef_ref[pl.ds(pl.multiple_of(rows, GROUP), GROUP), :]
            weight_re = weights[:, column : column + 1]
            weight_im = weights[:, column + 1 : column + 2]
            add_re = weight_re * cosine_sum + weight_im * sine_sum
            add_im = weight_im * cosine_sum - weight_re * sine_sum
            real = add_re if real is None else real + add_re
            imag = add_im if imag is None else imag + add_im
        return real, imag

    def store(band, rows, real, imag):
        for part, value in enumerate((real, imag)):
            value = value.astype(jnp.bfloat16)
            here = pl.ds(pl.multiple_of(part * slab + rows, GROUP), GROUP)
            for cut in range(4):
                out_ref[cut // 2, cut % 2, band, here, :] = value[
                    :, cut * quarter : (cut + 1) * quarter
                ]

    @pl.loop(0, slab // GROUP)
    def _(step):
        rows = step * GROUP
        terms = [(frame, 2 * frame) for frame in range(frames)]
        real, imag = combine(rows, terms)
        store(0, rows, real, imag)
        band = 0
        for which in range(angles):
            for multiple in range(1, len(MULTIPLES)):
                band += 1
                column = 2 * (frames + (band - 1) * phases)
                terms = [(which * phases + j, column + 2 * j) for j in range(phases)]
                real, imag = combine(rows, terms)
                shift = shift_ref[band]
                store(band, rows, pltpu.roll(real, shift, 1), pltpu.roll(imag, shift, 1))


def numer_kernel(
    slab, bands, angles, with_power, place_ref, row_ref, col_ref, pow_ref, own_ref, other_ref,
    lhs_ref, *rest
):
    pieces = rest[: len(rest) - (4 if with_power else 3)]
    rest = rest[len(pieces) :]
    out_ref = rest[0]
    power_ref = rest[1] if with_power else None
    wide, total = rest[-2:]
    pixels = lhs_ref.shape[1]
    lane_tiles = pixels // LANES
    extra = wide.shape[1] - pixels
    width = own_ref.shape[-1]
    tile = extra

    for index, piece in enumerate(pieces):
        start = pl.multiple_of(place_ref[index] * slab, slab)
        for lane in range(lane_tiles):
            wide[lane, pl.ds(start, slab), :] = piece[:, lane * LANES : (lane + 1) * LANES].astype(
                jnp.float32
            )
    for lane in range(lane_tiles):
        wide[lane, pixels : pixels + extra, :] = wide[lane, 0:extra, :]

    total[...] = jnp.zeros_like(total)

    def response(q0, band, column, count):
        start = (q0 + row_ref[band]) & (pixels - 1)
        rest_lanes = column & (LANES - 1)
        first = column // LANES
        turn = (LANES - rest_lanes) & (LANES - 1)
        lane = lax.broadcasted_iota(jnp.int32, (tile, LANES), 1)
        turned = [
            pltpu.roll(wide[(first + i) & (lane_tiles - 1), pl.ds(start, tile), :], turn, 1)
            for i in range(count + 1)
        ]
        return [
            jnp.where(lane < LANES - rest_lanes, turned[i], turned[i + 1]) for i in range(count)
        ]

    half = place_ref[len(pieces)]
    tiles = width // LANES

    @pl.loop(0, bands)
    def _(band):
        right = jnp.concatenate([own_ref[half, band], other_ref[0, band]], axis=0)

        @pl.loop(0, pixels // tile)
        def _(step):
            q0 = pl.multiple_of(step * tile, tile)
            weights = response(q0, band, col_ref[band], tiles)
            for part in range(2):
                product = jnp.dot(
                    lhs_ref[part, pl.ds(q0, tile), :], right, preferred_element_type=jnp.float32
                )
                for i in range(tiles):
                    total[part, pl.ds(q0, tile), i * LANES : (i + 1) * LANES] += (
                        weights[i] * product[:, i * LANES : (i + 1) * LANES]
                    )

    blocks = out_ref.shape[0]
    columns = width // blocks

    @pl.loop(0, pixels // tile)
    def _(step):
        q0 = pl.multiple_of(step * tile, tile)
        for block in range(blocks):
            cut = slice(block * columns, (block + 1) * columns)
            out_ref[block, pl.ds(q0, tile), :] = jnp.concatenate(
                [total[0, pl.ds(q0, tile), cut], total[1, pl.ds(q0, tile), cut]], axis=1
            ).astype(jnp.bfloat16)
        if with_power:
            gathered = None
            for band in range(bands):
                value = response(q0, band, pow_ref[band], 1)[0]
                value = value * value
                if band == 0:
                    gathered = value * float(angles)
                else:
                    gathered = gathered + value
            power_ref[pl.ds(q0, tile), :] = jnp.concatenate(
                [gathered[:, :columns], gathered[:, :columns]], axis=1
            )


def smem():
    return pl.BlockSpec(memory_space=pltpu.SMEM)


def vmem():
    return pl.BlockSpec(memory_space=pltpu.VMEM)


def swap(value, axis, mask):
    size = lax.axis_size(axis)
    return lax.ppermute(value, axis, [(i, i ^ mask) for i in range(size)])


def shards(raw, otf, offsets, phase_order, unmix):
    pixels = raw.shape[-1]
    slab = raw.shape[3]
    angles, phases = raw.shape[1:3]
    devices = lax.axis_size("row")
    index = lax.axis_index("row")
    slices = raw.shape[0] * lax.axis_size("cuts")
    chips = devices // 2
    levels = chips.bit_length() - 1
    core = index & 1
    chip = index >> 1
    columns = pixels // devices
    frames = angles * phases
    steps = len(MULTIPLES) - 1
    bands = 1 + angles * steps
    place = sum(((chip >> bit) & 1) << (levels - 1 - bit) for bit in range(levels))

    mine = otf.reshape(slab, pixels).astype(jnp.bfloat16)
    pieces = {0: mine}
    for mask in range(4, devices, 4):
        pieces[mask] = swap(mine, "row", mask)
    for mask in range(0, devices, 4):
        pieces[mask | 2] = swap(pieces[mask], "row", 2)
    for mask in range(0, devices, 2):
        pieces[mask | 1] = swap(pieces[mask], "row", 1)

    cosine, sine = tables(pixels)
    mix_re, mix_im = mixing(unmix, phase_order)
    factors = jnp.array(MULTIPLES[1:], dtype=jnp.int32)
    row_shift = (factors[None, :] * offsets[:, 0:1]).reshape(-1)
    col_shift = (factors[None, :] * offsets[:, 1:2]).reshape(-1)
    zero = jnp.zeros((1,), jnp.int32)
    row_all = jnp.concatenate([zero, row_shift])
    col_all = jnp.concatenate([zero, col_shift])

    def own_rows(which):
        return which * slab + jnp.arange(slab, dtype=jnp.int32)

    turn = (own_rows(index)[:, None] * row_shift[None, :]) & (pixels - 1)
    turn = turn.astype(jnp.float32) * (2.0 * math.pi / pixels)
    turn_re = jnp.cos(turn)[:, :, None]
    turn_im = jnp.sin(turn)[:, :, None]
    rest_re = mix_re[:, 1:].reshape(1, bands - 1, phases)
    rest_im = mix_im[:, 1:].reshape(1, bands - 1, phases)
    coef_re = (rest_re * turn_re - rest_im * turn_im).reshape(slab, -1)
    coef_im = (rest_re * turn_im + rest_im * turn_re).reshape(slab, -1)
    plain_re = jnp.broadcast_to(mix_re[:, 0].reshape(1, frames), (slab, frames))
    plain_im = jnp.broadcast_to(mix_im[:, 0].reshape(1, frames), (slab, frames))
    coef = jnp.stack(
        [
            jnp.concatenate([plain_re, coef_re], axis=1),
            jnp.concatenate([plain_im, coef_im], axis=1),
        ],
        axis=2,
    ).reshape(slab, -1)

    quarter = pixels // 4
    band_flops = 2 * frames * slab * pixels * 2 * pixels
    packed = pl.pallas_call(
        functools.partial(band_kernel, angles, phases),
        out_shape=jax.ShapeDtypeStruct((2, 2, bands, 2 * slab, quarter), jnp.bfloat16),
        in_specs=[smem(), vmem(), vmem(), vmem(), vmem()],
        out_specs=vmem(),
        scratch_shapes=[pltpu.VMEM((2, frames * slab, pixels), jnp.float32)],
        cost_estimate=pl.CostEstimate(
            flops=2 * band_flops, bytes_accessed=12 << 20, transcendentals=0
        ),
        name="bands",
    )(col_all & (pixels - 1), raw.reshape(frames * slab, pixels), cosine, sine, coef)

    near = chip & 1
    here = lax.dynamic_index_in_dim(packed, core, 0, keepdims=False)
    there = lax.dynamic_index_in_dim(packed, 1 - core, 0, keepdims=False)
    got = [
        swap(lax.dynamic_slice_in_dim(there, half, 1, 0), "row", 1) for half in (1 - near, near)
    ]

    def table_rows(which):
        cut = which * slab
        return (
            lax.dynamic_slice_in_dim(cosine, cut, slab, 0),
            lax.dynamic_slice_in_dim(sine, cut, slab, 0),
        )

    cos_own, sin_own = table_rows(index)
    cos_other, sin_other = table_rows(index ^ 1)
    left = jnp.stack(
        [
            jnp.concatenate([cos_own, sin_own, cos_other, sin_other], axis=0).T,
            jnp.concatenate([-sin_own, cos_own, -sin_other, cos_other], axis=0).T,
        ]
    )
    masks = sorted(pieces)
    tile = 128

    def partial(half, other, with_power):
        start = core * (pixels // 2) + half * quarter
        places = jnp.stack([index ^ mask for mask in masks] + [half])
        row_base = (-row_all) & (pixels - 1)
        col_base = (start - col_all) & (pixels - 1)
        own_start = core * (pixels // 2) + place * columns
        pow_base = (own_start - col_all) & (pixels - 1)
        out_shape = [jax.ShapeDtypeStruct((chips // 2, pixels, 2 * columns), jnp.bfloat16)]
        if with_power:
            out_shape.append(jax.ShapeDtypeStruct((pixels, 2 * columns), jnp.float32))
        return pl.pallas_call(
            functools.partial(numer_kernel, slab, bands, angles, with_power),
            out_shape=out_shape,
            in_specs=[smem()] * 4 + [vmem()] * (3 + len(masks)),
            out_specs=[vmem()] * len(out_shape),
            scratch_shapes=[
                pltpu.VMEM((pixels // LANES, pixels + tile, LANES), jnp.float32),
                pltpu.VMEM((2, pixels, quarter), jnp.float32),
            ],
            cost_estimate=pl.CostEstimate(
                flops=16 * bands * slab * pixels * quarter, bytes_accessed=8 << 20, transcendentals=0
            ),
            name="own" if with_power else "away",
        )(places, row_base, col_base, pow_base, here, other, left, *[pieces[m] for m in masks])

    (away,) = partial(1 - near, got[0], False)
    kept, power = partial(near, got[1], True)

    def split(blocks, bit):
        count = blocks.shape[0] // 2
        side = (chip >> bit) & 1
        return (
            lax.dynamic_slice_in_dim(blocks, (1 - side) * count, count, 0),
            lax.dynamic_slice_in_dim(blocks, side * count, count, 0),
        )

    def widen(value):
        return value.astype(jnp.float32)

    far, stay = [swap(part, "row", 2) for part in split(away, 1)]
    kept_far, kept_stay = split(kept, 1)
    far = widen(far) + widen(kept_far)
    stay = widen(stay) + widen(kept_stay)
    for bit in range(1, levels):
        got_next = swap(far.astype(jnp.bfloat16), "row", 2 << bit)
        stay = stay + widen(got_next)
        if bit < levels - 1:
            far, stay = split(stay, bit + 1)
    numer = stay[0]

    total_power = power
    moving = power
    cuts = lax.axis_size("cuts")
    for _ in range(cuts - 1):
        moving = lax.ppermute(moving, "cuts", [(i, (i + 1) % cuts) for i in range(cuts)])
        total_power = total_power + moving
    denom = WIENER + total_power / (slices * angles)
    ratio = (numer / denom).astype(jnp.bfloat16)

    by_cos = jnp.dot(cosine, ratio, preferred_element_type=jnp.float32)
    by_sin = jnp.dot(sine, ratio, preferred_element_type=jnp.float32)
    half = jnp.concatenate(
        [
            by_cos[:, :columns] - by_sin[:, columns:],
            by_cos[:, columns:] + by_sin[:, :columns],
        ],
        axis=1,
    ).astype(jnp.bfloat16)
    back = lax.all_to_all(
        half.reshape(devices, slab, 2 * columns), "row", split_axis=0, concat_axis=0, tiled=True
    )
    back = jnp.swapaxes(back, 0, 1).reshape(slab, devices * 2 * columns)

    def by_owner(table):
        table = table.reshape((2,) + (2,) * levels + (columns, pixels))
        order = tuple(range(levels, 0, -1)) + (0, levels + 1, levels + 2)
        return jnp.transpose(table, order).reshape(devices, columns, pixels)

    final = jnp.concatenate([by_owner(cosine), -by_owner(sine)], axis=1).reshape(-1, pixels)
    recon = jnp.dot(back, final, preferred_element_type=jnp.float32)
    return recon.reshape(otf.shape)


def solution(mesh):
    in_specs = (P("cuts", None, None, "row", None), P("cuts", "row", None), P(), P(), P())
    out_specs = P("cuts", "row", None)
    return jax.shard_map(shards, mesh=mesh, in_specs=in_specs, out_specs=out_specs, check_vma=False)
```

profile of v0, /device:TPU:0, one launch (start us, length us, event | category | flops | bytes accessed | tf_op | source)
XLA Modules:
  0.0 185.2 jit_solution(17432347195164153077)
XLA Ops:
  0.0 0.5 fusion.24
  0.5 0.8 fusion.25
  1.3 0.9 multiply_reduce_fusion
  2.2 0.2 copy.34
  2.4 0.2 copy.32
  2.7 1.0 sine_multiply_fusion
  3.7 2.6 %add_convert_fusion = (bf16[1024,32,32]{0,2,1:T(8,128)(2,1)S(1)}, bf16[1024,32,32]{0,2,1:T(8,128)(2,1)}) fusion(f32[1024,32]{0,1:T(8,128)S(1)} %get-tuple-element.16, f32[1024,32]{0,1:T(8,128)S(1)} %get-tuple-element.15, f32[1024,32]{0,1:T(8,128)S(1)} %fusion.24, f32[1024,32]{0,1:T(8,128)S(1)} %get-tuple-element.13), kind=kLoop, calls=%fused_computation.4 | loop fusion | flops 8388608 | bytes 4718592 | tf_op jit(solution)/shard_map/convert_element_type | solution.py:36
  7.4 0.7 copy.41.coef_ref
  8.2 4.0 %copy.39.cos_ref = bf16[1024,1024]{1,0:T(8,128)(2,1)} copy(bf16[1024,1024]{0,1:T(8,128)(2,1)} %bitcast.85) | data formatting | bytes 4194304 | tf_op jit(solution)/shard_map/optimization_barrier | solution.py:36
  12.2 2.6 %copy.40.sin_ref = bf16[1024,1024]{1,0:T(8,128)(2,1)} copy(bf16[1024,1024]{0,1:T(8,128)(2,1)S(1)} %bitcast.81) | data formatting | bytes 4194304 | tf_op jit(solution)/shard_map/optimization_barrier | solution.py:36
  14.8 0.7 subtract_and_fusion.2
  15.5 19.3 %bands.1 = bf16[2,2,13,128,256]{4,3,2,1,0:T(8,128)(2,1)} custom-call(s32[13]{0:T(128)} %get-tuple-element.49.shift_ref, bf16[960,1024]{1,0:T(8,128)(2,1)} %bitcast.98, bf16[1024,1024]{1,0:T(8,128)(2,1)} %copy.39.cos_ref, bf16[1024,1024]{1,0:T(8,128)(2,1)} %copy.40.sin_ref, f32[64,150]{1,0:T(8,128)} %copy.41.coef_ref), custom_call_target="tpu_custom_call" | custom-call | flops 8053063680 | bytes 12582912 | tf_op jit(solution)/shard_map/bands/pallas_call | solution.py:258
  34.8 2.8 %dynamic-slice_bitcast_fusion.2 = (bf16[1,13,128,256]{3,2,1,0:T(8,128)(2,1)}, bf16[1,13,128,256]{3,2,1,0:T(8,128)(2,1)}) fusion(bf16[2,2,13,128,256]{4,3,2,1,0:T(8,128)(2,1)} %bands.1, s32[]{:T(128)S(6)} %select_n.60, s32[]{:T(128)S(6)} %select_n.62, s32[]{:T(128)S(6)} %select_n.67), kind=kLoop, calls=%fused_computation.12 | loop fusion | bytes 3407884 | tf_op jit(solution)/shard_map/dynamic_slice | solution.py:274
  37.6 0.5 collective-permute-start
  38.1 3.6 %collective-permute-start.8 = (bf16[64,1024]{1,0:T(8,128)(2,1)S(1)}, bf16[64,1024]{1,0:T(8,128)(2,1)S(1)}, u32[]{:S(2)}, u32[]{:S(2)}) collective-permute-start(bf16[64,1024]{1,0:T(8,128)(2,1)S(1)} %convert_bitcast_fusion.rest_0_), channel_id=1, source_target_pairs={{0,8},{1,9},{2,10},{3,11},{4,12},{5,13},{6,14},{7,15},{8,0},{9,1},... | collective-permute-start | bytes 393224 | tf_op jit(solution)/shard_map/ppermute | solution.py:197
  41.8 1.3 collective-permute-start.12
  43.1 0.2 collective-permute-start.4
  43.4 1.5 collective-permute-start.2
  44.9 2.9 %dynamic-slice_bitcast_fusion.own_ref = bf16[2,13,128,256]{3,2,1,0:T(8,128)(2,1)} fusion(bf16[2,2,13,128,256]{4,3,2,1,0:T(8,128)(2,1)} %bands.1, s32[]{:T(128)S(6)} %select_n.58), kind=kLoop, calls=%fused_computation.6 | loop fusion | bytes 3407876 | tf_op jit(solution)/shard_map/jit(dynamic_index_in_dim)/squeeze | solution.py:271
  47.7 4.1 %collective-permute-done.8.rest_8_ = bf16[64,1024]{1,0:T(8,128)(2,1)S(1)} collective-permute-done((bf16[64,1024]{1,0:T(8,128)(2,1)S(1)}, bf16[64,1024]{1,0:T(8,128)(2,1)S(1)}, u32[]{:S(2)}, u32[]{:S(2)}) %collective-permute-start.8) | collective-permute-done | bytes 131104 | tf_op jit(solution)/shard_map/ppermute | solution.py:197
  51.8 1.9 %collective-permute-start.10 = (bf16[64,1024]{1,0:T(8,128)(2,1)S(1)}, bf16[64,1024]{1,0:T(8,128)(2,1)S(1)}, u32[]{:S(2)}, u32[]{:S(2)}) collective-permute-start(bf16[64,1024]{1,0:T(8,128)(2,1)S(1)} %collective-permute-done.8.rest_8_), channel_id=1, source_target_pairs={{0,2},{1,3},{2,0},{3,1},{4,6},{5,7},{6,4},{7,5},{8,10},{9,11},{10,... | collective-permute-start | bytes 393224 | tf_op jit(solution)/shard_map/ppermute | solution.py:197
  53.7 0.9 collective-permute-start.14
  54.6 1.1 collective-permute-start.6
  55.7 0.3 fusion.31
  56.0 1.3 constant_dynamic-slice_fusion.5
  57.4 0.9 collective-permute-done.10.rest_10_
  58.3 2.8 %collective-permute-done.14.rest_14_ = bf16[64,1024]{1,0:T(8,128)(2,1)S(1)} collective-permute-done((bf16[64,1024]{1,0:T(8,128)(2,1)S(1)}, bf16[64,1024]{1,0:T(8,128)(2,1)S(1)}, u32[]{:S(2)}, u32[]{:S(2)}) %collective-permute-start.14) | collective-permute-done | bytes 131104 | tf_op jit(solution)/shard_map/ppermute | solution.py:197
  61.1 2.4 %collective-permute-done.6.rest_6_ = bf16[64,1024]{1,0:T(8,128)(2,1)S(1)} collective-permute-done((bf16[64,1024]{1,0:T(8,128)(2,1)}, bf16[64,1024]{1,0:T(8,128)(2,1)S(1)}, u32[]{:S(2)}, u32[]{:S(2)}) %collective-permute-start.6) | collective-permute-done | bytes 131104 | tf_op jit(solution)/shard_map/ppermute | solution.py:197
  63.5 0.6 copy-done.12
  64.1 0.7 maximum_bitcast_fusion
  64.8 0.6 copy-done.13
  65.5 0.7 fusion.29.row_ref
  66.1 0.6 stack.111.place_ref
  66.8 0.5 collective-permute-start.11
  67.4 0.4 collective-permute-start.7
  67.8 1.1 pad_maximum_fusion.lhs_ref
  68.9 0.3 collective-permute-done.7.rest_7_
  69.2 0.4 copy-done.14
  69.6 25.4 %away.1 = bf16[4,1024,128]{2,1,0:T(8,128)(2,1)} custom-call(s32[17]{0:T(128)} %stack.111.place_ref, s32[13]{0:T(128)} %fusion.29.row_ref, s32[13]{0:T(128)} %get-tuple-element.47.col_ref, s32[13]{0:T(128)} %get-tuple-element.48.pow_ref, bf16[2,13,128,256]{3,2,1,0:T(8,128)(2,1)} %dynamic-slice_bitcast_fusion.own_ref, ...), custom_call_target="tpu_custom_call" | custom-call | flops 3489660928 | bytes 8388608 | tf_op jit(solution)/shard_map/away/pallas_call | solution.py:305
  95.0 2.1 %constant_dynamic-slice_fusion.1 = (bf16[2,1024,128]{2,1,0:T(8,128)(2,1)}, bf16[2,1024,128]{2,1,0:T(8,128)(2,1)S(1)}) fusion(bf16[4,1024,128]{2,1,0:T(8,128)(2,1)} %away.1, s32[]{:T(128)S(6)} %select_n.65, s32[]{:T(128)S(6)} %select_n.68), kind=kLoop, calls=%fused_computation.59 | loop fusion | bytes 2097160 | tf_op jit(solution)/shard_map/dynamic_slice | solution.py:328
  97.0 1.7 collective-permute-start.18
  98.8 0.6 stack.119.place_ref
  99.4 0.3 collective-permute-start.16
  99.7 29.7 %own.1 = (bf16[4,1024,128]{2,1,0:T(8,128)(2,1)}, f32[1024,128]{1,0:T(8,128)}) custom-call(s32[17]{0:T(128)} %stack.119.place_ref, s32[13]{0:T(128)} %fusion.29.row_ref, s32[13]{0:T(128)} %get-tuple-element.50.col_ref, s32[13]{0:T(128)} %get-tuple-element.48.pow_ref, bf16[2,13,128,256]{3,2,1,0:T(8,128)(2,1)} %dynamic-slice_bitcast_fusion.own_ref, ...), custom_call_target="tpu_custom_call" | custom-call | flops 3489660928 | bytes 8388608 | tf_op jit(solution)/shard_map/own/pallas_call | solution.py:305
  129.4 1.2 add_convert_fusion.1
  130.6 2.9 %collective-permute-start.19 = (bf16[2,1024,128]{2,1,0:T(8,128)(2,1)S(1)}, bf16[2,1024,128]{2,1,0:T(8,128)(2,1)}, u32[]{:S(2)}, u32[]{:S(2)}) collective-permute-start(bf16[2,1024,128]{2,1,0:T(8,128)(2,1)S(1)} %add_convert_fusion.1), channel_id=1, source_target_pairs={{0,4},{1,5},{2,6},{3,7},{4,0},{5,1},{6,2},{7,3},{8,12},{9,13},{10,... | collective-permute-start | bytes 1572872 | tf_op jit(solution)/shard_map/ppermute | solution.py:197
  133.5 1.5 collective-permute-start.21
  135.0 10.2 %collective-permute-done.19 = bf16[2,1024,128]{2,1,0:T(8,128)(2,1)} collective-permute-done((bf16[2,1024,128]{2,1,0:T(8,128)(2,1)S(1)}, bf16[2,1024,128]{2,1,0:T(8,128)(2,1)}, u32[]{:S(2)}, u32[]{:S(2)}) %collective-permute-start.19) | collective-permute-done | bytes 524320 | tf_op jit(solution)/shard_map/ppermute | solution.py:197
  145.2 1.5 convert_add_fusion
  146.7 0.7 dynamic-slice_convert_fusion
  147.4 3.7 %collective-permute-start.20 = (bf16[1,1024,128]{2,1,0:T(8,128)(2,1)}, bf16[1,1024,128]{2,1,0:T(8,128)(2,1)S(1)}, u32[]{:S(2)}, u32[]{:S(2)}) collective-permute-start(bf16[1,1024,128]{2,1,0:T(8,128)(2,1)} %dynamic-slice_convert_fusion), channel_id=1, source_target_pairs={{0,8},{1,9},{2,10},{3,11},{4,12},{5,13},{6,14},{7,15},{8,0},{9,1},... | collective-permute-start | bytes 786440 | tf_op jit(solution)/shard_map/ppermute | solution.py:197
  151.1 11.0 %collective-permute-done.20 = bf16[1,1024,128]{2,1,0:T(8,128)(2,1)S(1)} collective-permute-done((bf16[1,1024,128]{2,1,0:T(8,128)(2,1)}, bf16[1,1024,128]{2,1,0:T(8,128)(2,1)S(1)}, u32[]{:S(2)}, u32[]{:S(2)}) %collective-permute-start.20) | collective-permute-done | bytes 262176 | tf_op jit(solution)/shard_map/ppermute | solution.py:197
  162.1 1.3 fusion.7
  163.4 0.5 fusion.34
  163.9 0.5 fusion.35
  164.5 0.2 copy.49
  164.6 0.2 copy.50
  164.8 0.9 pad_maximum_fusion.1
  165.7 5.0 %all-to-all-start = ((bf16[16,64,128]{2,1,0:T(8,128)(2,1)}), bf16[16,64,128]{2,1,0:T(8,128)(2,1)S(1)}, u32[]{:S(2)}, u32[]{:S(2)}) async-start(bf16[16,64,128]{2,1,0:T(8,128)(2,1)} %pad_maximum_fusion.1), calls=%async_computation | async-start | bytes 524288 | tf_op jit(solution)/shard_map/all_to_all | solution.py:363
  170.7 1.8 neg.25
  172.5 4.0 %copy.46 = bf16[1024,1024]{1,0:T(8,128)(2,1)} copy(bf16[1024,1024]{0,1:T(8,128)(2,1)} %neg.25) | data formatting | bytes 4194304 | tf_op jit(solution)/shard_map/neg | solution.py:373
  176.5 3.3 %copy.47 = bf16[2,2,2,2,64,1024]{5,4,3,2,1,0:T(8,128)(2,1)} copy(bf16[2,2,2,2,64,1024]{5,4,0,1,2,3:T(8,128)(2,1)} %bitcast.89) | data formatting | bytes 4194304 | tf_op jit(solution)/shard_map/neg | solution.py:373
  179.8 1.6 copy.45
  181.4 3.8 %fusion.4 = f32[1,64,1024]{2,1,0:T(8,128)} fusion(bf16[16,64,1024]{2,1,0:T(8,128)(2,1)} %bitcast.90, bf16[16,64,1024]{2,1,0:T(8,128)(2,1)} %bitcast.91, bf16[16,64,128]{2,1,0:T(8,128)(2,1)S(1)} %all-to-all-done), kind=kOutput, calls=%fused_computation.7 | convolution fusion | flops 276824064 | bytes 4718592 | tf_op jit(solution)/shard_map/dot_general | solution.py:374
  (83 shorter events, 1.5 us)
Async XLA Ops:
  3.7 2.7 %copy-start.4 = (s32[3,2]{0,1:T(2,128)S(1)}, s32[3,2]{0,1:T(2,128)}, u32[]{:S(2)}) copy-start(s32[3,2]{0,1:T(2,128)} %param.8) | copy-start | bytes 76
  3.7 2.7 %copy-start.5 = (s32[4]{0:T(128)S(1)}, s32[4]{0:T(128)}, u32[]{:S(2)}) copy-start(s32[4]{0:T(128)} %constant.138.clone) | copy-start | bytes 52
  34.8 3.3 %copy-start.2 = (f32[1,64,1024]{2,1,0:T(8,128)S(1)}, f32[1,64,1024]{2,1,0:T(8,128)}, u32[]{:S(2)}) copy-start(f32[1,64,1024]{2,1,0:T(8,128)} %param.7) | copy-start | bytes 786436
  37.6 31.5 %collective-permute-start = (bf16[1,13,128,256]{3,2,1,0:T(8,128)(2,1)}, bf16[1,13,128,256]{3,2,1,0:T(8,128)(2,1)}, u32[]{:S(2)}, u32[]{:S(2)}) collective-permute-start(bf16[1,13,128,256]{3,2,1,0:T(8,128)(2,1)} %get-tuple-element.25), channel_id=1, source_target_pairs={{0,1},{1,0},{2,3},{3,2},{4,5},{5,4},{6,7},{7,6},{8,9},{9,8},{10,11... | collective-permute-start | bytes 2555912 | tf_op jit(solution)/shard_map/ppermute | solution.py:197
  38.1 17.9 %copy-start.3 = (bf16[64,1024]{1,0:T(8,128)(2,1)}, bf16[64,1024]{1,0:T(8,128)(2,1)S(1)}, u32[]{:S(2)}) copy-start(bf16[64,1024]{1,0:T(8,128)(2,1)S(1)} %convert_bitcast_fusion.rest_0_) | copy-start | bytes 393220
  38.1 13.7 %collective-permute-start.8 = (bf16[64,1024]{1,0:T(8,128)(2,1)S(1)}, bf16[64,1024]{1,0:T(8,128)(2,1)S(1)}, u32[]{:S(2)}, u32[]{:S(2)}) collective-permute-start(bf16[64,1024]{1,0:T(8,128)(2,1)S(1)} %convert_bitcast_fusion.rest_0_), channel_id=1, source_target_pairs={{0,8},{1,9},{2,10},{3,11},{4,12},{5,13},{6,14},{7,15},{8,0},{9,1},... | collective-permute-start | bytes 393224 | tf_op jit(solution)/shard_map/ppermute | solution.py:197
  41.8 10.0 %collective-permute-start.12 = (bf16[64,1024]{1,0:T(8,128)(2,1)S(1)}, bf16[64,1024]{1,0:T(8,128)(2,1)S(1)}, u32[]{:S(2)}, u32[]{:S(2)}) collective-permute-start(bf16[64,1024]{1,0:T(8,128)(2,1)S(1)} %convert_bitcast_fusion.rest_0_), channel_id=1, source_target_pairs={{0,12},{1,13},{2,14},{3,15},{4,8},{5,9},{6,10},{7,11},{8,4},{9,5},... | collective-permute-start | bytes 393224 | tf_op jit(solution)/shard_map/ppermute | solution.py:197
  43.1 10.6 %collective-permute-start.4 = (bf16[64,1024]{1,0:T(8,128)(2,1)S(1)}, bf16[64,1024]{1,0:T(8,128)(2,1)}, u32[]{:S(2)}, u32[]{:S(2)}) collective-permute-start(bf16[64,1024]{1,0:T(8,128)(2,1)S(1)} %convert_bitcast_fusion.rest_0_), channel_id=1, source_target_pairs={{0,4},{1,5},{2,6},{3,7},{4,0},{5,1},{6,2},{7,3},{8,12},{9,13},{10,... | collective-permute-start | bytes 393224 | tf_op jit(solution)/shard_map/ppermute | solution.py:197
  43.4 11.3 %collective-permute-start.2 = (bf16[64,1024]{1,0:T(8,128)(2,1)S(1)}, bf16[64,1024]{1,0:T(8,128)(2,1)}, u32[]{:S(2)}, u32[]{:S(2)}) collective-permute-start(bf16[64,1024]{1,0:T(8,128)(2,1)S(1)} %convert_bitcast_fusion.rest_0_), channel_id=1, source_target_pairs={{0,2},{1,3},{2,0},{3,1},{4,6},{5,7},{6,4},{7,5},{8,10},{9,11},{10,... | collective-permute-start | bytes 393224 | tf_op jit(solution)/shard_map/ppermute | solution.py:197
  51.8 13.0 %copy-start.6 = (bf16[64,1024]{1,0:T(8,128)(2,1)}, bf16[64,1024]{1,0:T(8,128)(2,1)S(1)}, u32[]{:S(2)}) copy-start(bf16[64,1024]{1,0:T(8,128)(2,1)S(1)} %collective-permute-done.8.rest_8_) | copy-start | bytes 393220
  51.8 5.5 %collective-permute-start.1 = (bf16[64,1024]{1,0:T(8,128)(2,1)S(1)}, bf16[64,1024]{1,0:T(8,128)(2,1)S(1)}, u32[]{:S(2)}, u32[]{:S(2)}) collective-permute-start(bf16[64,1024]{1,0:T(8,128)(2,1)S(1)} %convert_bitcast_fusion.rest_0_), channel_id=1, source_target_pairs={{0,1},{1,0},{2,3},{3,2},{4,5},{5,4},{6,7},{7,6},{8,9},{9,8},{10,11... | collective-permute-start | bytes 393224 | tf_op jit(solution)/shard_map/ppermute | solution.py:197
  51.8 13.0 %copy-start.7 = (bf16[64,1024]{1,0:T(8,128)(2,1)}, bf16[64,1024]{1,0:T(8,128)(2,1)S(1)}, u32[]{:S(2)}) copy-start(bf16[64,1024]{1,0:T(8,128)(2,1)S(1)} %collective-permute-done.12.rest_12_) | copy-start | bytes 393220
  51.8 6.4 %collective-permute-start.10 = (bf16[64,1024]{1,0:T(8,128)(2,1)S(1)}, bf16[64,1024]{1,0:T(8,128)(2,1)S(1)}, u32[]{:S(2)}, u32[]{:S(2)}) collective-permute-start(bf16[64,1024]{1,0:T(8,128)(2,1)S(1)} %collective-permute-done.8.rest_8_), channel_id=1, source_target_pairs={{0,2},{1,3},{2,0},{3,1},{4,6},{5,7},{6,4},{7,5},{8,10},{9,11},{10,... | collective-permute-start | bytes 393224 | tf_op jit(solution)/shard_map/ppermute | solution.py:197
  53.7 7.3 %collective-permute-start.14 = (bf16[64,1024]{1,0:T(8,128)(2,1)S(1)}, bf16[64,1024]{1,0:T(8,128)(2,1)S(1)}, u32[]{:S(2)}, u32[]{:S(2)}) collective-permute-start(bf16[64,1024]{1,0:T(8,128)(2,1)S(1)} %collective-permute-done.12.rest_12_), channel_id=1, source_target_pairs={{0,2},{1,3},{2,0},{3,1},{4,6},{5,7},{6,4},{7,5},{8,10},{9,11},{10,... | collective-permute-start | bytes 393224 | tf_op jit(solution)/shard_map/ppermute | solution.py:197
  54.6 8.8 %collective-permute-start.6 = (bf16[64,1024]{1,0:T(8,128)(2,1)}, bf16[64,1024]{1,0:T(8,128)(2,1)S(1)}, u32[]{:S(2)}, u32[]{:S(2)}) collective-permute-start(bf16[64,1024]{1,0:T(8,128)(2,1)} %collective-permute-done.4.rest_4_), channel_id=1, source_target_pairs={{0,2},{1,3},{2,0},{3,1},{4,6},{5,7},{6,4},{7,5},{8,10},{9,11},{10,... | collective-permute-start | bytes 393224 | tf_op jit(solution)/shard_map/ppermute | solution.py:197
  57.3 6.1 %copy-start.8 = (bf16[64,1024]{1,0:T(8,128)(2,1)}, bf16[64,1024]{1,0:T(8,128)(2,1)S(1)}, u32[]{:S(2)}) copy-start(bf16[64,1024]{1,0:T(8,128)(2,1)S(1)} %collective-permute-done.1.rest_1_) | copy-start | bytes 393220
  57.3 7.5 %collective-permute-start.13 = (bf16[64,1024]{1,0:T(8,128)(2,1)S(1)}, bf16[64,1024]{1,0:T(8,128)(2,1)S(1)}, u32[]{:S(2)}, u32[]{:S(2)}) collective-permute-start(bf16[64,1024]{1,0:T(8,128)(2,1)S(1)} %collective-permute-done.12.rest_12_), channel_id=1, source_target_pairs={{0,1},{1,0},{2,3},{3,2},{4,5},{5,4},{6,7},{7,6},{8,9},{9,8},{10,11... | collective-permute-start | bytes 393224 | tf_op jit(solution)/shard_map/ppermute | solution.py:197
  58.3 5.2 %copy-start.9 = (bf16[64,1024]{1,0:T(8,128)(2,1)}, bf16[64,1024]{1,0:T(8,128)(2,1)S(1)}, u32[]{:S(2)}) copy-start(bf16[64,1024]{1,0:T(8,128)(2,1)S(1)} %collective-permute-done.10.rest_10_) | copy-start | bytes 393220
  58.3 8.5 %collective-permute-start.5 = (bf16[64,1024]{1,0:T(8,128)(2,1)}, bf16[64,1024]{1,0:T(8,128)(2,1)}, u32[]{:S(2)}, u32[]{:S(2)}) collective-permute-start(bf16[64,1024]{1,0:T(8,128)(2,1)} %collective-permute-done.4.rest_4_), channel_id=1, source_target_pairs={{0,1},{1,0},{2,3},{3,2},{4,5},{5,4},{6,7},{7,6},{8,9},{9,8},{10,11... | collective-permute-start | bytes 393224 | tf_op jit(solution)/shard_map/ppermute | solution.py:197
  61.1 2.4 %copy-start.11 = (bf16[64,1024]{1,0:T(8,128)(2,1)}, bf16[64,1024]{1,0:T(8,128)(2,1)S(1)}, u32[]{:S(2)}) copy-start(bf16[64,1024]{1,0:T(8,128)(2,1)S(1)} %collective-permute-done.14.rest_14_) | copy-start | bytes 393220
  61.1 6.2 %collective-permute-start.9 = (bf16[64,1024]{1,0:T(8,128)(2,1)S(1)}, bf16[64,1024]{1,0:T(8,128)(2,1)}, u32[]{:S(2)}, u32[]{:S(2)}) collective-permute-start(bf16[64,1024]{1,0:T(8,128)(2,1)S(1)} %collective-permute-done.8.rest_8_), channel_id=1, source_target_pairs={{0,1},{1,0},{2,3},{3,2},{4,5},{5,4},{6,7},{7,6},{8,9},{9,8},{10,11... | collective-permute-start | bytes 393224 | tf_op jit(solution)/shard_map/ppermute | solution.py:197
  63.4 0.7 copy-start.12
  63.4 3.9 %collective-permute-start.3 = (bf16[64,1024]{1,0:T(8,128)(2,1)}, bf16[64,1024]{1,0:T(8,128)(2,1)}, u32[]{:S(2)}, u32[]{:S(2)}) collective-permute-start(bf16[64,1024]{1,0:T(8,128)(2,1)} %collective-permute-done.2.rest_2_), channel_id=1, source_target_pairs={{0,1},{1,0},{2,3},{3,2},{4,5},{5,4},{6,7},{7,6},{8,9},{9,8},{10,11... | collective-permute-start | bytes 393224 | tf_op jit(solution)/shard_map/ppermute | solution.py:197
  64.1 2.7 %copy-start.10 = (bf16[64,1024]{1,0:T(8,128)(2,1)S(1)}, bf16[64,1024]{1,0:T(8,128)(2,1)}, u32[]{:S(2)}) copy-start(bf16[64,1024]{1,0:T(8,128)(2,1)} %copy-done.9) | copy-start | bytes 393220
  64.8 0.6 copy-start.13
  65.5 34.2 %collective-permute-start.17 = (bf16[1,13,128,256]{3,2,1,0:T(8,128)(2,1)}, bf16[1,13,128,256]{3,2,1,0:T(8,128)(2,1)}, u32[]{:S(2)}, u32[]{:S(2)}) collective-permute-start(bf16[1,13,128,256]{3,2,1,0:T(8,128)(2,1)} %get-tuple-element.26), channel_id=1, source_target_pairs={{0,1},{1,0},{2,3},{3,2},{4,5},{5,4},{6,7},{7,6},{8,9},{9,8},{10,11... | collective-permute-start | bytes 2555912 | tf_op jit(solution)/shard_map/ppermute | solution.py:197
  66.8 2.1 %collective-permute-start.11 = (bf16[64,1024]{1,0:T(8,128)(2,1)S(1)}, bf16[64,1024]{1,0:T(8,128)(2,1)S(1)}, u32[]{:S(2)}, u32[]{:S(2)}) collective-permute-start(bf16[64,1024]{1,0:T(8,128)(2,1)S(1)} %copy-done.10), channel_id=1, source_target_pairs={{0,1},{1,0},{2,3},{3,2},{4,5},{5,4},{6,7},{7,6},{8,9},{9,8},{10,11... | collective-permute-start | bytes 393224 | tf_op jit(solution)/shard_map/ppermute | solution.py:197
  67.3 1.6 collective-permute-start.15
  67.4 1.8 collective-permute-start.7
  68.9 0.6 copy-start.14
  68.9 0.7 copy-start.15
  97.0 32.4 %collective-permute-start.18 = (bf16[2,1024,128]{2,1,0:T(8,128)(2,1)S(1)}, bf16[2,1024,128]{2,1,0:T(8,128)(2,1)S(1)}, u32[]{:S(2)}, u32[]{:S(2)}) collective-permute-start(bf16[2,1024,128]{2,1,0:T(8,128)(2,1)S(1)} %get-tuple-element.34), channel_id=1, source_target_pairs={{0,2},{1,3},{2,0},{3,1},{4,6},{5,7},{6,4},{7,5},{8,10},{9,11},{10,... | collective-permute-start | bytes 1572872 | tf_op jit(solution)/shard_map/ppermute | solution.py:197
  99.4 35.6 %collective-permute-start.16 = (bf16[2,1024,128]{2,1,0:T(8,128)(2,1)}, bf16[2,1024,128]{2,1,0:T(8,128)(2,1)}, u32[]{:S(2)}, u32[]{:S(2)}) collective-permute-start(bf16[2,1024,128]{2,1,0:T(8,128)(2,1)} %get-tuple-element.33), channel_id=1, source_target_pairs={{0,2},{1,3},{2,0},{3,1},{4,6},{5,7},{6,4},{7,5},{8,10},{9,11},{10,... | collective-permute-start | bytes 1572872 | tf_op jit(solution)/shard_map/ppermute | solution.py:197
  130.6 14.6 %collective-permute-start.19 = (bf16[2,1024,128]{2,1,0:T(8,128)(2,1)S(1)}, bf16[2,1024,128]{2,1,0:T(8,128)(2,1)}, u32[]{:S(2)}, u32[]{:S(2)}) collective-permute-start(bf16[2,1024,128]{2,1,0:T(8,128)(2,1)S(1)} %add_convert_fusion.1), channel_id=1, source_target_pairs={{0,4},{1,5},{2,6},{3,7},{4,0},{5,1},{6,2},{7,3},{8,12},{9,13},{10,... | collective-permute-start | bytes 1572872 | tf_op jit(solution)/shard_map/ppermute | solution.py:197
  133.5 17.6 %collective-permute-start.21 = (f32[1024,128]{1,0:T(8,128)}, f32[1024,128]{1,0:T(8,128)}, u32[]{:S(2)}, u32[]{:S(2)}) collective-permute-start(f32[1024,128]{1,0:T(8,128)} %get-tuple-element.20), channel_id=1, source_target_pairs={{0,16},{16,0},{1,17},{17,1},{2,18},{18,2},{3,19},{19,3},{4,20},{20... | collective-permute-start | bytes 1572872 | tf_op jit(solution)/shard_map/ppermute | solution.py:349
  147.4 14.6 %collective-permute-start.20 = (bf16[1,1024,128]{2,1,0:T(8,128)(2,1)}, bf16[1,1024,128]{2,1,0:T(8,128)(2,1)S(1)}, u32[]{:S(2)}, u32[]{:S(2)}) collective-permute-start(bf16[1,1024,128]{2,1,0:T(8,128)(2,1)} %dynamic-slice_convert_fusion), channel_id=1, source_target_pairs={{0,8},{1,9},{2,10},{3,11},{4,12},{5,13},{6,14},{7,15},{8,0},{9,1},... | collective-permute-start | bytes 786440 | tf_op jit(solution)/shard_map/ppermute | solution.py:197
  151.1 12.3 %copy-start = (bf16[1024,32,32]{0,2,1:T(8,128)(2,1)S(1)}, bf16[1024,32,32]{0,2,1:T(8,128)(2,1)}, u32[]{:S(2)}) copy-start(bf16[1024,32,32]{0,2,1:T(8,128)(2,1)} %get-tuple-element.38) | copy-start | bytes 6291460
  165.7 15.7 %all-to-all-start = ((bf16[16,64,128]{2,1,0:T(8,128)(2,1)}), bf16[16,64,128]{2,1,0:T(8,128)(2,1)S(1)}, u32[]{:S(2)}, u32[]{:S(2)}) async-start(bf16[16,64,128]{2,1,0:T(8,128)(2,1)} %pad_maximum_fusion.1), calls=%async_computation | async-start | bytes 524288 | tf_op jit(solution)/shard_map/all_to_all | solution.py:363
  176.5 3.3 %copy-start.1 = (bf16[1024,1024]{1,0:T(8,128)(2,1)S(1)}, bf16[1024,1024]{1,0:T(8,128)(2,1)}, u32[]{:S(2)}) copy-start(bf16[1024,1024]{1,0:T(8,128)(2,1)} %copy.39.cos_ref) | copy-start | bytes 6291460
where the time goes:
time: 186 us; the launch traced here: 185 us
  Pallas kernels  74.4 us (40%)
  waiting for transfers between devices  31.5 us (17%)
  local copies, waits for them, and re-layouts  30.4 us (16%)
  starting transfers between devices  27.3 us (15%)
  other arithmetic  16.4 us (9%)
  matrix products  4.74 us (3%)
    pallas_call x2, Pallas kernels, partial(): pl.pallas_call(functools.partial(numer_kernel, slab, bands, angles, with_...  55.1 us
    ppermute x21, waiting for transfers between devices, swap(): return lax.ppermute(value, axis, [(i, i ^ mask) for i in range(size)])  31.5 us
    ppermute x21, starting transfers between devices, swap(): return lax.ppermute(value, axis, [(i, i ^ mask) for i in range(size)])  20.8 us
    pallas_call x1, Pallas kernels, shards(): pl.pallas_call(functools.partial(band_kernel, angles, phases), out_shape=...  19.3 us
    neg x2, local copies, waits for them, and re-layouts, shards(): -by_owner(sine)  7.29 us
    optimization_barrier x2, local copies, waits for them, and re-layouts, tables(): lax.optimization_barrier((cosine.astype(jnp.bfloat16), sine.astype(jnp.bf...  6.6 us
    all_to_all x1, starting transfers between devices, shards(): lax.all_to_all(half.reshape(devices, slab, 2 * columns), 'row', split_axi...  4.97 us
    dot_general x1, matrix products, shards(): recon = jnp.dot(back, final, preferred_element_type=jnp.float32)  3.77 us
  transfers between devices with their start and end apart: 23, of which 7 were waited for; matrix products, arithmetic and copies ran while one was open for 13% of the time, Pallas kernels for 30%

commit v1 on v0

v1 whole, which is shorter than its diff:
```python
import functools
import math

import jax
import jax.numpy as jnp
import numpy as np
from jax import lax
from jax.experimental import pallas as pl
from jax.experimental.pallas import tpu as pltpu
from jax.sharding import PartitionSpec as P


MULTIPLES = (0, 1, -1, 2, -2)
WIENER = 0.1
LANES = 128
GROUP = 16


def factors_of(pixels):
    rows = np.arange(pixels)[:, None]

    def angle(columns):
        return (rows * columns[None, :] % pixels) * (2.0 * math.pi / pixels)

    high = angle(np.arange(pixels // LANES) * LANES)
    low = angle(np.arange(LANES))
    factor = 1.0 / math.sqrt(pixels)
    return (
        jnp.asarray(np.concatenate([np.cos(high), np.sin(high)], axis=1) * factor, jnp.float32),
        jnp.asarray(np.stack([np.cos(low), np.sin(low)]), jnp.float32),
    )


def mixing(unmix, phase_order):
    phases = unmix.shape[-1]
    onehot = (phase_order[:, :, None] == jnp.arange(phases, dtype=jnp.int32)[None, None, :]).astype(
        jnp.float32
    )
    mixed = jnp.sum(unmix[:, :, :, None, :] * onehot[None, :, None, :, :], axis=-1)
    return (mixed[0], mixed[1])


def band_kernel(
    angles, phases, shift_ref, base_ref, raw_ref, high_ref, low_ref, coef_ref, *rest
):
    outs = rest[:4]
    cos_ref, sin_ref, spec, turned = rest[4:]
    frames = angles * phases
    slab = outs[0].shape[1] // 2
    pixels = raw_ref.shape[1]
    lane_tiles = pixels // LANES
    tile = 256

    @pl.loop(0, pixels // LANES)
    def _(step):
        rows = pl.ds(pl.multiple_of(step * LANES, LANES), LANES)
        low_cos = low_ref[0, rows, :]
        low_sin = low_ref[1, rows, :]
        high = high_ref[rows, :]
        for index in range(lane_tiles):
            cut = slice(index * LANES, (index + 1) * LANES)
            high_cos = high[:, index : index + 1]
            high_sin = high[:, lane_tiles + index : lane_tiles + index + 1]
            cos_ref[rows, cut] = (high_cos * low_cos - high_sin * low_sin).astype(jnp.bfloat16)
            sin_ref[rows, cut] = (high_sin * low_cos + high_cos * low_sin).astype(jnp.bfloat16)

    @pl.loop(0, pixels // tile)
    def _(step):
        cut = pl.ds(pl.multiple_of(step * tile, tile), tile)
        spec[0, :, cut] = jnp.dot(raw_ref[...], cos_ref[:, cut], preferred_element_type=jnp.float32)
        spec[1, :, cut] = jnp.dot(raw_ref[...], sin_ref[:, cut], preferred_element_type=jnp.float32)

    lane = lax.broadcasted_iota(jnp.int32, (GROUP, LANES), 1)

    @pl.loop(0, slab // GROUP)
    def _(step):
        rows = step * GROUP
        weights = coef_ref[pl.ds(pl.multiple_of(rows, GROUP), GROUP), :]

        def combine(band, terms):
            pairs = []
            for frame, column in terms:
                here = pl.ds(pl.multiple_of(frame * slab + rows, GROUP), GROUP)
                weight_re = jnp.broadcast_to(weights[:, column : column + 1], (GROUP, LANES))
                weight_im = jnp.broadcast_to(weights[:, column + 1 : column + 2], (GROUP, LANES))
                pairs.append((here, weight_re, weight_im))
            for index in range(lane_tiles):
                cut = slice(index * LANES, (index + 1) * LANES)
                real = imag = None
                for here, weight_re, weight_im in pairs:
                    cosine_sum = spec[0, here, cut]
                    sine_sum = spec[1, here, cut]
                    add_re = weight_re * cosine_sum + weight_im * sine_sum
                    add_im = weight_im * cosine_sum - weight_re * sine_sum
                    real = add_re if real is None else real + add_re
                    imag = add_im if imag is None else imag + add_im
                turned[band & 1, 0, index] = real
                turned[band & 1, 1, index] = imag
            move = (-shift_ref[band]) & (pixels - 1)
            rest_lanes = move & (LANES - 1)
            turn = (LANES - rest_lanes) & (LANES - 1)
            for which, out in enumerate(outs):
                first = base_ref[which] + move // LANES
                count = out.shape[2] // LANES
                for part in range(2):
                    tiles = [
                        pltpu.roll(
                            turned[band & 1, part, (first + i) & (lane_tiles - 1)], turn, 1
                        )
                        for i in range(count + 1)
                    ]
                    put = pl.ds(pl.multiple_of(part * slab + rows, GROUP), GROUP)
                    for i in range(count):
                        out[band, put, i * LANES : (i + 1) * LANES] = jnp.where(
                            lane < LANES - rest_lanes, tiles[i], tiles[i + 1]
                        ).astype(jnp.bfloat16)

        combine(0, [(frame, 2 * frame) for frame in range(frames)])
        band = 0
        for which in range(angles):
            for _ in MULTIPLES[1:]:
                band += 1
                column = 2 * (frames + (band - 1) * phases)
                combine(band, [(which * phases + j, column + 2 * j) for j in range(phases)])


def numer_kernel(
    slab, bands, angles, columns, with_power, place_ref, row_ref, col_ref, pow_ref, own_ref,
    other_ref, left_ref, near_ref, far_ref, *rest
):
    outs = rest[:2]
    power_ref = rest[2] if with_power else None
    wide, total = rest[-2:]
    lane_tiles = wide.shape[0]
    pixels = lane_tiles * LANES
    tile = wide.shape[1] - pixels
    tiles = own_ref.shape[2] // LANES
    half = tiles // 2
    pieces = near_ref.shape[0]

    for index in range(2 * pieces):
        ref = far_ref if index >= pieces else near_ref
        start = pl.multiple_of(place_ref[index] * slab, slab)
        for lane in range(lane_tiles):
            wide[lane, pl.ds(start, slab), :] = ref[
                index % pieces, :, lane * LANES : (lane + 1) * LANES
            ].astype(jnp.float32)
    for lane in range(lane_tiles):
        wide[lane, pixels : pixels + tile, :] = wide[lane, 0:tile, :]

    lanes = lax.broadcasted_iota(jnp.int32, (tile, LANES), 1)

    def response(q0, band, column, count):
        start = (q0 + row_ref[band]) & (pixels - 1)
        rest_lanes = column & (LANES - 1)
        first = column // LANES
        turn = (LANES - rest_lanes) & (LANES - 1)
        turned = [
            pltpu.roll(wide[(first + i) & (lane_tiles - 1), pl.ds(start, tile), :], turn, 1)
            for i in range(count + 1)
        ]
        return [
            jnp.where(lanes < LANES - rest_lanes, turned[i], turned[i + 1]) for i in range(count)
        ]

    side = place_ref[2 * pieces]

    @pl.loop(0, pixels // tile)
    def _(step):
        q0 = pl.multiple_of(step * tile, tile)
        left = left_ref[step]
        for band in range(bands):
            right = jnp.concatenate([own_ref[band], other_ref[band]], axis=0)
            product = jnp.dot(left, right, preferred_element_type=jnp.float32)
            weights = response(q0, band, col_ref[band], tiles)
            for i in range(tiles):
                cut = slice(i * LANES, (i + 1) * LANES)
                for part in range(2):
                    value = weights[i] * product[part * tile : (part + 1) * tile, cut]
                    if band == 0:
                        total[i, part] = value
                    else:
                        total[i, part] += value
        for which, out in enumerate(outs):
            first = (side if which == 1 else 1 - side) * half
            per_tile = LANES // columns
            for i in range(half):
                real = total[first + i, 0]
                imag = total[first + i, 1]
                for j in range(per_tile):
                    cut = slice(j * columns, (j + 1) * columns)
                    out[i * per_tile + j, pl.ds(q0, tile), :] = jnp.concatenate(
                        [real[:, cut], imag[:, cut]], axis=1
                    ).astype(jnp.bfloat16)
        if with_power:
            gathered = None
            for band in range(bands):
                value = response(q0, band, pow_ref[band], 1)[0]
                value = value * value
                if band == 0:
                    gathered = value * float(angles)
                else:
                    gathered = gathered + value
            power_ref[pl.ds(q0, tile), :] = jnp.concatenate(
                [gathered[:, :columns], gathered[:, :columns]], axis=1
            )


def image_kernel(back_ref, cos_ref, sin_ref, out_ref):
    devices, _, twice = back_ref.shape
    columns = twice // 2
    chips = devices // 2
    levels = chips.bit_length() - 1
    pixels = out_ref.shape[1]
    total = None
    for chip in range(chips):
        place = sum(((chip >> bit) & 1) << (levels - 1 - bit) for bit in range(levels))
        rows = []
        for core in range(2):
            start = core * (pixels // 2) + place * columns
            rows += [cos_ref[start : start + columns, :], sin_ref[start : start + columns, :]]
        left = jnp.concatenate([back_ref[2 * chip], back_ref[2 * chip + 1]], axis=1)
        value = jnp.dot(left, jnp.concatenate(rows, axis=0), preferred_element_type=jnp.float32)
        total = value if total is None else total + value
    out_ref[...] = total


def smem():
    return pl.BlockSpec(memory_space=pltpu.SMEM)


def vmem():
    return pl.BlockSpec(memory_space=pltpu.VMEM)


def swap(value, axis, mask):
    size = lax.axis_size(axis)
    return lax.ppermute(value, axis, [(i, i ^ mask) for i in range(size)])


def shards(raw, otf, offsets, phase_order, unmix):
    pixels = raw.shape[-1]
    slab = raw.shape[3]
    angles, phases = raw.shape[1:3]
    devices = lax.axis_size("row")
    index = lax.axis_index("row")
    slices = raw.shape[0] * lax.axis_size("cuts")
    chips = devices // 2
    levels = chips.bit_length() - 1
    core = index & 1
    chip = index >> 1
    columns = pixels // devices
    frames = angles * phases
    steps = len(MULTIPLES) - 1
    bands = 1 + angles * steps
    place = sum(((chip >> bit) & 1) << (levels - 1 - bit) for bit in range(levels))

    mine = otf.reshape(slab, pixels).astype(jnp.bfloat16)
    across = swap(mine, "row", 2)
    far = [swap(mine, "row", mask) for mask in range(4, devices, 4)]

    mix_re, mix_im = mixing(unmix, phase_order)
    factors = jnp.array(MULTIPLES[1:], dtype=jnp.int32)
    row_shift = (factors[None, :] * offsets[:, 0:1]).reshape(-1)
    col_shift = (factors[None, :] * offsets[:, 1:2]).reshape(-1)
    zero = jnp.zeros((1,), jnp.int32)
    row_all = jnp.concatenate([zero, row_shift])
    col_all = jnp.concatenate([zero, col_shift])

    def own_rows(which):
        return which * slab + jnp.arange(slab, dtype=jnp.int32)

    turn = (own_rows(index)[:, None] * row_shift[None, :]) & (pixels - 1)
    turn = turn.astype(jnp.float32) * (2.0 * math.pi / pixels)
    turn_re = jnp.cos(turn)[:, :, None]
    turn_im = jnp.sin(turn)[:, :, None]
    rest_re = mix_re[:, 1:].reshape(1, bands - 1, phases)
    rest_im = mix_im[:, 1:].reshape(1, bands - 1, phases)
    coef_re = (rest_re * turn_re - rest_im * turn_im).reshape(slab, -1)
    coef_im = (rest_re * turn_im + rest_im * turn_re).reshape(slab, -1)
    plain_re = jnp.broadcast_to(mix_re[:, 0].reshape(1, frames), (slab, frames))
    plain_im = jnp.broadcast_to(mix_im[:, 0].reshape(1, frames), (slab, frames))
    coef = jnp.stack(
        [
            jnp.concatenate([plain_re, coef_re], axis=1),
            jnp.concatenate([plain_im, coef_im], axis=1),
        ],
        axis=2,
    ).reshape(slab, -1)

    quarter = pixels // 4
    near = chip & 1
    half_tiles = quarter // LANES
    base = jnp.stack(
        [(2 * c + h) * half_tiles for c in (1 - core, core) for h in (1 - near, near)]
    )
    high, low = factors_of(pixels)
    table = jax.ShapeDtypeStruct((pixels, pixels), jnp.bfloat16)
    send_away, send_near, keep_away, keep_near, cosine, sine = pl.pallas_call(
        functools.partial(band_kernel, angles, phases),
        out_shape=[jax.ShapeDtypeStruct((bands, 2 * slab, quarter), jnp.bfloat16)] * 4
        + [table] * 2,
        in_specs=[smem(), smem(), vmem(), vmem(), vmem(), vmem()],
        out_specs=[vmem()] * 6,
        scratch_shapes=[
            pltpu.VMEM((2, frames * slab, pixels), jnp.float32),
            pltpu.VMEM((2, 2, pixels // LANES, GROUP, LANES), jnp.float32),
        ],
        cost_estimate=pl.CostEstimate(
            flops=8 * frames * slab * pixels * pixels,
            bytes_accessed=12 << 20,
            transcendentals=0,
        ),
        name="bands",
    )(col_all & (pixels - 1), base, raw.reshape(frames * slab, pixels), high, low, coef)

    got_away = swap(send_away, "row", 1)
    first_half = jnp.stack([mine] + far)
    second_half = jnp.concatenate([across[None], swap(jnp.stack(far), "row", 2)])
    own_pieces = jnp.concatenate([first_half, second_half])
    other_pieces = jnp.concatenate([swap(first_half, "row", 1), swap(second_half, "row", 1)])
    got_near = swap(send_near, "row", 1)
    masks = list(range(0, devices, 4)) + list(range(2, devices, 4))
    masks += [mask | 1 for mask in masks]

    def table_rows(which):
        cut = which * slab
        return (
            lax.dynamic_slice_in_dim(cosine, cut, slab, 0),
            lax.dynamic_slice_in_dim(sine, cut, slab, 0),
        )

    tile = 128
    cos_own, sin_own = table_rows(index)
    cos_other, sin_other = table_rows(index ^ 1)
    left = jnp.stack(
        [
            jnp.concatenate([cos_own, sin_own, cos_other, sin_other], axis=0).T,
            jnp.concatenate([-sin_own, cos_own, -sin_other, cos_other], axis=0).T,
        ]
    )
    left = left.reshape(2, pixels // tile, tile, 4 * slab)
    left = jnp.swapaxes(left, 0, 1).reshape(pixels // tile, 2 * tile, 4 * slab)
    row_base = (-row_all) & (pixels - 1)
    pow_base = (core * (pixels // 2) + place * columns - col_all) & (pixels - 1)
    places = jnp.stack([index ^ mask for mask in masks] + [(chip >> 1) & 1])

    def partial(half, own, other, with_power):
        start = core * (pixels // 2) + half * quarter
        col_base = (start - col_all) & (pixels - 1)
        out_shape = [jax.ShapeDtypeStruct((chips // 4, pixels, 2 * columns), jnp.bfloat16)] * 2
        if with_power:
            out_shape = out_shape + [jax.ShapeDtypeStruct((pixels, 2 * columns), jnp.float32)]
        return pl.pallas_call(
            functools.partial(numer_kernel, slab, bands, angles, columns, with_power),
            out_shape=out_shape,
            in_specs=[smem()] * 4 + [vmem()] * 5,
            out_specs=[vmem()] * len(out_shape),
            scratch_shapes=[
                pltpu.VMEM((pixels // LANES, pixels + tile, LANES), jnp.float32),
                pltpu.VMEM((quarter // LANES, 2, tile, LANES), jnp.float32),
            ],
            cost_estimate=pl.CostEstimate(
                flops=16 * bands * slab * pixels * quarter,
                bytes_accessed=8 << 20,
                transcendentals=0,
            ),
        )(places, row_base, col_base, pow_base, own, other, left, own_pieces, other_pieces)

    away_far, away_stay = partial(1 - near, keep_away, got_away, False)
    far, stay = swap(away_far, "row", 2), swap(away_stay, "row", 2)
    kept_far, kept_stay, power = partial(near, keep_near, got_near, True)

    def split(blocks, bit):
        count = blocks.shape[0] // 2
        side = (chip >> bit) & 1
        return (
            lax.dynamic_slice_in_dim(blocks, (1 - side) * count, count, 0),
            lax.dynamic_slice_in_dim(blocks, side * count, count, 0),
        )

    def widen(value):
        return value.astype(jnp.float32)

    far = widen(far) + widen(kept_far)
    stay = widen(stay) + widen(kept_stay)
    for bit in range(1, levels):
        got_next = swap(far.astype(jnp.bfloat16), "row", 2 << bit)
        stay = stay + widen(got_next)
        if bit < levels - 1:
            far, stay = split(stay, bit + 1)
    numer = stay[0]

    total_power = power
    moving = power
    cuts = lax.axis_size("cuts")
    for _ in range(cuts - 1):
        moving = lax.ppermute(moving, "cuts", [(i, (i + 1) % cuts) for i in range(cuts)])
        total_power = total_power + moving
    denom = WIENER + total_power / (slices * angles)
    ratio = (numer / denom).astype(jnp.bfloat16)

    by_cos = jnp.dot(cosine, ratio, preferred_element_type=jnp.float32)
    by_sin = jnp.dot(sine, ratio, preferred_element_type=jnp.float32)
    half = jnp.concatenate(
        [
            by_cos[:, :columns] - by_sin[:, columns:],
            -by_cos[:, columns:] - by_sin[:, :columns],
        ],
        axis=1,
    ).astype(jnp.bfloat16)
    back = lax.all_to_all(
        half.reshape(devices, slab, 2 * columns), "row", split_axis=0, concat_axis=0, tiled=True
    )
    recon = pl.pallas_call(
        image_kernel,
        out_shape=jax.ShapeDtypeStruct((slab, pixels), jnp.float32),
        in_specs=[vmem()] * 3,
        out_specs=vmem(),
        cost_estimate=pl.CostEstimate(
            flops=4 * slab * pixels * pixels, bytes_accessed=6 << 20, transcendentals=0
        ),
        name="image",
    )(back, cosine, sine)
    return recon.reshape(otf.shape)


def solution(mesh):
    in_specs = (P("cuts", None, None, "row", None), P("cuts", "row", None), P(), P(), P())
    out_specs = P("cuts", "row", None)

    return jax.shard_map(shards, mesh=mesh, in_specs=in_specs, out_specs=out_specs, check_vma=False)
```

time: 186 us -> 143 us (0.77)
  local copies, waits for them, and re-layouts: 30.4 us -> 6.96 us
  Pallas kernels: 74.4 us -> 56.4 us
  blocking collectives: 0 us -> 14.8 us
  starting transfers between devices: 27.3 us -> 15.5 us
  other arithmetic: 16.4 us -> 12.4 us
  waiting for transfers between devices: 31.5 us -> 34.6 us
  matrix products: 4.74 us -> 1.66 us
    pallas_call x2 -> x3, Pallas kernels: 55.1 us -> 32.1 us  [the longest x2 28.3 us: partial(): pl.pallas_call(functools.partial(numer_kernel, slab, bands, angles, colum...]
    all_to_all x0 -> x1, blocking collectives: none -> 14.8 us  [shards(): lax.all_to_all(half.reshape(devices, slab, 2 * columns), 'row', split_axi...]
    neg x2 -> x0, local copies, waits for them, and re-layouts: 7.29 us -> none  [shards(): -by_owner(sine)]
    ppermute x21 -> x13, starting transfers between devices: 20.8 us -> 14 us  [swap(): return lax.ppermute(value, axis, [(i, i ^ mask) for i in range(size)])]
    optimization_barrier x2 -> x0, local copies, waits for them, and re-layouts: 6.6 us -> none  [tables(): lax.optimization_barrier((cosine.astype(jnp.bfloat16), sine.astype(jnp.bf...]
    pallas_call x1, Pallas kernels: 19.3 us -> 24.3 us  [shards(): pl.pallas_call(functools.partial(band_kernel, angles, phases), out_shape=...]
    all_to_all x1 -> x0, starting transfers between devices: 4.97 us -> none  [shards(): lax.all_to_all(half.reshape(devices, slab, 2 * columns), 'row', split_axi...]
    dynamic_slice x2 -> x0, local copies, waits for them, and re-layouts: 4.89 us -> none  [the longest x1 2.83 us: shards(): lax.dynamic_slice_in_dim(there, half, 1, 0)]
  transfers between devices with their start and end apart: 23 -> 14, of which waited for: 7 -> 5; matrix products, arithmetic and copies ran while one was open for 13% -> 10% of each run, Pallas kernels for 30% -> 37%
where the time goes in v1:
time: 143 us
  Pallas kernels  56.4 us (39%)
  waiting for transfers between devices  34.6 us (24%)
  starting transfers between devices  15.5 us (11%)
  blocking collectives  14.8 us (10%)
  other arithmetic  12.4 us (9%)
  local copies, waits for them, and re-layouts  6.96 us (5%)
  matrix products  1.66 us (1%)
    ppermute x13, waiting for transfers between devices, swap(): return lax.ppermute(value, axis, [(i, i ^ mask) for i in range(size)])  34.6 us
    pallas_call x2, Pallas kernels, partial(): pl.pallas_call(functools.partial(numer_kernel, slab, bands, angles, colum...  28.3 us
    pallas_call x1, Pallas kernels, shards(): pl.pallas_call(functools.partial(band_kernel, angles, phases), out_shape=...  24.3 us
    all_to_all x1, blocking collectives, shards(): lax.all_to_all(half.reshape(devices, slab, 2 * columns), 'row', split_axi...  14.8 us
    ppermute x13, starting transfers between devices, swap(): return lax.ppermute(value, axis, [(i, i ^ mask) for i in range(size)])  14 us
    pallas_call x1, Pallas kernels, shards(): pl.pallas_call(image_kernel, out_shape=jax.ShapeDtypeStruct((slab, pixels...  3.85 us
  transfers between devices with their start and end apart: 14, of which 5 were waited for; matrix products, arithmetic and copies ran while one was open for 10% of the time, Pallas kernels for 37%

profile of v1, /device:TPU:0, one launch (start us, length us, event | category | flops | bytes accessed | tf_op | source)
XLA Modules:
  0.0 142.6 jit_solution(2976782732502352469)
XLA Ops:
  0.0 1.0 constant_dynamic-update-slice_fusion.5
  1.0 3.1 %collective-permute-start.4 = (bf16[64,1024]{1,0:T(8,128)(2,1)S(1)}, bf16[64,1024]{1,0:T(8,128)(2,1)S(1)}, u32[]{:S(2)}, u32[]{:S(2)}) collective-permute-start(bf16[64,1024]{1,0:T(8,128)(2,1)S(1)} %bitcast.84), channel_id=1, source_target_pairs={{0,2},{1,3},{2,0},{3,1},{4,6},{5,7},{6,4},{7,5},{8,10},{9,11},{10,... | collective-permute-start | bytes 393224 | tf_op jit(solution)/shard_map/ppermute | solution.py:238
  4.0 3.6 %collective-permute-start.3 = (bf16[64,1024]{1,0:T(8,128)(2,1)S(1)}, bf16[64,1024]{1,0:T(8,128)(2,1)S(1)}, u32[]{:S(2)}, u32[]{:S(2)}) collective-permute-start(bf16[64,1024]{1,0:T(8,128)(2,1)S(1)} %bitcast.85), channel_id=1, source_target_pairs={{0,12},{1,13},{2,14},{3,15},{4,8},{5,9},{6,10},{7,11},{8,4},{9,5},... | collective-permute-start | bytes 393224 | tf_op jit(solution)/shard_map/ppermute | solution.py:238
  7.6 0.0 collective-permute-start.2
  7.6 0.8 collective-permute-start.1
  8.4 0.8 fusion.3
  9.2 0.9 multiply_reduce_fusion
  10.1 0.1 fusion.10
  10.1 0.2 copy.28
  10.4 0.2 copy.30
  10.6 0.8 slice_bitcast_fusion
  11.4 0.7 broadcast_multiply_fusion
  12.1 0.1 mul.204
  12.2 0.1 mul.187
  12.3 0.1 fusion.4
  12.5 0.1 mul.197
  12.6 0.1 reshape.138
  12.6 0.1 mul.212
  12.7 0.1 reshape.139
  12.8 0.1 multiply_subtract_fusion
  12.9 0.1 maximum_bitcast_fusion.2
  13.1 0.1 reshape.135
  13.1 0.7 copy.35.coef_ref
  13.9 0.7 pad_add_fusion.2.base_ref
  14.5 0.6 subtract_and_fusion.2
  15.1 24.3 %bands.1 = (bf16[13,128,256]{2,1,0:T(8,128)(2,1)}, bf16[13,128,256]{2,1,0:T(8,128)(2,1)}, bf16[13,128,256]{2,1,0:T(8,128)(2,1)}, bf16[13,128,256]{2,1,0:T(8,128)...) custom-call(s32[13]{0:T(128)} %get-tuple-element.52.shift_ref, s32[4]{0:T(128)} %pad_add_fusion.2.base_ref, ...), custom_call_target="tpu_custom_call" | custom-call | flops 8053063680 | bytes 12582912 | tf_op jit(solution)/shard_map/bands/pallas_call | solution.py:299
  39.4 0.0 collective-permute-start
  39.4 0.6 fusion.7.row_ref
  40.0 1.0 constant_dynamic-slice_fusion.3
  41.0 1.0 fusion.8
  42.0 0.1 maximum_bitcast_fusion
  42.2 0.2 copy.41
  42.4 0.2 copy.42
  42.6 0.6 stack.131.place_ref
  43.2 1.1 pad_maximum_fusion
  44.4 0.5 collective-permute-start.9
  44.9 0.1 pad_maximum_fusion.1
  45.0 0.3 collective-permute-start.5
  45.4 10.7 %collective-permute-done.5 = bf16[3,64,1024]{2,1,0:T(8,128)(2,1)S(1)} collective-permute-done((bf16[3,64,1024]{2,1,0:T(8,128)(2,1)S(1)}, bf16[3,64,1024]{2,1,0:T(8,128)(2,1)S(1)}, u32[]{:S(2)}, u32[]{:S(2)}) %collective-permute-start.5) | collective-permute-done | bytes 393248 | tf_op jit(solution)/shard_map/ppermute | solution.py:238
  56.1 0.1 collective-permute-start.7
  56.4 1.8 %collective-permute-done.7 = bf16[4,64,1024]{2,1,0:T(8,128)(2,1)S(1)} collective-permute-done((bf16[4,64,1024]{2,1,0:T(8,128)(2,1)S(1)}, bf16[4,64,1024]{2,1,0:T(8,128)(2,1)S(1)}, u32[]{:S(2)}, u32[]{:S(2)}) %collective-permute-start.7) | collective-permute-done | bytes 524320 | tf_op jit(solution)/shard_map/ppermute | solution.py:238
  58.2 0.9 copy-done.4
  59.1 12.0 %shard_map.82 = (bf16[2,1024,128]{2,1,0:T(8,128)(2,1)}, bf16[2,1024,128]{2,1,0:T(8,128)(2,1)}) custom-call(s32[17]{0:T(128)} %stack.131.place_ref, s32[13]{0:T(128)} %fusion.7.row_ref, s32[13]{0:T(128)} %get-tuple-element.49.col_ref, s32[13]{0:T(128)} %get-tuple-element.50.pow_ref, bf16[13,128,256]{2,1,0:T(8,128)(2,1)} %get-tuple-element.17.own_ref, ...), custom_call_target="tpu_custom_call" | custom-call | flops 3489660928 | bytes 8388608 | tf_op jit(solution)/shard_map/pallas_call | solution.py:354
  71.1 0.3 collective-permute-start.10
  71.4 1.7 %collective-permute-start.8 = (bf16[2,1024,128]{2,1,0:T(8,128)(2,1)}, bf16[2,1024,128]{2,1,0:T(8,128)(2,1)S(1)}, u32[]{:S(2)}, u32[]{:S(2)}) collective-permute-start(bf16[2,1024,128]{2,1,0:T(8,128)(2,1)} %get-tuple-element.20), channel_id=1, source_target_pairs={{0,2},{1,3},{2,0},{3,1},{4,6},{5,7},{6,4},{7,5},{8,10},{9,11},{10,... | collective-permute-start | bytes 1572872 | tf_op jit(solution)/shard_map/ppermute | solution.py:238
  73.1 16.3 %shard_map.83 = (bf16[2,1024,128]{2,1,0:T(8,128)(2,1)}, bf16[2,1024,128]{2,1,0:T(8,128)(2,1)}, f32[1024,128]{1,0:T(8,128)}) custom-call(s32[17]{0:T(128)} %stack.131.place_ref, s32[13]{0:T(128)} %fusion.7.row_ref, s32[13]{0:T(128)} %get-tuple-element.51.col_ref, s32[13]{0:T(128)} %get-tuple-element.50.pow_ref, ...), custom_call_target="tpu_custom_call" | custom-call | flops 3489660928 | bytes 8388608 | tf_op jit(solution)/shard_map/pallas_call | solution.py:354
  89.4 1.2 add_convert_fusion
  90.6 1.2 collective-permute-start.11
  91.8 1.4 %collective-permute-start.13 = (f32[1024,128]{1,0:T(8,128)}, f32[1024,128]{1,0:T(8,128)}, u32[]{:S(2)}, u32[]{:S(2)}) collective-permute-start(f32[1024,128]{1,0:T(8,128)} %get-tuple-element.26), channel_id=1, source_target_pairs={{0,16},{16,0},{1,17},{17,1},{2,18},{18,2},{3,19},{19,3},{4,20},{20... | collective-permute-start | bytes 1572872 | tf_op jit(solution)/shard_map/ppermute | solution.py:398
  93.3 3.2 %collective-permute-done.8 = bf16[2,1024,128]{2,1,0:T(8,128)(2,1)S(1)} collective-permute-done((bf16[2,1024,128]{2,1,0:T(8,128)(2,1)}, bf16[2,1024,128]{2,1,0:T(8,128)(2,1)S(1)}, u32[]{:S(2)}, u32[]{:S(2)}) %collective-permute-start.8) | collective-permute-done | bytes 524320 | tf_op jit(solution)/shard_map/ppermute | solution.py:238
  96.5 7.6 %collective-permute-done.11 = bf16[2,1024,128]{2,1,0:T(8,128)(2,1)S(1)} collective-permute-done((bf16[2,1024,128]{2,1,0:T(8,128)(2,1)S(1)}, bf16[2,1024,128]{2,1,0:T(8,128)(2,1)S(1)}, u32[]{:S(2)}, u32[]{:S(2)}) %collective-permute-start.11) | collective-permute-done | bytes 524320 | tf_op jit(solution)/shard_map/ppermute | solution.py:238
  104.1 0.8 copy-done.3
  104.9 1.7 %convert_add_fusion = f32[2,1024,128]{2,1,0:T(8,128)S(1)} fusion(bf16[2,1024,128]{2,1,0:T(8,128)(2,1)} %copy-done.3, bf16[2,1024,128]{2,1,0:T(8,128)(2,1)} %get-tuple-element.23, bf16[2,1024,128]{2,1,0:T(8,128)(2,1)} %copy-done.2), kind=kLoop, calls=%fused_computation.1 | loop fusion | flops 1310720 | bytes 2621440 | tf_op jit(solution)/shard_map/add | solution.py:389
  106.6 2.4 %collective-permute-start.12 = (bf16[1,1024,128]{2,1,0:T(8,128)(2,1)S(1)}, bf16[1,1024,128]{2,1,0:T(8,128)(2,1)}, u32[]{:S(2)}, u32[]{:S(2)}) collective-permute-start(bf16[1,1024,128]{2,1,0:T(8,128)(2,1)S(1)} %dynamic-slice_convert_fusion), channel_id=1, source_target_pairs={{0,8},{1,9},{2,10},{3,11},{4,12},{5,13},{6,14},{7,15},{8,0},{9,1},... | collective-permute-start | bytes 786440 | tf_op jit(solution)/shard_map/ppermute | solution.py:238
  109.0 11.3 %collective-permute-done.12 = bf16[1,1024,128]{2,1,0:T(8,128)(2,1)} collective-permute-done((bf16[1,1024,128]{2,1,0:T(8,128)(2,1)S(1)}, bf16[1,1024,128]{2,1,0:T(8,128)(2,1)}, u32[]{:S(2)}, u32[]{:S(2)}) %collective-permute-start.12) | collective-permute-done | bytes 262176 | tf_op jit(solution)/shard_map/ppermute | solution.py:238
  120.3 1.4 fusion
  121.7 0.8 fusion.12
  122.6 0.8 fusion.11
  123.4 0.1 fusion.2
  123.5 0.2 copy.38
  123.6 0.2 copy.39
  123.8 0.2 pad_maximum_fusion.4
  124.0 14.8 %all_to_all.5.back_ref = bf16[16,64,128]{2,1,0:T(8,128)(2,1)} all-to-all(bf16[16,64,128]{2,1,0:T(8,128)(2,1)S(1)} %pad_maximum_fusion.4), channel_id=1, replica_groups=mesh['cuts'=2,'row'=16] {'row'}, dimensions={0} | all-to-all | bytes 524288 | tf_op jit(solution)/shard_map/all_to_all | solution.py:412
  138.8 3.8 %image.1 = f32[64,1024]{1,0:T(8,128)} custom-call(bf16[16,64,128]{2,1,0:T(8,128)(2,1)} %all_to_all.5.back_ref, bf16[1024,1024]{1,0:T(8,128)(2,1)} %get-tuple-element.16.cos_ref, bf16[1024,1024]{1,0:T(8,128)(2,1)} %get-tuple-element.19.sin_ref), custom_call_target="tpu_custom_call" | custom-call | flops 268435456 | bytes 6291456 | tf_op jit(solution)/shard_map/image/pallas_call | solution.py:415
  (45 shorter events, 0.4 us)
Async XLA Ops:
  1.0 44.4 %collective-permute-start.4 = (bf16[64,1024]{1,0:T(8,128)(2,1)S(1)}, bf16[64,1024]{1,0:T(8,128)(2,1)S(1)}, u32[]{:S(2)}, u32[]{:S(2)}) collective-permute-start(bf16[64,1024]{1,0:T(8,128)(2,1)S(1)} %bitcast.84), channel_id=1, source_target_pairs={{0,2},{1,3},{2,0},{3,1},{4,6},{5,7},{6,4},{7,5},{8,10},{9,11},{10,... | collective-permute-start | bytes 393224 | tf_op jit(solution)/shard_map/ppermute | solution.py:238
  4.0 40.3 %collective-permute-start.3 = (bf16[64,1024]{1,0:T(8,128)(2,1)S(1)}, bf16[64,1024]{1,0:T(8,128)(2,1)S(1)}, u32[]{:S(2)}, u32[]{:S(2)}) collective-permute-start(bf16[64,1024]{1,0:T(8,128)(2,1)S(1)} %bitcast.85), channel_id=1, source_target_pairs={{0,12},{1,13},{2,14},{3,15},{4,8},{5,9},{6,10},{7,11},{8,4},{9,5},... | collective-permute-start | bytes 393224 | tf_op jit(solution)/shard_map/ppermute | solution.py:238
  7.6 37.2 %collective-permute-start.2 = (bf16[64,1024]{1,0:T(8,128)(2,1)S(1)}, bf16[64,1024]{1,0:T(8,128)(2,1)S(1)}, u32[]{:S(2)}, u32[]{:S(2)}) collective-permute-start(bf16[64,1024]{1,0:T(8,128)(2,1)S(1)} %bitcast.86), channel_id=1, source_target_pairs={{0,8},{1,9},{2,10},{3,11},{4,12},{5,13},{6,14},{7,15},{8,0},{9,1},... | collective-permute-start | bytes 393224 | tf_op jit(solution)/shard_map/ppermute | solution.py:238
  7.6 37.2 %collective-permute-start.1 = (bf16[64,1024]{1,0:T(8,128)(2,1)S(1)}, bf16[64,1024]{1,0:T(8,128)(2,1)S(1)}, u32[]{:S(2)}, u32[]{:S(2)}) collective-permute-start(bf16[64,1024]{1,0:T(8,128)(2,1)S(1)} %bitcast.87), channel_id=1, source_target_pairs={{0,4},{1,5},{2,6},{3,7},{4,0},{5,1},{6,2},{7,3},{8,12},{9,13},{10,... | collective-permute-start | bytes 393224 | tf_op jit(solution)/shard_map/ppermute | solution.py:238
  39.4 18.7 %collective-permute-start = (bf16[13,128,256]{2,1,0:T(8,128)(2,1)}, bf16[13,128,256]{2,1,0:T(8,128)(2,1)}, u32[]{:S(2)}, u32[]{:S(2)}) collective-permute-start(bf16[13,128,256]{2,1,0:T(8,128)(2,1)} %get-tuple-element.18), channel_id=1, source_target_pairs={{0,1},{1,0},{2,3},{3,2},{4,5},{5,4},{6,7},{7,6},{8,9},{9,8},{10,11... | collective-permute-start | bytes 2555912 | tf_op jit(solution)/shard_map/ppermute | solution.py:238
  44.4 28.8 %collective-permute-start.9 = (bf16[13,128,256]{2,1,0:T(8,128)(2,1)}, bf16[13,128,256]{2,1,0:T(8,128)(2,1)}, u32[]{:S(2)}, u32[]{:S(2)}) collective-permute-start(bf16[13,128,256]{2,1,0:T(8,128)(2,1)} %get-tuple-element.22), channel_id=1, source_target_pairs={{0,1},{1,0},{2,3},{3,2},{4,5},{5,4},{6,7},{7,6},{8,9},{9,8},{10,11... | collective-permute-start | bytes 2555912 | tf_op jit(solution)/shard_map/ppermute | solution.py:238
  45.0 11.1 %collective-permute-start.5 = (bf16[3,64,1024]{2,1,0:T(8,128)(2,1)S(1)}, bf16[3,64,1024]{2,1,0:T(8,128)(2,1)S(1)}, u32[]{:S(2)}, u32[]{:S(2)}) collective-permute-start(bf16[3,64,1024]{2,1,0:T(8,128)(2,1)S(1)} %pad_maximum_fusion.3), channel_id=1, source_target_pairs={{0,2},{1,3},{2,0},{3,1},{4,6},{5,7},{6,4},{7,5},{8,10},{9,11},{10,... | collective-permute-start | bytes 1179656 | tf_op jit(solution)/shard_map/ppermute | solution.py:238
  45.3 11.0 %collective-permute-start.6 = (bf16[4,64,1024]{2,1,0:T(8,128)(2,1)S(1)}, bf16[4,64,1024]{2,1,0:T(8,128)(2,1)S(1)}, u32[]{:S(2)}, u32[]{:S(2)}) collective-permute-start(bf16[4,64,1024]{2,1,0:T(8,128)(2,1)S(1)} %pad_maximum_fusion.1), channel_id=1, source_target_pairs={{0,1},{1,0},{2,3},{3,2},{4,5},{5,4},{6,7},{7,6},{8,9},{9,8},{10,11... | collective-permute-start | bytes 1572872 | tf_op jit(solution)/shard_map/ppermute | solution.py:238
  56.1 2.0 %collective-permute-start.7 = (bf16[4,64,1024]{2,1,0:T(8,128)(2,1)S(1)}, bf16[4,64,1024]{2,1,0:T(8,128)(2,1)S(1)}, u32[]{:S(2)}, u32[]{:S(2)}) collective-permute-start(bf16[4,64,1024]{2,1,0:T(8,128)(2,1)S(1)} %pad_maximum_fusion.2), channel_id=1, source_target_pairs={{0,1},{1,0},{2,3},{3,2},{4,5},{5,4},{6,7},{7,6},{8,9},{9,8},{10,11... | collective-permute-start | bytes 1572872 | tf_op jit(solution)/shard_map/ppermute | solution.py:238
  56.3 1.9 %copy-start.5 = (bf16[8,64,1024]{2,1,0:T(8,128)(2,1)}, bf16[8,64,1024]{2,1,0:T(8,128)(2,1)S(1)}, u32[]{:S(2)}) copy-start(bf16[8,64,1024]{2,1,0:T(8,128)(2,1)S(1)} %constant_dynamic-update-slice_fusion.near_ref) | copy-start | bytes 3145732
  58.2 1.0 copy-start.4
  71.1 18.3 %collective-permute-start.10 = (bf16[2,1024,128]{2,1,0:T(8,128)(2,1)}, bf16[2,1024,128]{2,1,0:T(8,128)(2,1)S(1)}, u32[]{:S(2)}, u32[]{:S(2)}) collective-permute-start(bf16[2,1024,128]{2,1,0:T(8,128)(2,1)} %get-tuple-element.24), channel_id=1, source_target_pairs={{0,2},{1,3},{2,0},{3,1},{4,6},{5,7},{6,4},{7,5},{8,10},{9,11},{10,... | collective-permute-start | bytes 1572872 | tf_op jit(solution)/shard_map/ppermute | solution.py:238
  71.4 25.1 %collective-permute-start.8 = (bf16[2,1024,128]{2,1,0:T(8,128)(2,1)}, bf16[2,1024,128]{2,1,0:T(8,128)(2,1)S(1)}, u32[]{:S(2)}, u32[]{:S(2)}) collective-permute-start(bf16[2,1024,128]{2,1,0:T(8,128)(2,1)} %get-tuple-element.20), channel_id=1, source_target_pairs={{0,2},{1,3},{2,0},{3,1},{4,6},{5,7},{6,4},{7,5},{8,10},{9,11},{10,... | collective-permute-start | bytes 1572872 | tf_op jit(solution)/shard_map/ppermute | solution.py:238
  90.6 13.5 %collective-permute-start.11 = (bf16[2,1024,128]{2,1,0:T(8,128)(2,1)S(1)}, bf16[2,1024,128]{2,1,0:T(8,128)(2,1)S(1)}, u32[]{:S(2)}, u32[]{:S(2)}) collective-permute-start(bf16[2,1024,128]{2,1,0:T(8,128)(2,1)S(1)} %add_convert_fusion), channel_id=1, source_target_pairs={{0,4},{1,5},{2,6},{3,7},{4,0},{5,1},{6,2},{7,3},{8,12},{9,13},{10,... | collective-permute-start | bytes 1572872 | tf_op jit(solution)/shard_map/ppermute | solution.py:238
  91.8 17.2 %collective-permute-start.13 = (f32[1024,128]{1,0:T(8,128)}, f32[1024,128]{1,0:T(8,128)}, u32[]{:S(2)}, u32[]{:S(2)}) collective-permute-start(f32[1024,128]{1,0:T(8,128)} %get-tuple-element.26), channel_id=1, source_target_pairs={{0,16},{16,0},{1,17},{17,1},{2,18},{18,2},{3,19},{19,3},{4,20},{20... | collective-permute-start | bytes 1572872 | tf_op jit(solution)/shard_map/ppermute | solution.py:398
  96.5 7.6 %copy-start.2 = (bf16[2,1024,128]{2,1,0:T(8,128)(2,1)}, bf16[2,1024,128]{2,1,0:T(8,128)(2,1)S(1)}, u32[]{:S(2)}) copy-start(bf16[2,1024,128]{2,1,0:T(8,128)(2,1)S(1)} %collective-permute-done.8) | copy-start | bytes 1572868
  104.0 0.8 copy-start.3
  104.9 16.9 %copy-start.1 = (bf16[1024,1024]{1,0:T(8,128)(2,1)S(1)}, bf16[1024,1024]{1,0:T(8,128)(2,1)}, u32[]{:S(2)}) copy-start(bf16[1024,1024]{1,0:T(8,128)(2,1)} %get-tuple-element.19.sin_ref) | copy-start | bytes 6291460
  106.6 13.7 %collective-permute-start.12 = (bf16[1,1024,128]{2,1,0:T(8,128)(2,1)S(1)}, bf16[1,1024,128]{2,1,0:T(8,128)(2,1)}, u32[]{:S(2)}, u32[]{:S(2)}) collective-permute-start(bf16[1,1024,128]{2,1,0:T(8,128)(2,1)S(1)} %dynamic-slice_convert_fusion), channel_id=1, source_target_pairs={{0,8},{1,9},{2,10},{3,11},{4,12},{5,13},{6,14},{7,15},{8,0},{9,1},... | collective-permute-start | bytes 786440 | tf_op jit(solution)/shard_map/ppermute | solution.py:238
  109.0 13.6 %copy-start = (bf16[1024,1024]{1,0:T(8,128)(2,1)S(1)}, bf16[1024,1024]{1,0:T(8,128)(2,1)}, u32[]{:S(2)}) copy-start(bf16[1024,1024]{1,0:T(8,128)(2,1)} %get-tuple-element.16.cos_ref) | copy-start | bytes 6291460

commit v2 on v1

v2 whole, which is shorter than its diff:
```python
import functools
import math

import jax
import jax.numpy as jnp
import numpy as np
from jax import lax
from jax.experimental import pallas as pl
from jax.experimental.pallas import tpu as pltpu
from jax.sharding import PartitionSpec as P


MULTIPLES = (0, 1, -1, 2, -2)
WIENER = 0.1
LANES = 128
GROUP = 16


def factors_of(pixels):
    rows = np.arange(pixels)[:, None]

    def angle(columns):
        return (rows * columns[None, :] % pixels) * (2.0 * math.pi / pixels)

    high = angle(np.arange(pixels // LANES) * LANES)
    low = angle(np.arange(LANES))
    factor = 1.0 / math.sqrt(pixels)
    return (
        jnp.asarray(np.concatenate([np.cos(high), np.sin(high)], axis=1) * factor, jnp.float32),
        jnp.asarray(np.stack([np.cos(low), np.sin(low)]), jnp.float32),
    )


def turn_of(angle):
    square = angle * angle
    cosine = jnp.zeros_like(angle)
    sine = jnp.zeros_like(angle)
    for order in range(9, -1, -1):
        sign = -1.0 if order % 2 else 1.0
        cosine = cosine * square + sign / math.factorial(2 * order)
        sine = sine * square + sign / math.factorial(2 * order + 1)
    return cosine, sine * angle


def band_kernel(
    angles, phases, index_ref, unmix_ref, order_ref, offset_ref, raw_hbm, high_ref, low_ref, *rest
):
    outs = rest[:4]
    cos_hbm, sin_hbm, left_hbm = rest[4:7]
    parts = rest[7:11]
    raw_ref, cos_ref, sin_ref, left_ref, spec, turned, phase, sems, row_sems = rest[11:]
    frames = angles * phases
    slab = raw_ref.shape[0] // frames
    pixels = raw_ref.shape[1]
    lane_tiles = pixels // LANES
    tile = 256
    others = len(MULTIPLES) - 1
    index = index_ref[0]
    core = index & 1
    chip = index >> 1
    near = chip & 1
    pair = 2 * slab

    fetch = pltpu.make_async_copy(raw_hbm, raw_ref, sems.at[0])
    fetch.start()

    @pl.loop(0, pixels // LANES)
    def _(step):
        rows = pl.ds(pl.multiple_of(step * LANES, LANES), LANES)
        low_cos = low_ref[0, rows, :]
        low_sin = low_ref[1, rows, :]
        high = high_ref[rows, :]
        for tab in range(lane_tiles):
            cut = slice(tab * LANES, (tab + 1) * LANES)
            high_cos = high[:, tab : tab + 1]
            high_sin = high[:, lane_tiles + tab : lane_tiles + tab + 1]
            cos_ref[rows, cut] = (high_cos * low_cos - high_sin * low_sin).astype(jnp.bfloat16)
            sin_ref[rows, cut] = (high_sin * low_cos + high_cos * low_sin).astype(jnp.bfloat16)
        first = pl.multiple_of(chip * pair // LANES * LANES, LANES)
        mine = []
        for ref in (cos_ref, sin_ref):
            value = ref[rows, pl.ds(first, LANES)]
            if pair < LANES:
                turn = (LANES - (chip * pair & (LANES - 1))) & (LANES - 1)
                value = pltpu.roll(value.astype(jnp.float32), turn, 1)[:, :pair]
                value = value.astype(jnp.bfloat16)
            mine.append(value)
        left_ref[step, 0:LANES, 0:pair] = mine[0]
        left_ref[step, 0:LANES, pair:] = mine[1]
        left_ref[step, LANES:, 0:pair] = -mine[1]
        left_ref[step, LANES:, pair:] = mine[0]

    keep = [
        pltpu.make_async_copy(cos_ref, cos_hbm, sems.at[1]),
        pltpu.make_async_copy(sin_ref, sin_hbm, sems.at[2]),
        pltpu.make_async_copy(left_ref, left_hbm, sems.at[3]),
    ]
    for copy in keep:
        copy.start()
    fetch.wait()

    @pl.loop(0, pixels // tile)
    def _(step):
        cut = pl.ds(pl.multiple_of(step * tile, tile), tile)
        spec[0, :, cut] = jnp.dot(raw_ref[...], cos_ref[:, cut], preferred_element_type=jnp.float32)
        spec[1, :, cut] = jnp.dot(raw_ref[...], sin_ref[:, cut], preferred_element_type=jnp.float32)

    image_row = index * slab + lax.broadcasted_iota(jnp.int32, (slab, LANES), 0)
    for which in range(angles):
        for m in range(1, others + 1):
            shift = MULTIPLES[m] * offset_ref[which, 0]
            around = ((image_row * shift + pixels // 2) & (pixels - 1)) - pixels // 2
            cosine, sine = turn_of(around.astype(jnp.float32) * (2.0 * math.pi / pixels))
            phase[which * others + m - 1, 0] = cosine
            phase[which * others + m - 1, 1] = sine

    lane = lax.broadcasted_iota(jnp.int32, (GROUP, LANES), 1)
    quarter_tiles = lane_tiles // 4

    def weight(which, m, j):
        column = order_ref[which, j]
        return unmix_ref[0, which, m, column], unmix_ref[1, which, m, column]

    def combine(terms, rows, slot):
        for tab in range(lane_tiles):
            cut = slice(tab * LANES, (tab + 1) * LANES)
            real = imag = None
            for frame, weight_re, weight_im in terms:
                here = pl.ds(pl.multiple_of(frame * slab + rows, GROUP), GROUP)
                cosine_sum = spec[0, here, cut]
                sine_sum = spec[1, here, cut]
                add_re = weight_re * cosine_sum + weight_im * sine_sum
                add_im = weight_im * cosine_sum - weight_re * sine_sum
                real = add_re if real is None else real + add_re
                imag = add_im if imag is None else imag + add_im
            turned[slot, 0, tab] = real
            turned[slot, 1, tab] = imag

    def put_out(band, rows, slot, shift):
        move = (-shift) & (pixels - 1)
        rest_lanes = move & (LANES - 1)
        turn = (LANES - rest_lanes) & (LANES - 1)
        for which, out in enumerate(parts):
            side = (1 - core) if which < 2 else core
            half = (1 - near) if which % 2 == 0 else near
            first = (2 * side + half) * quarter_tiles + move // LANES
            for part in range(2):
                tiles = [
                    pltpu.roll(turned[slot, part, (first + i) & (lane_tiles - 1)], turn, 1)
                    for i in range(quarter_tiles + 1)
                ]
                put = pl.ds(pl.multiple_of(part * slab + rows, GROUP), GROUP)
                for i in range(quarter_tiles):
                    out[band, put, i * LANES : (i + 1) * LANES] = jnp.where(
                        lane < LANES - rest_lanes, tiles[i], tiles[i + 1]
                    ).astype(jnp.bfloat16)

    def copies(step):
        done = []
        for which in range(4):
            for part in range(2):
                put = pl.ds(pl.multiple_of(part * slab + step * GROUP, GROUP), GROUP)
                done.append(
                    pltpu.make_async_copy(
                        parts[which].at[:, put, :],
                        outs[which].at[:, put, :],
                        row_sems.at[step, 2 * which + part],
                    )
                )
        return done

    @pl.loop(0, slab // GROUP)
    def _(step):
        rows = step * GROUP
        terms = [
            (which * phases + j, *weight(which, 0, j))
            for which in range(angles)
            for j in range(phases)
        ]
        combine(terms, rows, 0)
        put_out(0, rows, 0, 0)

        @pl.loop(0, angles * others)
        def _(band):
            which = band // others
            m = band - which * others + 1
            mult = jnp.where(m <= 2, 1, 2) * jnp.where(m & 1, 1, -1)
            here = pl.ds(pl.multiple_of(rows, GROUP), GROUP)
            phase_re = phase[band, 0, here, :]
            phase_im = phase[band, 1, here, :]
            terms = []
            for j in range(phases):
                weight_re, weight_im = weight(which, m, j)
                terms.append(
                    (
                        which * phases + j,
                        weight_re * phase_re - weight_im * phase_im,
                        weight_re * phase_im + weight_im * phase_re,
                    )
                )
            combine(terms, rows, 1)
            put_out(band + 1, rows, 1, mult * offset_ref[which, 1])

        for copy in copies(step):
            copy.start()

    for copy in keep:
        copy.wait()

    @pl.loop(0, slab // GROUP)
    def _(step):
        for copy in copies(step):
            copy.wait()


def numer_kernel(
    slab, bands, columns, masks, with_power, index_ref, offset_ref, own_ref, other_ref, left_ref,
    near_ref, far_ref, *rest
):
    outs = rest[:4]
    power_ref = rest[4] if with_power else None
    wide, total, right = rest[-3:]
    lane_tiles = wide.shape[0]
    pixels = lane_tiles * LANES
    tile = wide.shape[1] - pixels
    tiles = own_ref.shape[2] // LANES
    half = tiles // 2
    pieces = near_ref.shape[0]
    others = len(MULTIPLES) - 1
    index = index_ref[0]
    core = index & 1
    chip = index >> 1
    levels = (pixels // columns // 2).bit_length() - 1
    place = sum(((chip >> bit) & 1) << (levels - 1 - bit) for bit in range(levels))
    quarter = (chip & 1) if with_power else 1 - (chip & 1)
    start_column = (2 * core + quarter) * (pixels // 4)
    own_column = core * (pixels // 2) + place * columns

    def shift_of(band, axis):
        if band == 0:
            return 0
        which, m = divmod(band - 1, others)
        return MULTIPLES[m + 1] * offset_ref[which, axis]

    @pl.loop(0, bands)
    def _(band):
        for ref, side in ((own_ref, core), (other_ref, 1 - core)):
            for part in range(2):
                put = pl.ds(pl.multiple_of((2 * part + side) * slab, slab), slab)
                right[band, put, :] = ref[band, part * slab : (part + 1) * slab, :]

    for piece in range(2 * pieces):
        ref = far_ref if piece >= pieces else near_ref
        start = pl.multiple_of((index ^ masks[piece]) * slab, slab)
        for lane in range(lane_tiles):
            wide[lane, pl.ds(start, slab), :] = ref[
                piece % pieces, :, lane * LANES : (lane + 1) * LANES
            ].astype(jnp.float32)
    for lane in range(lane_tiles):
        wide[lane, pixels : pixels + tile, :] = wide[lane, 0:tile, :]

    lanes = lax.broadcasted_iota(jnp.int32, (tile, LANES), 1)

    def response(q0, band, column, count):
        start = (q0 - shift_of(band, 0)) & (pixels - 1)
        column = (column - shift_of(band, 1)) & (pixels - 1)
        rest_lanes = column & (LANES - 1)
        first = column // LANES
        turn = (LANES - rest_lanes) & (LANES - 1)
        turned = [
            pltpu.roll(wide[(first + i) & (lane_tiles - 1), pl.ds(start, tile), :], turn, 1)
            for i in range(count + 1)
        ]
        return [
            jnp.where(lanes < LANES - rest_lanes, turned[i], turned[i + 1]) for i in range(count)
        ]

    side = (chip >> 1) & 1

    def tile_of(step, upper):
        q0 = pl.multiple_of((step + upper * (pixels // tile // 2)) * tile, tile)
        to = pl.ds(pl.multiple_of(step * tile, tile), tile)
        left = left_ref[step + upper * (pixels // tile // 2)]
        for band in range(bands):
            product = jnp.dot(left, right[band], preferred_element_type=jnp.float32)
            weights = response(q0, band, start_column, tiles)
            for i in range(tiles):
                cut = slice(i * LANES, (i + 1) * LANES)
                for part in range(2):
                    value = weights[i] * product[part * tile : (part + 1) * tile, cut]
                    if band == 0:
                        total[i, part] = value
                    else:
                        total[i, part] += value
        for which in range(2):
            out = outs[2 * which + upper]
            first = (side if which == 1 else 1 - side) * half
            per_tile = LANES // columns
            for i in range(half):
                real = total[first + i, 0]
                imag = total[first + i, 1]
                for j in range(per_tile):
                    cut = slice(j * columns, (j + 1) * columns)
                    out[i * per_tile + j, to, :] = jnp.concatenate(
                        [real[:, cut], imag[:, cut]], axis=1
                    ).astype(jnp.bfloat16)
        if with_power:
            gathered = None
            for band in range(bands):
                value = response(q0, band, own_column, 1)[0]
                value = value * value
                if band == 0:
                    gathered = value * float((bands - 1) // others)
                else:
                    gathered = gathered + value
            power_ref[pl.ds(q0, tile), :] = jnp.concatenate(
                [gathered[:, :columns], gathered[:, :columns]], axis=1
            )

    for upper in range(2):
        pl.loop(0, pixels // tile // 2)(functools.partial(tile_of, upper=upper))


def image_kernel(back_ref, cos_ref, sin_ref, out_ref):
    devices, _, twice = back_ref.shape
    columns = twice // 2
    chips = devices // 2
    levels = chips.bit_length() - 1
    pixels = out_ref.shape[1]
    total = None
    for chip in range(chips):
        place = sum(((chip >> bit) & 1) << (levels - 1 - bit) for bit in range(levels))
        rows = []
        for core in range(2):
            start = core * (pixels // 2) + place * columns
            rows += [cos_ref[start : start + columns, :], sin_ref[start : start + columns, :]]
        left = jnp.concatenate([back_ref[2 * chip], back_ref[2 * chip + 1]], axis=1)
        value = jnp.dot(left, jnp.concatenate(rows, axis=0), preferred_element_type=jnp.float32)
        total = value if total is None else total + value
    out_ref[...] = total


def smem():
    return pl.BlockSpec(memory_space=pltpu.SMEM)


def vmem():
    return pl.BlockSpec(memory_space=pltpu.VMEM)


def swap(value, axis, mask):
    size = lax.axis_size(axis)
    return lax.ppermute(value, axis, [(i, i ^ mask) for i in range(size)])


def shards(raw, otf, offsets, phase_order, unmix):
    pixels = raw.shape[-1]
    slab = raw.shape[3]
    angles, phases = raw.shape[1:3]
    devices = lax.axis_size("row")
    index = lax.axis_index("row")
    slices = raw.shape[0] * lax.axis_size("cuts")
    chips = devices // 2
    levels = chips.bit_length() - 1
    chip = index >> 1
    columns = pixels // devices
    frames = angles * phases
    bands = 1 + angles * (len(MULTIPLES) - 1)

    mine = otf.reshape(slab, pixels).astype(jnp.bfloat16)
    masks = list(range(0, devices, 2))
    pieces = [mine] + [swap(mine, "row", mask) for mask in masks[1:]]
    masks += [mask | 1 for mask in masks]

    quarter = pixels // 4
    where = index.astype(jnp.int32).reshape(1)
    high, low = factors_of(pixels)
    table = jax.ShapeDtypeStruct((pixels, pixels), jnp.bfloat16)
    hbm = pl.BlockSpec(memory_space=pl.ANY)
    part = (bands, 2 * slab, quarter)
    left_shape = (pixels // LANES, 2 * LANES, 4 * slab)
    send_away, send_near, keep_away, keep_near, cosine, sine, left = pl.pallas_call(
        functools.partial(band_kernel, angles, phases),
        out_shape=[jax.ShapeDtypeStruct(part, jnp.bfloat16)] * 4
        + [table] * 2
        + [jax.ShapeDtypeStruct(left_shape, jnp.bfloat16)],
        in_specs=[smem()] * 4 + [hbm] + [vmem()] * 2,
        out_specs=[hbm] * 7,
        scratch_shapes=[pltpu.VMEM(part, jnp.bfloat16)] * 4
        + [
            pltpu.VMEM((frames * slab, pixels), jnp.bfloat16),
            pltpu.VMEM((pixels, pixels), jnp.bfloat16),
            pltpu.VMEM((pixels, pixels), jnp.bfloat16),
            pltpu.VMEM(left_shape, jnp.bfloat16),
            pltpu.VMEM((2, frames * slab, pixels), jnp.float32),
            pltpu.VMEM((2, 2, pixels // LANES, GROUP, LANES), jnp.float32),
            pltpu.VMEM((bands - 1, 2, slab, LANES), jnp.float32),
            pltpu.SemaphoreType.DMA((4,)),
            pltpu.SemaphoreType.DMA((slab // GROUP, 8)),
        ],
        cost_estimate=pl.CostEstimate(
            flops=8 * frames * slab * pixels * pixels,
            bytes_accessed=12 << 20,
            transcendentals=0,
        ),
        name="bands",
    )(where, unmix, phase_order, offsets, raw.reshape(frames * slab, pixels), high, low)

    got_away = swap(send_away, "row", 1)
    own_pieces = jnp.stack(pieces)
    other_pieces = swap(own_pieces, "row", 1)
    got_near = swap(send_near, "row", 1)

    def partial(own, other, with_power):
        half_shape = (chips // 4, pixels // 2, 2 * columns)
        out_shape = [jax.ShapeDtypeStruct(half_shape, jnp.bfloat16)] * 4
        if with_power:
            out_shape = out_shape + [jax.ShapeDtypeStruct((pixels, 2 * columns), jnp.float32)]
        return pl.pallas_call(
            functools.partial(numer_kernel, slab, bands, columns, masks, with_power),
            out_shape=out_shape,
            in_specs=[smem()] * 2 + [vmem()] * 5,
            out_specs=[vmem()] * len(out_shape),
            scratch_shapes=[
                pltpu.VMEM((pixels // LANES, pixels + LANES, LANES), jnp.float32),
                pltpu.VMEM((quarter // LANES, 2, LANES, LANES), jnp.float32),
                pltpu.VMEM((bands, 4 * slab, quarter), jnp.bfloat16),
            ],
            cost_estimate=pl.CostEstimate(
                flops=16 * bands * slab * pixels * quarter,
                bytes_accessed=8 << 20,
                transcendentals=0,
            ),
        )(where, offsets, own, other, left, own_pieces, other_pieces)

    away = partial(keep_away, got_away, False)
    moved = [swap(value, "row", 2) for value in away]
    *kept, power = partial(keep_near, got_near, True)

    def split(blocks, bit):
        count = blocks.shape[0] // 2
        side = (chip >> bit) & 1
        return (
            lax.dynamic_slice_in_dim(blocks, (1 - side) * count, count, 0),
            lax.dynamic_slice_in_dim(blocks, side * count, count, 0),
        )

    def widen(value):
        return value.astype(jnp.float32)

    fars = [widen(moved[h]) + widen(kept[h]) for h in range(2)]
    stays = [widen(moved[2 + h]) + widen(kept[2 + h]) for h in range(2)]
    for bit in range(1, levels):
        got_next = [swap(far.astype(jnp.bfloat16), "row", 2 << bit) for far in fars]
        stays = [stay + widen(got) for stay, got in zip(stays, got_next)]
        if bit < levels - 1:
            fars, stays = zip(*[split(stay, bit + 1) for stay in stays])
    numer = jnp.concatenate([stay[0] for stay in stays])

    total_power = power
    moving = power
    cuts = lax.axis_size("cuts")
    for _ in range(cuts - 1):
        moving = lax.ppermute(moving, "cuts", [(i, (i + 1) % cuts) for i in range(cuts)])
        total_power = total_power + moving
    denom = WIENER + total_power / (slices * angles)
    ratio = (numer / denom).astype(jnp.bfloat16)

    by_cos = jnp.dot(cosine, ratio, preferred_element_type=jnp.float32)
    by_sin = jnp.dot(sine, ratio, preferred_element_type=jnp.float32)
    half = jnp.concatenate(
        [
            by_cos[:, :columns] - by_sin[:, columns:],
            -by_cos[:, columns:] - by_sin[:, :columns],
        ],
        axis=1,
    ).astype(jnp.bfloat16)
    back = lax.all_to_all(
        half.reshape(devices, slab, 2 * columns), "row", split_axis=0, concat_axis=0, tiled=True
    )
    recon = pl.pallas_call(
        image_kernel,
        out_shape=jax.ShapeDtypeStruct((slab, pixels), jnp.float32),
        in_specs=[vmem()] * 3,
        out_specs=vmem(),
        cost_estimate=pl.CostEstimate(
            flops=4 * slab * pixels * pixels, bytes_accessed=6 << 20, transcendentals=0
        ),
        name="image",
    )(back, cosine, sine)
    return recon.reshape(otf.shape)


def solution(mesh):
    in_specs = (P("cuts", None, None, "row", None), P("cuts", "row", None), P(), P(), P())
    out_specs = P("cuts", "row", None)

    return jax.shard_map(shards, mesh=mesh, in_specs=in_specs, out_specs=out_specs, check_vma=False)
```

time: 143 us -> 138 us (0.965)
  starting transfers between devices: 15.5 us -> 32 us
  waiting for transfers between devices: 34.6 us -> 22.2 us
  other arithmetic: 12.4 us -> 5.59 us
    ppermute x13 -> x18, starting transfers between devices: 14 us -> 30.5 us  [swap(): return lax.ppermute(value, axis, [(i, i ^ mask) for i in range(size)])]
    ppermute x13 -> x18, waiting for transfers between devices: 34.6 us -> 22.2 us  [swap(): return lax.ppermute(value, axis, [(i, i ^ mask) for i in range(size)])]
    unnamed x17 -> x26, local copies, waits for them, and re-layouts: 1.84 us -> 6.2 us
    another operation x7 -> x1, other arithmetic: 2.03 us -> 0.06 us  [the longest x1 1.1 us: shards(): jnp.stack([jnp.concatenate([cos_own, sin_own, cos_other, sin_other], axis...]
    convert_element_type x2 -> x3, other arithmetic: 1.93 us -> 3.05 us  [the longest x2 2.09 us: shards(): got_next = [swap(far.astype(jnp.bfloat16), 'row', 2 << bit) for far in fars]]
  transfers between devices with their start and end apart: 14 -> 19, of which waited for: 5 -> 6; matrix products, arithmetic and copies ran while one was open for 10% -> 5% of each run, Pallas kernels for 37% -> 37%
where the time goes in v2:
time: 138 us
  Pallas kernels  55.4 us (40%)
  starting transfers between devices  32 us (23%)
  waiting for transfers between devices  22.2 us (16%)
  blocking collectives  13.8 us (10%)
  local copies, waits for them, and re-layouts  6.6 us (5%)
  other arithmetic  5.59 us (4%)
  matrix products  1.65 us (1%)
    ppermute x18, starting transfers between devices, swap(): return lax.ppermute(value, axis, [(i, i ^ mask) for i in range(size)])  30.5 us
    pallas_call x2, Pallas kernels, partial(): pl.pallas_call(functools.partial(numer_kernel, slab, bands, columns, mask...  28.4 us
    pallas_call x1, Pallas kernels, shards(): pl.pallas_call(functools.partial(band_kernel, angles, phases), out_shape=...  23.2 us
    ppermute x18, waiting for transfers between devices, swap(): return lax.ppermute(value, axis, [(i, i ^ mask) for i in range(size)])  22.2 us
    all_to_all x1, blocking collectives, shards(): lax.all_to_all(half.reshape(devices, slab, 2 * columns), 'row', split_axi...  13.8 us
    unnamed x26, local copies, waits for them, and re-layouts  6.2 us
    pallas_call x1, Pallas kernels, shards(): pl.pallas_call(image_kernel, out_shape=jax.ShapeDtypeStruct((slab, pixels...  3.85 us
  transfers between devices with their start and end apart: 19, of which 6 were waited for; matrix products, arithmetic and copies ran while one was open for 5% of the time, Pallas kernels for 37%

profile of v2, /device:TPU:0, one launch (start us, length us, event | category | flops | bytes accessed | tf_op | source)
XLA Modules:
  0.0 137.5 jit_solution(13961848767822916981)
XLA Ops:
  0.0 1.0 convert_bitcast_fusion
  1.0 3.1 %collective-permute-start.1 = (bf16[64,1024]{1,0:T(8,128)(2,1)S(1)}, bf16[64,1024]{1,0:T(8,128)(2,1)S(1)}, u32[]{:S(2)}, u32[]{:S(2)}) collective-permute-start(bf16[64,1024]{1,0:T(8,128)(2,1)S(1)} %convert_bitcast_fusion), channel_id=1, source_target_pairs={{0,2},{1,3},{2,0},{3,1},{4,6},{5,7},{6,4},{7,5},{8,10},{9,11},{10,... | collective-permute-start | bytes 393224 | tf_op jit(solution)/shard_map/ppermute | solution.py:353
  4.0 1.6 %collective-permute-start.2 = (bf16[64,1024]{1,0:T(8,128)(2,1)S(1)}, bf16[64,1024]{1,0:T(8,128)(2,1)S(1)}, u32[]{:S(2)}, u32[]{:S(2)}) collective-permute-start(bf16[64,1024]{1,0:T(8,128)(2,1)S(1)} %convert_bitcast_fusion), channel_id=1, source_target_pairs={{0,4},{1,5},{2,6},{3,7},{4,0},{5,1},{6,2},{7,3},{8,12},{9,13},{10,... | collective-permute-start | bytes 393224 | tf_op jit(solution)/shard_map/ppermute | solution.py:353
  5.6 0.0 collective-permute-start.3
  5.6 3.0 %collective-permute-start.4 = (bf16[64,1024]{1,0:T(8,128)(2,1)S(1)}, bf16[64,1024]{1,0:T(8,128)(2,1)S(1)}, u32[]{:S(2)}, u32[]{:S(2)}) collective-permute-start(bf16[64,1024]{1,0:T(8,128)(2,1)S(1)} %convert_bitcast_fusion), channel_id=1, source_target_pairs={{0,8},{1,9},{2,10},{3,11},{4,12},{5,13},{6,14},{7,15},{8,0},{9,1},... | collective-permute-start | bytes 393224 | tf_op jit(solution)/shard_map/ppermute | solution.py:353
  8.6 1.3 collective-permute-start.5
  9.9 1.4 copy.9.offset_ref
  11.2 1.3 copy.8.unmix_ref
  12.6 1.0 convert_dynamic-update-slice_fusion
  13.5 0.0 collective-permute-done.1
  13.5 3.7 %collective-permute-start.6 = (bf16[64,1024]{1,0:T(8,128)(2,1)S(1)}, bf16[64,1024]{1,0:T(8,128)(2,1)S(1)}, u32[]{:S(2)}, u32[]{:S(2)}) collective-permute-start(bf16[64,1024]{1,0:T(8,128)(2,1)S(1)} %convert_bitcast_fusion), channel_id=1, source_target_pairs={{0,12},{1,13},{2,14},{3,15},{4,8},{5,9},{6,10},{7,11},{8,4},{9,5},... | collective-permute-start | bytes 393224 | tf_op jit(solution)/shard_map/ppermute | solution.py:353
  17.2 0.0 collective-permute-done.2
  17.2 0.1 collective-permute-start.7
  17.3 0.0 collective-permute-done.3
  17.4 0.0 collective-permute-done.4
  17.4 10.7 %collective-permute-done.5 = bf16[64,1024]{1,0:T(8,128)(2,1)S(1)} collective-permute-done((bf16[64,1024]{1,0:T(8,128)(2,1)S(1)}, bf16[64,1024]{1,0:T(8,128)(2,1)S(1)}, u32[]{:S(2)}, u32[]{:S(2)}) %collective-permute-start.5) | collective-permute-done | bytes 131104 | tf_op jit(solution)/shard_map/ppermute | solution.py:353
  28.0 0.0 collective-permute-done.6
  28.1 0.0 collective-permute-done.7
  28.1 0.0 copy-start.4
  28.1 0.1 collective-permute-start.8
  28.2 23.2 %bands.1 = (bf16[13,128,256]{2,1,0:T(8,128)(2,1)}, bf16[13,128,256]{2,1,0:T(8,128)(2,1)}, bf16[13,128,256]{2,1,0:T(8,128)(2,1)}, bf16[13,128,256]{2,1,0:T(8,128)...) custom-call(s32[1]{0:T(128)} %bitcast.index_ref, ...), custom_call_target="tpu_custom_call" | custom-call | flops 8053063680 | bytes 12582912 | tf_op jit(solution)/shard_map/bands/pallas_call | solution.py:382
  51.4 0.3 collective-permute-start
  51.7 0.3 collective-permute-start.10
  51.9 2.1 %collective-permute-done.other_ref = bf16[13,128,256]{2,1,0:T(8,128)(2,1)S(1)} collective-permute-done((bf16[13,128,256]{2,1,0:T(8,128)(2,1)}, bf16[13,128,256]{2,1,0:T(8,128)(2,1)S(1)}, u32[]{:S(2)}, u32[]{:S(2)}) %collective-permute-start) | collective-permute-done | bytes 852000 | tf_op jit(solution)/shard_map/ppermute | solution.py:353
  54.0 0.0 collective-permute-done.8.far_ref
  54.0 0.9 copy-done.7
  54.9 1.0 copy-done.5
  55.9 12.0 %shard_map.73 = (bf16[2,512,128]{2,1,0:T(8,128)(2,1)}, bf16[2,512,128]{2,1,0:T(8,128)(2,1)}, bf16[2,512,128]{2,1,0:T(8,128)(2,1)}, bf16[2,512,128]{2,1,0:T(8,128)(2,1)}) custom-call(s32[1]{0:T(128)} %bitcast.index_ref, s32[3,2]{1,0:T(4,128)} %copy.9.offset_ref, bf16[13,128,256]{2,1,0:T(8,128)(2,1)} %get-tuple-element.22.own_ref, ...), custom_call_target="tpu_custom_call" | custom-call | flops 3489660928 | bytes 8388608 | tf_op jit(solution)/shard_map/pallas_call | solution.py:419
  67.9 0.1 collective-permute-start.11
  68.0 1.9 %collective-permute-start.9 = (bf16[2,512,128]{2,1,0:T(8,128)(2,1)}, bf16[2,512,128]{2,1,0:T(8,128)(2,1)S(1)}, u32[]{:S(2)}, u32[]{:S(2)}) collective-permute-start(bf16[2,512,128]{2,1,0:T(8,128)(2,1)} %get-tuple-element.25), channel_id=1, source_target_pairs={{0,2},{1,3},{2,0},{3,1},{4,6},{5,7},{6,4},{7,5},{8,10},{9,11},{10,... | collective-permute-start | bytes 786440 | tf_op jit(solution)/shard_map/ppermute | solution.py:353
  69.9 0.1 collective-permute-start.15
  70.0 0.0 collective-permute-done.10.other_ref
  70.0 1.0 copy-done.6
  71.0 16.4 %shard_map.74 = (bf16[2,512,128]{2,1,0:T(8,128)(2,1)}, bf16[2,512,128]{2,1,0:T(8,128)(2,1)}, bf16[2,512,128]{2,1,0:T(8,128)(2,1)}, bf16[2,512,128]{2,1,0:T(8,128)(2,1)}, f32[1024,128]{1,0:T(8,128)}) custom-call(s32[1]{0:T(128)} %bitcast.index_ref, s32[3,2]{1,0:T(4,128)} %copy.9.offset_ref, bf16[13,128,256]{2,1,0:T(8,128)(2,1)} %get-tuple-element.26.own_ref, ...), custom_call_target="tpu_custom_call" | custom-call | flops 3489660928 | bytes 8388608 | tf_op jit(solution)/shard_map/pallas_call | solution.py:419
  87.4 0.0 collective-permute-done.11
  87.4 1.1 add_convert_fusion.1
  88.5 5.4 %collective-permute-start.12 = (bf16[2,512,128]{2,1,0:T(8,128)(2,1)S(1)}, bf16[2,512,128]{2,1,0:T(8,128)(2,1)S(1)}, u32[]{:S(2)}, u32[]{:S(2)}) collective-permute-start(bf16[2,512,128]{2,1,0:T(8,128)(2,1)S(1)} %add_convert_fusion.1), channel_id=1, source_target_pairs={{0,4},{1,5},{2,6},{3,7},{4,0},{5,1},{6,2},{7,3},{8,12},{9,13},{10,... | collective-permute-start | bytes 786440 | tf_op jit(solution)/shard_map/ppermute | solution.py:353
  93.9 1.6 %collective-permute-start.14 = (bf16[2,512,128]{2,1,0:T(8,128)(2,1)S(1)}, bf16[2,512,128]{2,1,0:T(8,128)(2,1)S(1)}, u32[]{:S(2)}, u32[]{:S(2)}) collective-permute-start(bf16[2,512,128]{2,1,0:T(8,128)(2,1)S(1)} %copy-done.8), channel_id=1, source_target_pairs={{0,2},{1,3},{2,0},{3,1},{4,6},{5,7},{6,4},{7,5},{8,10},{9,11},{10,... | collective-permute-start | bytes 786440 | tf_op jit(solution)/shard_map/ppermute | solution.py:353
  95.5 1.5 %collective-permute-start.18 = (f32[1024,128]{1,0:T(8,128)}, f32[1024,128]{1,0:T(8,128)S(1)}, u32[]{:S(2)}, u32[]{:S(2)}) collective-permute-start(f32[1024,128]{1,0:T(8,128)} %get-tuple-element.35), channel_id=1, source_target_pairs={{0,16},{16,0},{1,17},{17,1},{2,18},{18,2},{3,19},{19,3},{4,20},{20... | collective-permute-start | bytes 1572872 | tf_op jit(solution)/shard_map/ppermute | solution.py:464
  96.9 0.0 collective-permute-done.15
  96.9 1.0 add_convert_fusion
  98.0 0.2 collective-permute-start.16
  98.1 0.0 collective-permute-done.9
  98.1 2.4 %collective-permute-done.12 = bf16[2,512,128]{2,1,0:T(8,128)(2,1)S(1)} collective-permute-done((bf16[2,512,128]{2,1,0:T(8,128)(2,1)S(1)}, bf16[2,512,128]{2,1,0:T(8,128)(2,1)S(1)}, u32[]{:S(2)}, u32[]{:S(2)}) %collective-permute-start.12) | collective-permute-done | bytes 262176 | tf_op jit(solution)/shard_map/ppermute | solution.py:353
  100.6 1.1 convert_add_fusion.1
  101.7 4.2 %collective-permute-start.13 = (bf16[1,512,128]{2,1,0:T(8,128)(2,1)S(1)}, bf16[1,512,128]{2,1,0:T(8,128)(2,1)S(1)}, u32[]{:S(2)}, u32[]{:S(2)}) collective-permute-start(bf16[1,512,128]{2,1,0:T(8,128)(2,1)S(1)} %dynamic-slice_convert_fusion.1), channel_id=1, source_target_pairs={{0,8},{1,9},{2,10},{3,11},{4,12},{5,13},{6,14},{7,15},{8,0},{9,1},... | collective-permute-start | bytes 393224 | tf_op jit(solution)/shard_map/ppermute | solution.py:353
  105.9 0.0 collective-permute-done.14
  105.9 0.8 collective-permute-done.16
  106.7 0.1 convert_add_fusion
  106.8 3.7 %collective-permute-start.17 = (bf16[1,512,128]{2,1,0:T(8,128)(2,1)S(1)}, bf16[1,512,128]{2,1,0:T(8,128)(2,1)S(1)}, u32[]{:S(2)}, u32[]{:S(2)}) collective-permute-start(bf16[1,512,128]{2,1,0:T(8,128)(2,1)S(1)} %dynamic-slice_convert_fusion), channel_id=1, source_target_pairs={{0,8},{1,9},{2,10},{3,11},{4,12},{5,13},{6,14},{7,15},{8,0},{9,1},... | collective-permute-start | bytes 393224 | tf_op jit(solution)/shard_map/ppermute | solution.py:353
  110.5 4.5 %collective-permute-done.13 = bf16[1,512,128]{2,1,0:T(8,128)(2,1)S(1)} collective-permute-done((bf16[1,512,128]{2,1,0:T(8,128)(2,1)S(1)}, bf16[1,512,128]{2,1,0:T(8,128)(2,1)S(1)}, u32[]{:S(2)}, u32[]{:S(2)}) %collective-permute-start.13) | collective-permute-done | bytes 131104 | tf_op jit(solution)/shard_map/ppermute | solution.py:353
  115.1 1.8 %collective-permute-done.17 = bf16[1,512,128]{2,1,0:T(8,128)(2,1)S(1)} collective-permute-done((bf16[1,512,128]{2,1,0:T(8,128)(2,1)S(1)}, bf16[1,512,128]{2,1,0:T(8,128)(2,1)S(1)}, u32[]{:S(2)}, u32[]{:S(2)}) %collective-permute-start.17) | collective-permute-done | bytes 131104 | tf_op jit(solution)/shard_map/ppermute | solution.py:353
  116.9 0.0 collective-permute-done.18
  116.9 0.1 fusion
  117.0 0.0 copy-done
  117.0 0.8 fusion.3
  117.9 0.6 copy-done.1
  118.4 0.8 fusion.4
  119.3 0.1 fusion.2
  119.3 0.2 copy.12
  119.5 0.2 copy.13
  119.7 0.2 pad_maximum_fusion
  119.9 13.8 %all_to_all.5.back_ref = bf16[16,64,128]{2,1,0:T(8,128)(2,1)} all-to-all(bf16[16,64,128]{2,1,0:T(8,128)(2,1)S(1)} %pad_maximum_fusion), channel_id=1, replica_groups=mesh['cuts'=2,'row'=16] {'row'}, dimensions={0} | all-to-all | bytes 524288 | tf_op jit(solution)/shard_map/all_to_all | solution.py:478
  133.7 3.9 %image.1 = f32[64,1024]{1,0:T(8,128)} custom-call(bf16[16,64,128]{2,1,0:T(8,128)(2,1)} %all_to_all.5.back_ref, bf16[1024,1024]{1,0:T(8,128)(2,1)} %get-tuple-element.21.cos_ref, bf16[1024,1024]{1,0:T(8,128)(2,1)} %get-tuple-element.36.sin_ref), custom_call_target="tpu_custom_call" | custom-call | flops 268435456 | bytes 6291456 | tf_op jit(solution)/shard_map/image/pallas_call | solution.py:481
  (23 shorter events, 0.2 us)
Async XLA Ops:
  1.0 12.6 %collective-permute-start.1 = (bf16[64,1024]{1,0:T(8,128)(2,1)S(1)}, bf16[64,1024]{1,0:T(8,128)(2,1)S(1)}, u32[]{:S(2)}, u32[]{:S(2)}) collective-permute-start(bf16[64,1024]{1,0:T(8,128)(2,1)S(1)} %convert_bitcast_fusion), channel_id=1, source_target_pairs={{0,2},{1,3},{2,0},{3,1},{4,6},{5,7},{6,4},{7,5},{8,10},{9,11},{10,... | collective-permute-start | bytes 393224 | tf_op jit(solution)/shard_map/ppermute | solution.py:353
  4.0 13.2 %collective-permute-start.2 = (bf16[64,1024]{1,0:T(8,128)(2,1)S(1)}, bf16[64,1024]{1,0:T(8,128)(2,1)S(1)}, u32[]{:S(2)}, u32[]{:S(2)}) collective-permute-start(bf16[64,1024]{1,0:T(8,128)(2,1)S(1)} %convert_bitcast_fusion), channel_id=1, source_target_pairs={{0,4},{1,5},{2,6},{3,7},{4,0},{5,1},{6,2},{7,3},{8,12},{9,13},{10,... | collective-permute-start | bytes 393224 | tf_op jit(solution)/shard_map/ppermute | solution.py:353
  5.6 11.7 %collective-permute-start.3 = (bf16[64,1024]{1,0:T(8,128)(2,1)S(1)}, bf16[64,1024]{1,0:T(8,128)(2,1)S(1)}, u32[]{:S(2)}, u32[]{:S(2)}) collective-permute-start(bf16[64,1024]{1,0:T(8,128)(2,1)S(1)} %convert_bitcast_fusion), channel_id=1, source_target_pairs={{0,6},{1,7},{2,4},{3,5},{4,2},{5,3},{6,0},{7,1},{8,14},{9,15},{10,... | collective-permute-start | bytes 393224 | tf_op jit(solution)/shard_map/ppermute | solution.py:353
  5.6 11.7 %collective-permute-start.4 = (bf16[64,1024]{1,0:T(8,128)(2,1)S(1)}, bf16[64,1024]{1,0:T(8,128)(2,1)S(1)}, u32[]{:S(2)}, u32[]{:S(2)}) collective-permute-start(bf16[64,1024]{1,0:T(8,128)(2,1)S(1)} %convert_bitcast_fusion), channel_id=1, source_target_pairs={{0,8},{1,9},{2,10},{3,11},{4,12},{5,13},{6,14},{7,15},{8,0},{9,1},... | collective-permute-start | bytes 393224 | tf_op jit(solution)/shard_map/ppermute | solution.py:353
  8.6 19.4 %collective-permute-start.5 = (bf16[64,1024]{1,0:T(8,128)(2,1)S(1)}, bf16[64,1024]{1,0:T(8,128)(2,1)S(1)}, u32[]{:S(2)}, u32[]{:S(2)}) collective-permute-start(bf16[64,1024]{1,0:T(8,128)(2,1)S(1)} %convert_bitcast_fusion), channel_id=1, source_target_pairs={{0,10},{1,11},{2,8},{3,9},{4,14},{5,15},{6,12},{7,13},{8,2},{9,3},... | collective-permute-start | bytes 393224 | tf_op jit(solution)/shard_map/ppermute | solution.py:353
  13.5 14.5 %collective-permute-start.6 = (bf16[64,1024]{1,0:T(8,128)(2,1)S(1)}, bf16[64,1024]{1,0:T(8,128)(2,1)S(1)}, u32[]{:S(2)}, u32[]{:S(2)}) collective-permute-start(bf16[64,1024]{1,0:T(8,128)(2,1)S(1)} %convert_bitcast_fusion), channel_id=1, source_target_pairs={{0,12},{1,13},{2,14},{3,15},{4,8},{5,9},{6,10},{7,11},{8,4},{9,5},... | collective-permute-start | bytes 393224 | tf_op jit(solution)/shard_map/ppermute | solution.py:353
  17.2 10.9 %collective-permute-start.7 = (bf16[64,1024]{1,0:T(8,128)(2,1)S(1)}, bf16[64,1024]{1,0:T(8,128)(2,1)S(1)}, u32[]{:S(2)}, u32[]{:S(2)}) collective-permute-start(bf16[64,1024]{1,0:T(8,128)(2,1)S(1)} %convert_bitcast_fusion), channel_id=1, source_target_pairs={{0,14},{1,15},{2,12},{3,13},{4,10},{5,11},{6,8},{7,9},{8,6},{9,7},... | collective-permute-start | bytes 393224 | tf_op jit(solution)/shard_map/ppermute | solution.py:353
  28.1 23.3 %copy-start.4 = (bf16[8,64,1024]{2,1,0:T(8,128)(2,1)}, bf16[8,64,1024]{2,1,0:T(8,128)(2,1)S(1)}, u32[]{:S(2)}) copy-start(bf16[8,64,1024]{2,1,0:T(8,128)(2,1)S(1)} %bitcast_dynamic-update-slice_fusion.near_ref) | copy-start | bytes 3145732
  28.1 25.9 %collective-permute-start.8 = (bf16[8,64,1024]{2,1,0:T(8,128)(2,1)S(1)}, bf16[8,64,1024]{2,1,0:T(8,128)(2,1)S(1)}, u32[]{:S(2)}, u32[]{:S(2)}) collective-permute-start(bf16[8,64,1024]{2,1,0:T(8,128)(2,1)S(1)} %bitcast_dynamic-update-slice_fusion.near_ref), channel_id=1, source_target_pairs={{0,1},{1,0},{2,3},{3,2},{4,5},{5,4},{6,7},{7,6},{8,9},{9,8},{10,11... | collective-permute-start | bytes 3145736 | tf_op jit(solution)/shard_map/ppermute | solution.py:353
  51.4 2.7 %collective-permute-start = (bf16[13,128,256]{2,1,0:T(8,128)(2,1)}, bf16[13,128,256]{2,1,0:T(8,128)(2,1)S(1)}, u32[]{:S(2)}, u32[]{:S(2)}) collective-permute-start(bf16[13,128,256]{2,1,0:T(8,128)(2,1)} %get-tuple-element.23), channel_id=1, source_target_pairs={{0,1},{1,0},{2,3},{3,2},{4,5},{5,4},{6,7},{7,6},{8,9},{9,8},{10,11... | collective-permute-start | bytes 2555912 | tf_op jit(solution)/shard_map/ppermute | solution.py:353
  51.7 18.3 %collective-permute-start.10 = (bf16[13,128,256]{2,1,0:T(8,128)(2,1)}, bf16[13,128,256]{2,1,0:T(8,128)(2,1)S(1)}, u32[]{:S(2)}, u32[]{:S(2)}) collective-permute-start(bf16[13,128,256]{2,1,0:T(8,128)(2,1)} %get-tuple-element.27), channel_id=1, source_target_pairs={{0,1},{1,0},{2,3},{3,2},{4,5},{5,4},{6,7},{7,6},{8,9},{9,8},{10,11... | collective-permute-start | bytes 2555912 | tf_op jit(solution)/shard_map/ppermute | solution.py:353
  54.0 0.9 copy-start.7
  54.9 1.0 copy-start.5
  67.9 19.5 %collective-permute-start.11 = (bf16[2,512,128]{2,1,0:T(8,128)(2,1)}, bf16[2,512,128]{2,1,0:T(8,128)(2,1)S(1)}, u32[]{:S(2)}, u32[]{:S(2)}) collective-permute-start(bf16[2,512,128]{2,1,0:T(8,128)(2,1)} %get-tuple-element.29), channel_id=1, source_target_pairs={{0,2},{1,3},{2,0},{3,1},{4,6},{5,7},{6,4},{7,5},{8,10},{9,11},{10,... | collective-permute-start | bytes 786440 | tf_op jit(solution)/shard_map/ppermute | solution.py:353
  68.0 30.2 %collective-permute-start.9 = (bf16[2,512,128]{2,1,0:T(8,128)(2,1)}, bf16[2,512,128]{2,1,0:T(8,128)(2,1)S(1)}, u32[]{:S(2)}, u32[]{:S(2)}) collective-permute-start(bf16[2,512,128]{2,1,0:T(8,128)(2,1)} %get-tuple-element.25), channel_id=1, source_target_pairs={{0,2},{1,3},{2,0},{3,1},{4,6},{5,7},{6,4},{7,5},{8,10},{9,11},{10,... | collective-permute-start | bytes 786440 | tf_op jit(solution)/shard_map/ppermute | solution.py:353
  69.9 27.0 %collective-permute-start.15 = (bf16[2,512,128]{2,1,0:T(8,128)(2,1)}, bf16[2,512,128]{2,1,0:T(8,128)(2,1)S(1)}, u32[]{:S(2)}, u32[]{:S(2)}) collective-permute-start(bf16[2,512,128]{2,1,0:T(8,128)(2,1)} %get-tuple-element.33), channel_id=1, source_target_pairs={{0,2},{1,3},{2,0},{3,1},{4,6},{5,7},{6,4},{7,5},{8,10},{9,11},{10,... | collective-permute-start | bytes 786440 | tf_op jit(solution)/shard_map/ppermute | solution.py:353
  70.0 1.0 copy-start.6
  71.0 22.9 %copy-start.8 = (bf16[2,512,128]{2,1,0:T(8,128)(2,1)S(1)}, bf16[2,512,128]{2,1,0:T(8,128)(2,1)}, u32[]{:S(2)}) copy-start(bf16[2,512,128]{2,1,0:T(8,128)(2,1)} %get-tuple-element.31) | copy-start | bytes 786436
  87.4 19.3 %copy-start.3 = (bf16[2,512,128]{2,1,0:T(8,128)(2,1)S(1)}, bf16[2,512,128]{2,1,0:T(8,128)(2,1)}, u32[]{:S(2)}) copy-start(bf16[2,512,128]{2,1,0:T(8,128)(2,1)} %get-tuple-element.32) | copy-start | bytes 786436
  88.5 12.1 %collective-permute-start.12 = (bf16[2,512,128]{2,1,0:T(8,128)(2,1)S(1)}, bf16[2,512,128]{2,1,0:T(8,128)(2,1)S(1)}, u32[]{:S(2)}, u32[]{:S(2)}) collective-permute-start(bf16[2,512,128]{2,1,0:T(8,128)(2,1)S(1)} %add_convert_fusion.1), channel_id=1, source_target_pairs={{0,4},{1,5},{2,6},{3,7},{4,0},{5,1},{6,2},{7,3},{8,12},{9,13},{10,... | collective-permute-start | bytes 786440 | tf_op jit(solution)/shard_map/ppermute | solution.py:353
  93.9 12.0 %collective-permute-start.14 = (bf16[2,512,128]{2,1,0:T(8,128)(2,1)S(1)}, bf16[2,512,128]{2,1,0:T(8,128)(2,1)S(1)}, u32[]{:S(2)}, u32[]{:S(2)}) collective-permute-start(bf16[2,512,128]{2,1,0:T(8,128)(2,1)S(1)} %copy-done.8), channel_id=1, source_target_pairs={{0,2},{1,3},{2,0},{3,1},{4,6},{5,7},{6,4},{7,5},{8,10},{9,11},{10,... | collective-permute-start | bytes 786440 | tf_op jit(solution)/shard_map/ppermute | solution.py:353
  95.5 21.4 %collective-permute-start.18 = (f32[1024,128]{1,0:T(8,128)}, f32[1024,128]{1,0:T(8,128)S(1)}, u32[]{:S(2)}, u32[]{:S(2)}) collective-permute-start(f32[1024,128]{1,0:T(8,128)} %get-tuple-element.35), channel_id=1, source_target_pairs={{0,16},{16,0},{1,17},{17,1},{2,18},{18,2},{3,19},{19,3},{4,20},{20... | collective-permute-start | bytes 1572872 | tf_op jit(solution)/shard_map/ppermute | solution.py:464
  98.0 8.7 %collective-permute-start.16 = (bf16[2,512,128]{2,1,0:T(8,128)(2,1)S(1)}, bf16[2,512,128]{2,1,0:T(8,128)(2,1)S(1)}, u32[]{:S(2)}, u32[]{:S(2)}) collective-permute-start(bf16[2,512,128]{2,1,0:T(8,128)(2,1)S(1)} %add_convert_fusion), channel_id=1, source_target_pairs={{0,4},{1,5},{2,6},{3,7},{4,0},{5,1},{6,2},{7,3},{8,12},{9,13},{10,... | collective-permute-start | bytes 786440 | tf_op jit(solution)/shard_map/ppermute | solution.py:353
  100.6 16.3 %copy-start.2 = (f32[1024,128]{1,0:T(8,128)S(1)}, f32[1024,128]{1,0:T(8,128)}, u32[]{:S(2)}) copy-start(f32[1024,128]{1,0:T(8,128)} %get-tuple-element.35) | copy-start | bytes 1572868
  101.7 13.3 %collective-permute-start.13 = (bf16[1,512,128]{2,1,0:T(8,128)(2,1)S(1)}, bf16[1,512,128]{2,1,0:T(8,128)(2,1)S(1)}, u32[]{:S(2)}, u32[]{:S(2)}) collective-permute-start(bf16[1,512,128]{2,1,0:T(8,128)(2,1)S(1)} %dynamic-slice_convert_fusion.1), channel_id=1, source_target_pairs={{0,8},{1,9},{2,10},{3,11},{4,12},{5,13},{6,14},{7,15},{8,0},{9,1},... | collective-permute-start | bytes 393224 | tf_op jit(solution)/shard_map/ppermute | solution.py:353
  106.7 10.3 %copy-start = (bf16[1024,1024]{1,0:T(8,128)(2,1)S(1)}, bf16[1024,1024]{1,0:T(8,128)(2,1)}, u32[]{:S(2)}) copy-start(bf16[1024,1024]{1,0:T(8,128)(2,1)} %get-tuple-element.21.cos_ref) | copy-start | bytes 6291460
  106.8 10.0 %collective-permute-start.17 = (bf16[1,512,128]{2,1,0:T(8,128)(2,1)S(1)}, bf16[1,512,128]{2,1,0:T(8,128)(2,1)S(1)}, u32[]{:S(2)}, u32[]{:S(2)}) collective-permute-start(bf16[1,512,128]{2,1,0:T(8,128)(2,1)S(1)} %dynamic-slice_convert_fusion), channel_id=1, source_target_pairs={{0,8},{1,9},{2,10},{3,11},{4,12},{5,13},{6,14},{7,15},{8,0},{9,1},... | collective-permute-start | bytes 393224 | tf_op jit(solution)/shard_map/ppermute | solution.py:353
  116.9 1.6 %copy-start.1 = (bf16[1024,1024]{1,0:T(8,128)(2,1)S(1)}, bf16[1024,1024]{1,0:T(8,128)(2,1)}, u32[]{:S(2)}) copy-start(bf16[1024,1024]{1,0:T(8,128)(2,1)} %get-tuple-element.36.sin_ref) | copy-start | bytes 6291460

commit v3 on v2

--- a/solution.py
+++ b/solution.py
@@ -3,7 +3,6 @@
 
 import jax
 import jax.numpy as jnp
-import numpy as np
 from jax import lax
 from jax.experimental import pallas as pl
 from jax.experimental.pallas import tpu as pltpu
@@ -14,21 +13,6 @@
 WIENER = 0.1
 LANES = 128
 GROUP = 16
-
-
-def factors_of(pixels):
-    rows = np.arange(pixels)[:, None]
-
-    def angle(columns):
-        return (rows * columns[None, :] % pixels) * (2.0 * math.pi / pixels)
-
-    high = angle(np.arange(pixels // LANES) * LANES)
-    low = angle(np.arange(LANES))
-    factor = 1.0 / math.sqrt(pixels)
-    return (
-        jnp.asarray(np.concatenate([np.cos(high), np.sin(high)], axis=1) * factor, jnp.float32),
-        jnp.asarray(np.stack([np.cos(low), np.sin(low)]), jnp.float32),
-    )
 
 
 def turn_of(angle):
@@ -43,12 +27,10 @@
 
 
 def band_kernel(
-    angles, phases, index_ref, unmix_ref, order_ref, offset_ref, raw_hbm, high_ref, low_ref, *rest
+    angles, phases, index_ref, scalar_ref, raw_hbm, *rest
 ):
-    outs = rest[:4]
-    cos_hbm, sin_hbm, left_hbm = rest[4:7]
-    parts = rest[7:11]
-    raw_ref, cos_ref, sin_ref, left_ref, spec, turned, phase, sems, row_sems = rest[11:]
+    parts = rest[:4]
+    cos_ref, sin_ref, left_ref, raw_ref, low, spec, turned_even, turned_odd, phase, sem = rest[4:]
     frames = angles * phases
     slab = raw_ref.shape[0] // frames
     pixels = raw_ref.shape[1]
@@ -61,21 +43,55 @@
     near = chip & 1
     pair = 2 * slab
 
-    fetch = pltpu.make_async_copy(raw_hbm, raw_ref, sems.at[0])
+    def offset(which, axis):
+        return scalar_ref[0, which, 0, 2 * phases + axis].astype(jnp.int32)
+
+    fetch = pltpu.make_async_copy(raw_hbm, raw_ref, sem)
     fetch.start()
+
+    column = lax.broadcasted_iota(jnp.int32, (LANES, LANES), 1)
+    unit = 2.0 * math.pi / pixels
+
+    @pl.loop(0, pixels // LANES)
+    def _(step):
+        first = pl.multiple_of(step * LANES, LANES)
+        row = first + lax.broadcasted_iota(jnp.int32, (LANES, LANES), 0)
+        around = ((row * column + pixels // 2) & (pixels - 1)) - pixels // 2
+        low[0, pl.ds(first, LANES), :], low[1, pl.ds(first, LANES), :] = turn_of(
+            around.astype(jnp.float32) * unit
+        )
+
+    repeat = lax.broadcasted_iota(jnp.int32, (GROUP, LANES), 0)
+    factor = 1.0 / math.sqrt(pixels)
+
+    def build(tab):
+        around = ((repeat * (tab * LANES) + pixels // 2) & (pixels - 1)) - pixels // 2
+        high_cos, high_sin = turn_of(around.astype(jnp.float32) * unit)
+        high_cos = high_cos * factor
+        high_sin = high_sin * factor
+        for first in range(0, pixels, GROUP):
+            rows = slice(first, first + GROUP)
+            low_cos = low[0, rows, :]
+            low_sin = low[1, rows, :]
+            cut = slice(tab * LANES, (tab + 1) * LANES)
+            cos_ref[rows, cut] = (high_cos * low_cos - high_sin * low_sin).astype(jnp.bfloat16)
+            sin_ref[rows, cut] = (high_sin * low_cos + high_cos * low_sin).astype(jnp.bfloat16)
+
+    per_tile = tile // LANES
+    for tab in range(per_tile):
+        build(tab)
+    fetch.wait()
+    for step in range(pixels // tile):
+        cut = slice(step * tile, (step + 1) * tile)
+        spec[0, :, cut] = jnp.dot(raw_ref[...], cos_ref[:, cut], preferred_element_type=jnp.float32)
+        spec[1, :, cut] = jnp.dot(raw_ref[...], sin_ref[:, cut], preferred_element_type=jnp.float32)
+        if step + 1 < pixels // tile:
+            for tab in range(per_tile):
+                build((step + 1) * per_tile + tab)
 
     @pl.loop(0, pixels // LANES)
     def _(step):
         rows = pl.ds(pl.multiple_of(step * LANES, LANES), LANES)
-        low_cos = low_ref[0, rows, :]
-        low_sin = low_ref[1, rows, :]
-        high = high_ref[rows, :]
-        for tab in range(lane_tiles):
-            cut = slice(tab * LANES, (tab + 1) * LANES)
-            high_cos = high[:, tab : tab + 1]
-            high_sin = high[:, lane_tiles + tab : lane_tiles + tab + 1]
-            cos_ref[rows, cut] = (high_cos * low_cos - high_sin * low_sin).astype(jnp.bfloat16)
-            sin_ref[rows, cut] = (high_sin * low_cos + high_cos * low_sin).astype(jnp.bfloat16)
         first = pl.multiple_of(chip * pair // LANES * LANES, LANES)
         mine = []
         for ref in (cos_ref, sin_ref):
@@ -90,25 +106,10 @@
         left_ref[step, LANES:, 0:pair] = -mine[1]
         left_ref[step, LANES:, pair:] = mine[0]
 
-    keep = [
-        pltpu.make_async_copy(cos_ref, cos_hbm, sems.at[1]),
-        pltpu.make_async_copy(sin_ref, sin_hbm, sems.at[2]),
-        pltpu.make_async_copy(left_ref, left_hbm, sems.at[3]),
-    ]
-    for copy in keep:
-        copy.start()
-    fetch.wait()
-
-    @pl.loop(0, pixels // tile)
-    def _(step):
-        cut = pl.ds(pl.multiple_of(step * tile, tile), tile)
-        spec[0, :, cut] = jnp.dot(raw_ref[...], cos_ref[:, cut], preferred_element_type=jnp.float32)
-        spec[1, :, cut] = jnp.dot(raw_ref[...], sin_ref[:, cut], preferred_element_type=jnp.float32)
-
     image_row = index * slab + lax.broadcasted_iota(jnp.int32, (slab, LANES), 0)
     for which in range(angles):
         for m in range(1, others + 1):
-            shift = MULTIPLES[m] * offset_ref[which, 0]
+            shift = MULTIPLES[m] * offset(which, 0)
             around = ((image_row * shift + pixels // 2) & (pixels - 1)) - pixels // 2
             cosine, sine = turn_of(around.astype(jnp.float32) * (2.0 * math.pi / pixels))
             phase[which * others + m - 1, 0] = cosine
@@ -118,8 +119,8 @@
     quarter_tiles = lane_tiles // 4
 
     def weight(which, m, j):
-        column = order_ref[which, j]
-        return unmix_ref[0, which, m, column], unmix_ref[1, which, m, column]
+        column = scalar_ref[0, which, 0, phases + j].astype(jnp.int32)
+        return scalar_ref[0, which, m, column], scalar_ref[1, which, m, column]
 
     def combine(terms, rows, slot):
         for tab in range(lane_tiles):
@@ -133,8 +134,8 @@
                 add_im = weight_im * cosine_sum - weight_re * sine_sum
                 real = add_re if real is None else real + add_re
                 imag = add_im if imag is None else imag + add_im
-            turned[slot, 0, tab] = real
-            turned[slot, 1, tab] = imag
+            slot[0, tab] = real
+            slot[1, tab] = imag
 
     def put_out(band, rows, slot, shift):
         move = (-shift) & (pixels - 1)
@@ -146,7 +147,7 @@
             first = (2 * side + half) * quarter_tiles + move // LANES
             for part in range(2):
                 tiles = [
-                    pltpu.roll(turned[slot, part, (first + i) & (lane_tiles - 1)], turn, 1)
+                    pltpu.roll(slot[part, (first + i) & (lane_tiles - 1)], turn, 1)
                     for i in range(quarter_tiles + 1)
                 ]
                 put = pl.ds(pl.multiple_of(part * slab + rows, GROUP), GROUP)
@@ -155,19 +156,30 @@
                         lane < LANES - rest_lanes, tiles[i], tiles[i + 1]
                     ).astype(jnp.bfloat16)
 
-    def copies(step):
-        done = []
-        for which in range(4):
-            for part in range(2):
-                put = pl.ds(pl.multiple_of(part * slab + step * GROUP, GROUP), GROUP)
-                done.append(
-                    pltpu.make_async_copy(
-                        parts[which].at[:, put, :],
-                        outs[which].at[:, put, :],
-                        row_sems.at[step, 2 * which + part],
-                    )
+    def terms_of(band, rows):
+        which = band // others
+        m = band - which * others + 1
+        here = pl.ds(pl.multiple_of(rows, GROUP), GROUP)
+        phase_re = phase[band, 0, here, :]
+        phase_im = phase[band, 1, here, :]
+        terms = []
+        for j in range(phases):
+            weight_re, weight_im = weight(which, m, j)
+            terms.append(
+                (
+                    which * phases + j,
+                    weight_re * phase_re - weight_im * phase_im,
+                    weight_re * phase_im + weight_im * phase_re,
                 )
-        return done
+            )
+        return terms
+
+    def shift_of(band):
+        other = jnp.maximum(band - 1, 0)
+        which = other // others
+        m = other - which * others + 1
+        mult = jnp.where(m <= 2, 1, 2) * jnp.where(m % 2 == 1, 1, -1)
+        return jnp.where(band == 0, 0, mult * offset(which, 1))
 
     @pl.loop(0, slab // GROUP)
     def _(step):
@@ -177,44 +189,21 @@
             for which in range(angles)
             for j in range(phases)
         ]
-        combine(terms, rows, 0)
-        put_out(0, rows, 0, 0)
-
-        @pl.loop(0, angles * others)
-        def _(band):
-            which = band // others
-            m = band - which * others + 1
-            mult = jnp.where(m <= 2, 1, 2) * jnp.where(m & 1, 1, -1)
-            here = pl.ds(pl.multiple_of(rows, GROUP), GROUP)
-            phase_re = phase[band, 0, here, :]
-            phase_im = phase[band, 1, here, :]
-            terms = []
-            for j in range(phases):
-                weight_re, weight_im = weight(which, m, j)
-                terms.append(
-                    (
-                        which * phases + j,
-                        weight_re * phase_re - weight_im * phase_im,
-                        weight_re * phase_im + weight_im * phase_re,
-                    )
-                )
-            combine(terms, rows, 1)
-            put_out(band + 1, rows, 1, mult * offset_ref[which, 1])
-
-        for copy in copies(step):
-            copy.start()
-
-    for copy in keep:
-        copy.wait()
-
-    @pl.loop(0, slab // GROUP)
-    def _(step):
-        for copy in copies(step):
-            copy.wait()
+        combine(terms, rows, turned_even)
+
+        @pl.loop(0, angles * others // 2)
+        def _(pair_index):
+            band = 2 * pair_index
+            combine(terms_of(band, rows), rows, turned_odd)
+            put_out(band, rows, turned_even, shift_of(band))
+            combine(terms_of(band + 1, rows), rows, turned_even)
+            put_out(band + 1, rows, turned_odd, shift_of(band + 1))
+
+        put_out(angles * others, rows, turned_even, shift_of(angles * others))
 
 
 def numer_kernel(
-    slab, bands, columns, masks, with_power, index_ref, offset_ref, own_ref, other_ref, left_ref,
+    slab, bands, columns, masks, with_power, index_ref, scalar_ref, own_ref, other_ref, left_ref,
     near_ref, far_ref, *rest
 ):
     outs = rest[:4]
@@ -240,7 +229,9 @@
         if band == 0:
             return 0
         which, m = divmod(band - 1, others)
-        return MULTIPLES[m + 1] * offset_ref[which, axis]
+        return MULTIPLES[m + 1] * scalar_ref[0, which, 0, scalar_ref.shape[3] - 2 + axis].astype(
+            jnp.int32
+        )
 
     @pl.loop(0, bands)
     def _(band):
@@ -321,6 +312,12 @@
         pl.loop(0, pixels // tile // 2)(functools.partial(tile_of, upper=upper))
 
 
+def pack_kernel(*refs):
+    out_ref = refs[-1]
+    for index, ref in enumerate(refs[:-1]):
+        out_ref[index] = ref[...]
+
+
 def image_kernel(back_ref, cos_ref, sin_ref, out_ref):
     devices, _, twice = back_ref.shape
     columns = twice // 2
@@ -374,7 +371,15 @@
 
     quarter = pixels // 4
     where = index.astype(jnp.int32).reshape(1)
-    high, low = factors_of(pixels)
+    share = unmix.shape[:3]
+    scalars = jnp.concatenate(
+        [
+            unmix,
+            jnp.broadcast_to(phase_order.astype(jnp.float32)[None, :, None, :], share + (phases,)),
+            jnp.broadcast_to(offsets.astype(jnp.float32)[None, :, None, :], share + (2,)),
+        ],
+        axis=3,
+    )
     table = jax.ShapeDtypeStruct((pixels, pixels), jnp.bfloat16)
     hbm = pl.BlockSpec(memory_space=pl.ANY)
     part = (bands, 2 * slab, quarter)
@@ -384,30 +389,38 @@
         out_shape=[jax.ShapeDtypeStruct(part, jnp.bfloat16)] * 4
         + [table] * 2
         + [jax.ShapeDtypeStruct(left_shape, jnp.bfloat16)],
-        in_specs=[smem()] * 4 + [hbm] + [vmem()] * 2,
-        out_specs=[hbm] * 7,
-        scratch_shapes=[pltpu.VMEM(part, jnp.bfloat16)] * 4
-        + [
+        in_specs=[smem()] * 2 + [hbm],
+        out_specs=[vmem()] * 7,
+        scratch_shapes=[
             pltpu.VMEM((frames * slab, pixels), jnp.bfloat16),
-            pltpu.VMEM((pixels, pixels), jnp.bfloat16),
-            pltpu.VMEM((pixels, pixels), jnp.bfloat16),
-            pltpu.VMEM(left_shape, jnp.bfloat16),
+            pltpu.VMEM((2, pixels, LANES), jnp.float32),
             pltpu.VMEM((2, frames * slab, pixels), jnp.float32),
-            pltpu.VMEM((2, 2, pixels // LANES, GROUP, LANES), jnp.float32),
+            pltpu.VMEM((2, pixels // LANES, GROUP, LANES), jnp.float32),
+            pltpu.VMEM((2, pixels // LANES, GROUP, LANES), jnp.float32),
             pltpu.VMEM((bands - 1, 2, slab, LANES), jnp.float32),
-            pltpu.SemaphoreType.DMA((4,)),
-            pltpu.SemaphoreType.DMA((slab // GROUP, 8)),
+            pltpu.SemaphoreType.DMA,
         ],
         cost_estimate=pl.CostEstimate(
             flops=8 * frames * slab * pixels * pixels,
             bytes_accessed=12 << 20,
             transcendentals=0,
         ),
+        compiler_params=pltpu.CompilerParams(vmem_limit_bytes=26 << 20),
         name="bands",
-    )(where, unmix, phase_order, offsets, raw.reshape(frames * slab, pixels), high, low)
+    )(where, scalars, raw.reshape(frames * slab, pixels))
 
     got_away = swap(send_away, "row", 1)
-    own_pieces = jnp.stack(pieces)
+    own_pieces = pl.pallas_call(
+        pack_kernel,
+        out_shape=jax.ShapeDtypeStruct((chips, slab, pixels), jnp.bfloat16),
+        in_specs=[vmem()] * chips,
+        out_specs=vmem(),
+        compiler_params=pltpu.CompilerParams(vmem_limit_bytes=8 << 20),
+        cost_estimate=pl.CostEstimate(
+            flops=chips * slab * pixels, bytes_accessed=2 << 20, transcendentals=0
+        ),
+        name="pack",
+    )(*pieces)
     other_pieces = swap(own_pieces, "row", 1)
     got_near = swap(send_near, "row", 1)
 
@@ -431,7 +444,8 @@
                 bytes_accessed=8 << 20,
                 transcendentals=0,
             ),
-        )(where, offsets, own, other, left, own_pieces, other_pieces)
+            compiler_params=pltpu.CompilerParams(vmem_limit_bytes=16 << 20),
+        )(where, scalars, own, other, left, own_pieces, other_pieces)
 
     away = partial(keep_away, got_away, False)
     moved = [swap(value, "row", 2) for value in away]
@@ -486,6 +500,7 @@
         cost_estimate=pl.CostEstimate(
             flops=4 * slab * pixels * pixels, bytes_accessed=6 << 20, transcendentals=0
         ),
+        compiler_params=pltpu.CompilerParams(vmem_limit_bytes=12 << 20),
         name="image",
     )(back, cosine, sine)
     return recon.reshape(otf.shape)

time: 138 us -> 127 us (0.920)
  Pallas kernels: 55.4 us -> 45.4 us
  local copies, waits for them, and re-layouts: 6.6 us -> 4.11 us
    pallas_call x1, Pallas kernels: 23.2 us -> 18.5 us  [shards(): pl.pallas_call(functools.partial(band_kernel, angles, phases), out_shape=...]
    pallas_call x2, Pallas kernels: 28.4 us -> 25.2 us  [partial(): pl.pallas_call(functools.partial(numer_kernel, slab, bands, columns, mask...]
    unnamed x26 -> x11, local copies, waits for them, and re-layouts: 6.2 us -> 3.62 us
    pallas_call x1, Pallas kernels: 3.85 us -> 1.55 us  [shards(): pl.pallas_call(image_kernel, out_shape=jax.ShapeDtypeStruct((slab, pixels...]
    convert_element_type x0 -> x2, other arithmetic: none -> 1.51 us  [the longest x1 0.83 us: shards(): phase_order.astype(jnp.float32)[None, :, None, :]]
  transfers between devices with their start and end apart: 19 -> 19, of which waited for: 6 -> 7; matrix products, arithmetic and copies ran while one was open for 5% -> 4% of each run, Pallas kernels for 37% -> 35%
where the time goes in v3:
time: 127 us
  Pallas kernels  45.4 us (36%)
  starting transfers between devices  32.4 us (26%)
  waiting for transfers between devices  23.4 us (18%)
  blocking collectives  13.7 us (11%)
  other arithmetic  5.96 us (5%)
  local copies, waits for them, and re-layouts  4.11 us (3%)
  matrix products  1.65 us (1%)
    ppermute x18, starting transfers between devices, swap(): return lax.ppermute(value, axis, [(i, i ^ mask) for i in range(size)])  30.9 us
    pallas_call x2, Pallas kernels, partial(): pl.pallas_call(functools.partial(numer_kernel, slab, bands, columns, mask...  25.2 us
    ppermute x18, waiting for transfers between devices, swap(): return lax.ppermute(value, axis, [(i, i ^ mask) for i in range(size)])  23.4 us
    pallas_call x1, Pallas kernels, shards(): pl.pallas_call(functools.partial(band_kernel, angles, phases), out_shape=...  18.5 us
    all_to_all x1, blocking collectives, shards(): lax.all_to_all(half.reshape(devices, slab, 2 * columns), 'row', split_axi...  13.7 us
    unnamed x11, local copies, waits for them, and re-layouts  3.62 us
  transfers between devices with their start and end apart: 19, of which 7 were waited for; matrix products, arithmetic and copies ran while one was open for 4% of the time, Pallas kernels for 35%

profile of v3, /device:TPU:0, one launch (start us, length us, event | category | flops | bytes accessed | tf_op | source)
XLA Modules:
  0.0 126.8 jit_solution(5952417587640847217)
XLA Ops:
  0.0 1.0 convert_bitcast_fusion.refs_0_
  1.0 3.1 %collective-permute-start.1 = (bf16[64,1024]{1,0:T(8,128)(2,1)S(1)}, bf16[64,1024]{1,0:T(8,128)(2,1)S(1)}, u32[]{:S(2)}, u32[]{:S(2)}) collective-permute-start(bf16[64,1024]{1,0:T(8,128)(2,1)S(1)} %convert_bitcast_fusion.refs_0_), channel_id=1, source_target_pairs={{0,2},{1,3},{2,0},{3,1},{4,6},{5,7},{6,4},{7,5},{8,10},{9,11},{10,... | collective-permute-start | bytes 393224 | tf_op jit(solution)/shard_map/ppermute | solution.py:350
  4.0 1.6 %collective-permute-start.2 = (bf16[64,1024]{1,0:T(8,128)(2,1)S(1)}, bf16[64,1024]{1,0:T(8,128)(2,1)S(1)}, u32[]{:S(2)}, u32[]{:S(2)}) collective-permute-start(bf16[64,1024]{1,0:T(8,128)(2,1)S(1)} %convert_bitcast_fusion.refs_0_), channel_id=1, source_target_pairs={{0,4},{1,5},{2,6},{3,7},{4,0},{5,1},{6,2},{7,3},{8,12},{9,13},{10,... | collective-permute-start | bytes 393224 | tf_op jit(solution)/shard_map/ppermute | solution.py:350
  5.6 0.0 collective-permute-start.3
  5.6 3.0 %collective-permute-start.4 = (bf16[64,1024]{1,0:T(8,128)(2,1)S(1)}, bf16[64,1024]{1,0:T(8,128)(2,1)S(1)}, u32[]{:S(2)}, u32[]{:S(2)}) collective-permute-start(bf16[64,1024]{1,0:T(8,128)(2,1)S(1)} %convert_bitcast_fusion.refs_0_), channel_id=1, source_target_pairs={{0,8},{1,9},{2,10},{3,11},{4,12},{5,13},{6,14},{7,15},{8,0},{9,1},... | collective-permute-start | bytes 393224 | tf_op jit(solution)/shard_map/ppermute | solution.py:350
  8.6 1.3 %collective-permute-start.5 = (bf16[64,1024]{1,0:T(8,128)(2,1)S(1)}, bf16[64,1024]{1,0:T(8,128)(2,1)S(1)}, u32[]{:S(2)}, u32[]{:S(2)}) collective-permute-start(bf16[64,1024]{1,0:T(8,128)(2,1)S(1)} %convert_bitcast_fusion.refs_0_), channel_id=1, source_target_pairs={{0,10},{1,11},{2,8},{3,9},{4,14},{5,15},{6,12},{7,13},{8,2},{9,3},... | collective-permute-start | bytes 393224 | tf_op jit(solution)/shard_map/ppermute | solution.py:350
  9.9 0.0 collective-permute-done.1.refs_1_
  9.9 3.6 %collective-permute-start.6 = (bf16[64,1024]{1,0:T(8,128)(2,1)S(1)}, bf16[64,1024]{1,0:T(8,128)(2,1)S(1)}, u32[]{:S(2)}, u32[]{:S(2)}) collective-permute-start(bf16[64,1024]{1,0:T(8,128)(2,1)S(1)} %convert_bitcast_fusion.refs_0_), channel_id=1, source_target_pairs={{0,12},{1,13},{2,14},{3,15},{4,8},{5,9},{6,10},{7,11},{8,4},{9,5},... | collective-permute-start | bytes 393224 | tf_op jit(solution)/shard_map/ppermute | solution.py:350
  13.5 1.3 %collective-permute-done.2.refs_2_ = bf16[64,1024]{1,0:T(8,128)(2,1)S(1)} collective-permute-done((bf16[64,1024]{1,0:T(8,128)(2,1)S(1)}, bf16[64,1024]{1,0:T(8,128)(2,1)S(1)}, u32[]{:S(2)}, u32[]{:S(2)}) %collective-permute-start.2) | collective-permute-done | bytes 131104 | tf_op jit(solution)/shard_map/ppermute | solution.py:350
  14.8 0.7 collective-permute-start.7
  15.5 0.7 convert_element_type.65
  16.2 0.1 copy.6
  16.3 0.8 convert_element_type.64
  17.1 0.7 copy.7
  17.8 0.1 pad_maximum_fusion.1.scalar_ref
  17.9 0.0 collective-permute-done.3.refs_3_
  17.9 0.0 collective-permute-done.4.refs_4_
  17.9 10.1 %collective-permute-done.5.refs_5_ = bf16[64,1024]{1,0:T(8,128)(2,1)S(1)} collective-permute-done((bf16[64,1024]{1,0:T(8,128)(2,1)S(1)}, bf16[64,1024]{1,0:T(8,128)(2,1)S(1)}, u32[]{:S(2)}, u32[]{:S(2)}) %collective-permute-start.5) | collective-permute-done | bytes 131104 | tf_op jit(solution)/shard_map/ppermute | solution.py:350
  28.0 0.0 collective-permute-done.6.refs_6_
  28.0 0.0 collective-permute-done.7.refs_7_
  28.0 0.1 pack.1.near_ref
  28.1 0.1 collective-permute-start.8
  28.2 18.5 %bands.1 = (bf16[13,128,256]{2,1,0:T(8,128)(2,1)S(1)}, bf16[13,128,256]{2,1,0:T(8,128)(2,1)S(1)}, bf16[13,128,256]{2,1,0:T(8,128)(2,1)S(1)}, bf16[13,128,256]{2,...) custom-call(s32[1]{0:T(128)} %bitcast.index_ref, ...), custom_call_target="tpu_custom_call" | custom-call | flops 8053063680 | bytes 12582912 | tf_op jit(solution)/shard_map/bands/pallas_call | solution.py:387
  46.8 0.5 collective-permute-start
  47.3 0.1 collective-permute-start.10
  47.4 1.9 %collective-permute-done.other_ref = bf16[13,128,256]{2,1,0:T(8,128)(2,1)S(1)} collective-permute-done((bf16[13,128,256]{2,1,0:T(8,128)(2,1)S(1)}, bf16[13,128,256]{2,1,0:T(8,128)(2,1)S(1)}, u32[]{:S(2)}, u32[]{:S(2)}) %collective-permute-start) | collective-permute-done | bytes 852000 | tf_op jit(solution)/shard_map/ppermute | solution.py:350
  49.3 0.0 collective-permute-done.8.far_ref
  49.3 10.8 %shard_map.55 = (bf16[2,512,128]{2,1,0:T(8,128)(2,1)S(1)}, bf16[2,512,128]{2,1,0:T(8,128)(2,1)}, bf16[2,512,128]{2,1,0:T(8,128)(2,1)}, bf16[2,512,128]{2,1,0:T(8,128)(2,1)S(1)}) custom-call(s32[1]{0:T(128)} %bitcast.index_ref, f32[2,3,5,12]{3,2,1,0:T(8,128)S(1)} %pad_maximum_fusion.1.scalar_ref, bf16[13,128,256]{2,1,0:T(8,128)(2,1)S(1)} %get-tuple-element.22.own_ref, ...), custom_call_target="tpu_custom_call" | custom-call | flops 3489660928 | bytes 8388608 | tf_op jit(solution)/shard_map/pallas_call | solution.py:432
  60.1 0.7 copy-done.4
  60.8 0.7 collective-permute-start.11
  61.5 1.3 %collective-permute-start.9 = (bf16[2,512,128]{2,1,0:T(8,128)(2,1)}, bf16[2,512,128]{2,1,0:T(8,128)(2,1)}, u32[]{:S(2)}, u32[]{:S(2)}) collective-permute-start(bf16[2,512,128]{2,1,0:T(8,128)(2,1)} %get-tuple-element.25), channel_id=1, source_target_pairs={{0,2},{1,3},{2,0},{3,1},{4,6},{5,7},{6,4},{7,5},{8,10},{9,11},{10,... | collective-permute-start | bytes 786440 | tf_op jit(solution)/shard_map/ppermute | solution.py:350
  62.8 0.7 collective-permute-start.15
  63.5 0.0 collective-permute-done.10.other_ref
  63.5 14.5 %shard_map.56 = (bf16[2,512,128]{2,1,0:T(8,128)(2,1)S(1)}, bf16[2,512,128]{2,1,0:T(8,128)(2,1)S(1)}, bf16[2,512,128]{2,1,0:T(8,128)(2,1)S(1)}, bf16[2,512,128]{2,1,0:T(8,128)(2,1)S(1)}, f32[1024,128]{1,0:T(8,128)S(1)}) custom-call(s32[1]{0:T(128)} %bitcast.index_ref, f32[2,3,5,12]{3,2,1,0:T(8,128)S(1)} %pad_maximum_fusion.1.scalar_ref, ...), custom_call_target="tpu_custom_call" | custom-call | flops 3489660928 | bytes 8388608 | tf_op jit(solution)/shard_map/pallas_call | solution.py:432
  78.0 0.0 collective-permute-done.11
  78.0 0.8 add_convert_fusion.1
  78.8 4.7 %collective-permute-start.12 = (bf16[2,512,128]{2,1,0:T(8,128)(2,1)}, bf16[2,512,128]{2,1,0:T(8,128)(2,1)}, u32[]{:S(2)}, u32[]{:S(2)}) collective-permute-start(bf16[2,512,128]{2,1,0:T(8,128)(2,1)} %add_convert_fusion.1), channel_id=1, source_target_pairs={{0,4},{1,5},{2,6},{3,7},{4,0},{5,1},{6,2},{7,3},{8,12},{9,13},{10,... | collective-permute-start | bytes 786440 | tf_op jit(solution)/shard_map/ppermute | solution.py:350
  83.5 1.7 %collective-permute-start.14 = (bf16[2,512,128]{2,1,0:T(8,128)(2,1)}, bf16[2,512,128]{2,1,0:T(8,128)(2,1)S(1)}, u32[]{:S(2)}, u32[]{:S(2)}) collective-permute-start(bf16[2,512,128]{2,1,0:T(8,128)(2,1)} %copy-done.4), channel_id=1, source_target_pairs={{0,2},{1,3},{2,0},{3,1},{4,6},{5,7},{6,4},{7,5},{8,10},{9,11},{10,... | collective-permute-start | bytes 786440 | tf_op jit(solution)/shard_map/ppermute | solution.py:350
  85.1 1.5 %collective-permute-start.18 = (f32[1024,128]{1,0:T(8,128)S(1)}, f32[1024,128]{1,0:T(8,128)S(1)}, u32[]{:S(2)}, u32[]{:S(2)}) collective-permute-start(f32[1024,128]{1,0:T(8,128)S(1)} %get-tuple-element.35), channel_id=1, source_target_pairs={{0,16},{16,0},{1,17},{17,1},{2,18},{18,2},{3,19},{19,3},{4,20},{20... | collective-permute-start | bytes 1572872 | tf_op jit(solution)/shard_map/ppermute | solution.py:478
  86.6 0.0 collective-permute-done.15
  86.6 1.0 add_convert_fusion
  87.7 0.1 collective-permute-start.16
  87.7 0.0 collective-permute-done.9
  87.7 2.7 %collective-permute-done.12 = bf16[2,512,128]{2,1,0:T(8,128)(2,1)} collective-permute-done((bf16[2,512,128]{2,1,0:T(8,128)(2,1)}, bf16[2,512,128]{2,1,0:T(8,128)(2,1)}, u32[]{:S(2)}, u32[]{:S(2)}) %collective-permute-start.12) | collective-permute-done | bytes 262176 | tf_op jit(solution)/shard_map/ppermute | solution.py:350
  90.5 1.1 convert_add_fusion.1
  91.6 4.3 %collective-permute-start.13 = (bf16[1,512,128]{2,1,0:T(8,128)(2,1)S(1)}, bf16[1,512,128]{2,1,0:T(8,128)(2,1)S(1)}, u32[]{:S(2)}, u32[]{:S(2)}) collective-permute-start(bf16[1,512,128]{2,1,0:T(8,128)(2,1)S(1)} %dynamic-slice_convert_fusion.1), channel_id=1, source_target_pairs={{0,8},{1,9},{2,10},{3,11},{4,12},{5,13},{6,14},{7,15},{8,0},{9,1},... | collective-permute-start | bytes 393224 | tf_op jit(solution)/shard_map/ppermute | solution.py:350
  95.9 0.0 collective-permute-done.14
  95.9 0.8 collective-permute-done.16
  96.7 0.1 convert_add_fusion
  96.8 3.6 %collective-permute-start.17 = (bf16[1,512,128]{2,1,0:T(8,128)(2,1)S(1)}, bf16[1,512,128]{2,1,0:T(8,128)(2,1)S(1)}, u32[]{:S(2)}, u32[]{:S(2)}) collective-permute-start(bf16[1,512,128]{2,1,0:T(8,128)(2,1)S(1)} %dynamic-slice_convert_fusion), channel_id=1, source_target_pairs={{0,8},{1,9},{2,10},{3,11},{4,12},{5,13},{6,14},{7,15},{8,0},{9,1},... | collective-permute-start | bytes 393224 | tf_op jit(solution)/shard_map/ppermute | solution.py:350
  100.4 4.6 %collective-permute-done.13 = bf16[1,512,128]{2,1,0:T(8,128)(2,1)S(1)} collective-permute-done((bf16[1,512,128]{2,1,0:T(8,128)(2,1)S(1)}, bf16[1,512,128]{2,1,0:T(8,128)(2,1)S(1)}, u32[]{:S(2)}, u32[]{:S(2)}) %collective-permute-start.13) | collective-permute-done | bytes 131104 | tf_op jit(solution)/shard_map/ppermute | solution.py:350
  105.1 1.9 %collective-permute-done.17 = bf16[1,512,128]{2,1,0:T(8,128)(2,1)S(1)} collective-permute-done((bf16[1,512,128]{2,1,0:T(8,128)(2,1)S(1)}, bf16[1,512,128]{2,1,0:T(8,128)(2,1)S(1)}, u32[]{:S(2)}, u32[]{:S(2)}) %collective-permute-start.17) | collective-permute-done | bytes 131104 | tf_op jit(solution)/shard_map/ppermute | solution.py:350
  107.0 0.0 collective-permute-done.18
  107.0 0.1 fusion
  107.1 0.8 fusion.3
  108.0 0.6 copy-done.1
  108.6 0.8 fusion.4
  109.4 0.1 fusion.2
  109.5 0.2 copy.8
  109.6 0.2 copy.9
  109.8 0.2 pad_maximum_fusion
  110.0 13.7 %all_to_all.5.back_ref = bf16[16,64,128]{2,1,0:T(8,128)(2,1)S(1)} all-to-all(bf16[16,64,128]{2,1,0:T(8,128)(2,1)S(1)} %pad_maximum_fusion), channel_id=1, replica_groups=mesh['cuts'=2,'row'=16] {'row'}, dimensions={0} | all-to-all | bytes 524288 | tf_op jit(solution)/shard_map/all_to_all | solution.py:492
  123.7 1.6 %copy-done.2 = bf16[1024,1024]{1,0:T(8,128)(2,1)S(1)} copy-done((bf16[1024,1024]{1,0:T(8,128)(2,1)S(1)}, bf16[1024,1024]{1,0:T(8,128)(2,1)}, u32[]{:S(2)}) %copy-start.2) | copy-done | bytes 2097176
  125.3 1.5 %image.1 = f32[64,1024]{1,0:T(8,128)} custom-call(bf16[16,64,128]{2,1,0:T(8,128)(2,1)S(1)} %all_to_all.5.back_ref, bf16[1024,1024]{1,0:T(8,128)(2,1)S(1)} %get-tuple-element.21.cos_ref, bf16[1024,1024]{1,0:T(8,128)(2,1)S(1)} %copy-done.2), custom_call_target="tpu_custom_call" | custom-call | flops 268435456 | bytes 6291456 | tf_op jit(solution)/shard_map/image/pallas_call | solution.py:495
  (13 shorter events, 0.1 us)
Async XLA Ops:
  1.0 8.9 %collective-permute-start.1 = (bf16[64,1024]{1,0:T(8,128)(2,1)S(1)}, bf16[64,1024]{1,0:T(8,128)(2,1)S(1)}, u32[]{:S(2)}, u32[]{:S(2)}) collective-permute-start(bf16[64,1024]{1,0:T(8,128)(2,1)S(1)} %convert_bitcast_fusion.refs_0_), channel_id=1, source_target_pairs={{0,2},{1,3},{2,0},{3,1},{4,6},{5,7},{6,4},{7,5},{8,10},{9,11},{10,... | collective-permute-start | bytes 393224 | tf_op jit(solution)/shard_map/ppermute | solution.py:350
  4.0 10.8 %collective-permute-start.2 = (bf16[64,1024]{1,0:T(8,128)(2,1)S(1)}, bf16[64,1024]{1,0:T(8,128)(2,1)S(1)}, u32[]{:S(2)}, u32[]{:S(2)}) collective-permute-start(bf16[64,1024]{1,0:T(8,128)(2,1)S(1)} %convert_bitcast_fusion.refs_0_), channel_id=1, source_target_pairs={{0,4},{1,5},{2,6},{3,7},{4,0},{5,1},{6,2},{7,3},{8,12},{9,13},{10,... | collective-permute-start | bytes 393224 | tf_op jit(solution)/shard_map/ppermute | solution.py:350
  5.6 12.3 %collective-permute-start.3 = (bf16[64,1024]{1,0:T(8,128)(2,1)S(1)}, bf16[64,1024]{1,0:T(8,128)(2,1)S(1)}, u32[]{:S(2)}, u32[]{:S(2)}) collective-permute-start(bf16[64,1024]{1,0:T(8,128)(2,1)S(1)} %convert_bitcast_fusion.refs_0_), channel_id=1, source_target_pairs={{0,6},{1,7},{2,4},{3,5},{4,2},{5,3},{6,0},{7,1},{8,14},{9,15},{10,... | collective-permute-start | bytes 393224 | tf_op jit(solution)/shard_map/ppermute | solution.py:350
  5.6 12.3 %collective-permute-start.4 = (bf16[64,1024]{1,0:T(8,128)(2,1)S(1)}, bf16[64,1024]{1,0:T(8,128)(2,1)S(1)}, u32[]{:S(2)}, u32[]{:S(2)}) collective-permute-start(bf16[64,1024]{1,0:T(8,128)(2,1)S(1)} %convert_bitcast_fusion.refs_0_), channel_id=1, source_target_pairs={{0,8},{1,9},{2,10},{3,11},{4,12},{5,13},{6,14},{7,15},{8,0},{9,1},... | collective-permute-start | bytes 393224 | tf_op jit(solution)/shard_map/ppermute | solution.py:350
  8.6 19.4 %collective-permute-start.5 = (bf16[64,1024]{1,0:T(8,128)(2,1)S(1)}, bf16[64,1024]{1,0:T(8,128)(2,1)S(1)}, u32[]{:S(2)}, u32[]{:S(2)}) collective-permute-start(bf16[64,1024]{1,0:T(8,128)(2,1)S(1)} %convert_bitcast_fusion.refs_0_), channel_id=1, source_target_pairs={{0,10},{1,11},{2,8},{3,9},{4,14},{5,15},{6,12},{7,13},{8,2},{9,3},... | collective-permute-start | bytes 393224 | tf_op jit(solution)/shard_map/ppermute | solution.py:350
  9.9 18.2 %collective-permute-start.6 = (bf16[64,1024]{1,0:T(8,128)(2,1)S(1)}, bf16[64,1024]{1,0:T(8,128)(2,1)S(1)}, u32[]{:S(2)}, u32[]{:S(2)}) collective-permute-start(bf16[64,1024]{1,0:T(8,128)(2,1)S(1)} %convert_bitcast_fusion.refs_0_), channel_id=1, source_target_pairs={{0,12},{1,13},{2,14},{3,15},{4,8},{5,9},{6,10},{7,11},{8,4},{9,5},... | collective-permute-start | bytes 393224 | tf_op jit(solution)/shard_map/ppermute | solution.py:350
  14.8 13.2 %collective-permute-start.7 = (bf16[64,1024]{1,0:T(8,128)(2,1)S(1)}, bf16[64,1024]{1,0:T(8,128)(2,1)S(1)}, u32[]{:S(2)}, u32[]{:S(2)}) collective-permute-start(bf16[64,1024]{1,0:T(8,128)(2,1)S(1)} %convert_bitcast_fusion.refs_0_), channel_id=1, source_target_pairs={{0,14},{1,15},{2,12},{3,13},{4,10},{5,11},{6,8},{7,9},{8,6},{9,7},... | collective-permute-start | bytes 393224 | tf_op jit(solution)/shard_map/ppermute | solution.py:350
  16.3 11.9 %copy-start.3 = (bf16[1,3,5,64,1024]{4,3,2,1,0:T(8,128)(2,1)S(1)}, bf16[1,3,5,64,1024]{4,3,2,1,0:T(8,128)(2,1)}, u32[]{:S(2)}) copy-start(bf16[1,3,5,64,1024]{4,3,2,1,0:T(8,128)(2,1)} %param.5) | copy-start | bytes 5898244
  28.1 21.2 %collective-permute-start.8 = (bf16[8,64,1024]{2,1,0:T(8,128)(2,1)S(1)}, bf16[8,64,1024]{2,1,0:T(8,128)(2,1)S(1)}, u32[]{:S(2)}, u32[]{:S(2)}) collective-permute-start(bf16[8,64,1024]{2,1,0:T(8,128)(2,1)S(1)} %pack.1.near_ref), channel_id=1, source_target_pairs={{0,1},{1,0},{2,3},{3,2},{4,5},{5,4},{6,7},{7,6},{8,9},{9,8},{10,11... | collective-permute-start | bytes 3145736 | tf_op jit(solution)/shard_map/ppermute | solution.py:350
  46.7 13.3 %copy-start = (bf16[1024,1024]{1,0:T(8,128)(2,1)}, bf16[1024,1024]{1,0:T(8,128)(2,1)S(1)}, u32[]{:S(2)}) copy-start(bf16[1024,1024]{1,0:T(8,128)(2,1)S(1)} %get-tuple-element.36.sin_ref) | copy-start | bytes 6291460
  46.8 2.5 %collective-permute-start = (bf16[13,128,256]{2,1,0:T(8,128)(2,1)S(1)}, bf16[13,128,256]{2,1,0:T(8,128)(2,1)S(1)}, u32[]{:S(2)}, u32[]{:S(2)}) collective-permute-start(bf16[13,128,256]{2,1,0:T(8,128)(2,1)S(1)} %get-tuple-element.23), channel_id=1, source_target_pairs={{0,1},{1,0},{2,3},{3,2},{4,5},{5,4},{6,7},{7,6},{8,9},{9,8},{10,11... | collective-permute-start | bytes 2555912 | tf_op jit(solution)/shard_map/ppermute | solution.py:350
  47.3 16.2 %collective-permute-start.10 = (bf16[13,128,256]{2,1,0:T(8,128)(2,1)S(1)}, bf16[13,128,256]{2,1,0:T(8,128)(2,1)S(1)}, u32[]{:S(2)}, u32[]{:S(2)}) collective-permute-start(bf16[13,128,256]{2,1,0:T(8,128)(2,1)S(1)} %get-tuple-element.27), channel_id=1, source_target_pairs={{0,1},{1,0},{2,3},{3,2},{4,5},{5,4},{6,7},{7,6},{8,9},{9,8},{10,11... | collective-permute-start | bytes 2555912 | tf_op jit(solution)/shard_map/ppermute | solution.py:350
  60.1 0.7 copy-start.4
  60.8 17.2 %collective-permute-start.11 = (bf16[2,512,128]{2,1,0:T(8,128)(2,1)S(1)}, bf16[2,512,128]{2,1,0:T(8,128)(2,1)S(1)}, u32[]{:S(2)}, u32[]{:S(2)}) collective-permute-start(bf16[2,512,128]{2,1,0:T(8,128)(2,1)S(1)} %get-tuple-element.29), channel_id=1, source_target_pairs={{0,2},{1,3},{2,0},{3,1},{4,6},{5,7},{6,4},{7,5},{8,10},{9,11},{10,... | collective-permute-start | bytes 786440 | tf_op jit(solution)/shard_map/ppermute | solution.py:350
  61.5 26.3 %collective-permute-start.9 = (bf16[2,512,128]{2,1,0:T(8,128)(2,1)}, bf16[2,512,128]{2,1,0:T(8,128)(2,1)}, u32[]{:S(2)}, u32[]{:S(2)}) collective-permute-start(bf16[2,512,128]{2,1,0:T(8,128)(2,1)} %get-tuple-element.25), channel_id=1, source_target_pairs={{0,2},{1,3},{2,0},{3,1},{4,6},{5,7},{6,4},{7,5},{8,10},{9,11},{10,... | collective-permute-start | bytes 786440 | tf_op jit(solution)/shard_map/ppermute | solution.py:350
  62.8 23.8 %collective-permute-start.15 = (bf16[2,512,128]{2,1,0:T(8,128)(2,1)}, bf16[2,512,128]{2,1,0:T(8,128)(2,1)}, u32[]{:S(2)}, u32[]{:S(2)}) collective-permute-start(bf16[2,512,128]{2,1,0:T(8,128)(2,1)} %get-tuple-element.33), channel_id=1, source_target_pairs={{0,2},{1,3},{2,0},{3,1},{4,6},{5,7},{6,4},{7,5},{8,10},{9,11},{10,... | collective-permute-start | bytes 786440 | tf_op jit(solution)/shard_map/ppermute | solution.py:350
  78.8 11.7 %collective-permute-start.12 = (bf16[2,512,128]{2,1,0:T(8,128)(2,1)}, bf16[2,512,128]{2,1,0:T(8,128)(2,1)}, u32[]{:S(2)}, u32[]{:S(2)}) collective-permute-start(bf16[2,512,128]{2,1,0:T(8,128)(2,1)} %add_convert_fusion.1), channel_id=1, source_target_pairs={{0,4},{1,5},{2,6},{3,7},{4,0},{5,1},{6,2},{7,3},{8,12},{9,13},{10,... | collective-permute-start | bytes 786440 | tf_op jit(solution)/shard_map/ppermute | solution.py:350
  83.5 12.5 %collective-permute-start.14 = (bf16[2,512,128]{2,1,0:T(8,128)(2,1)}, bf16[2,512,128]{2,1,0:T(8,128)(2,1)S(1)}, u32[]{:S(2)}, u32[]{:S(2)}) collective-permute-start(bf16[2,512,128]{2,1,0:T(8,128)(2,1)} %copy-done.4), channel_id=1, source_target_pairs={{0,2},{1,3},{2,0},{3,1},{4,6},{5,7},{6,4},{7,5},{8,10},{9,11},{10,... | collective-permute-start | bytes 786440 | tf_op jit(solution)/shard_map/ppermute | solution.py:350
  85.1 21.9 %collective-permute-start.18 = (f32[1024,128]{1,0:T(8,128)S(1)}, f32[1024,128]{1,0:T(8,128)S(1)}, u32[]{:S(2)}, u32[]{:S(2)}) collective-permute-start(f32[1024,128]{1,0:T(8,128)S(1)} %get-tuple-element.35), channel_id=1, source_target_pairs={{0,16},{16,0},{1,17},{17,1},{2,18},{18,2},{3,19},{19,3},{4,20},{20... | collective-permute-start | bytes 1572872 | tf_op jit(solution)/shard_map/ppermute | solution.py:478
  87.7 9.0 %collective-permute-start.16 = (bf16[2,512,128]{2,1,0:T(8,128)(2,1)S(1)}, bf16[2,512,128]{2,1,0:T(8,128)(2,1)S(1)}, u32[]{:S(2)}, u32[]{:S(2)}) collective-permute-start(bf16[2,512,128]{2,1,0:T(8,128)(2,1)S(1)} %add_convert_fusion), channel_id=1, source_target_pairs={{0,4},{1,5},{2,6},{3,7},{4,0},{5,1},{6,2},{7,3},{8,12},{9,13},{10,... | collective-permute-start | bytes 786440 | tf_op jit(solution)/shard_map/ppermute | solution.py:350
  91.6 13.4 %collective-permute-start.13 = (bf16[1,512,128]{2,1,0:T(8,128)(2,1)S(1)}, bf16[1,512,128]{2,1,0:T(8,128)(2,1)S(1)}, u32[]{:S(2)}, u32[]{:S(2)}) collective-permute-start(bf16[1,512,128]{2,1,0:T(8,128)(2,1)S(1)} %dynamic-slice_convert_fusion.1), channel_id=1, source_target_pairs={{0,8},{1,9},{2,10},{3,11},{4,12},{5,13},{6,14},{7,15},{8,0},{9,1},... | collective-permute-start | bytes 393224 | tf_op jit(solution)/shard_map/ppermute | solution.py:350
  96.8 10.1 %collective-permute-start.17 = (bf16[1,512,128]{2,1,0:T(8,128)(2,1)S(1)}, bf16[1,512,128]{2,1,0:T(8,128)(2,1)S(1)}, u32[]{:S(2)}, u32[]{:S(2)}) collective-permute-start(bf16[1,512,128]{2,1,0:T(8,128)(2,1)S(1)} %dynamic-slice_convert_fusion), channel_id=1, source_target_pairs={{0,8},{1,9},{2,10},{3,11},{4,12},{5,13},{6,14},{7,15},{8,0},{9,1},... | collective-permute-start | bytes 393224 | tf_op jit(solution)/shard_map/ppermute | solution.py:350
  107.0 1.6 %copy-start.1 = (bf16[1024,1024]{1,0:T(8,128)(2,1)S(1)}, bf16[1024,1024]{1,0:T(8,128)(2,1)}, u32[]{:S(2)}) copy-start(bf16[1024,1024]{1,0:T(8,128)(2,1)} %copy-done) | copy-start | bytes 6291460
  123.7 1.6 %copy-start.2 = (bf16[1024,1024]{1,0:T(8,128)(2,1)S(1)}, bf16[1024,1024]{1,0:T(8,128)(2,1)}, u32[]{:S(2)}) copy-start(bf16[1024,1024]{1,0:T(8,128)(2,1)} %copy-done) | copy-start | bytes 6291460

commit v4 on v3

--- a/solution.py
+++ b/solution.py
@@ -27,7 +27,7 @@
 
 
 def band_kernel(
-    angles, phases, index_ref, scalar_ref, raw_hbm, *rest
+    angles, phases, index_ref, whole_ref, unmix_ref, raw_hbm, *rest
 ):
     parts = rest[:4]
     cos_ref, sin_ref, left_ref, raw_ref, low, spec, turned_even, turned_odd, phase, sem = rest[4:]
@@ -44,7 +44,7 @@
     pair = 2 * slab
 
     def offset(which, axis):
-        return scalar_ref[0, which, 0, 2 * phases + axis].astype(jnp.int32)
+        return whole_ref[which, axis]
 
     fetch = pltpu.make_async_copy(raw_hbm, raw_ref, sem)
     fetch.start()
@@ -119,8 +119,8 @@
     quarter_tiles = lane_tiles // 4
 
     def weight(which, m, j):
-        column = scalar_ref[0, which, 0, phases + j].astype(jnp.int32)
-        return scalar_ref[0, which, m, column], scalar_ref[1, which, m, column]
+        column = whole_ref[which, 2 + j]
+        return unmix_ref[0, which, m, column], unmix_ref[1, which, m, column]
 
     def combine(terms, rows, slot):
         for tab in range(lane_tiles):
@@ -202,44 +202,17 @@
         put_out(angles * others, rows, turned_even, shift_of(angles * others))
 
 
-def numer_kernel(
-    slab, bands, columns, masks, with_power, index_ref, scalar_ref, own_ref, other_ref, left_ref,
-    near_ref, far_ref, *rest
-):
-    outs = rest[:4]
-    power_ref = rest[4] if with_power else None
-    wide, total, right = rest[-3:]
+def shift_by(whole_ref, band, axis):
+    if band == 0:
+        return 0
+    which, m = divmod(band - 1, len(MULTIPLES) - 1)
+    return MULTIPLES[m + 1] * whole_ref[which, axis]
+
+
+def widen_otf(wide, masks, index, near_ref, far_ref):
     lane_tiles = wide.shape[0]
     pixels = lane_tiles * LANES
-    tile = wide.shape[1] - pixels
-    tiles = own_ref.shape[2] // LANES
-    half = tiles // 2
-    pieces = near_ref.shape[0]
-    others = len(MULTIPLES) - 1
-    index = index_ref[0]
-    core = index & 1
-    chip = index >> 1
-    levels = (pixels // columns // 2).bit_length() - 1
-    place = sum(((chip >> bit) & 1) << (levels - 1 - bit) for bit in range(levels))
-    quarter = (chip & 1) if with_power else 1 - (chip & 1)
-    start_column = (2 * core + quarter) * (pixels // 4)
-    own_column = core * (pixels // 2) + place * columns
-
-    def shift_of(band, axis):
-        if band == 0:
-            return 0
-        which, m = divmod(band - 1, others)
-        return MULTIPLES[m + 1] * scalar_ref[0, which, 0, scalar_ref.shape[3] - 2 + axis].astype(
-            jnp.int32
-        )
-
-    @pl.loop(0, bands)
-    def _(band):
-        for ref, side in ((own_ref, core), (other_ref, 1 - core)):
-            for part in range(2):
-                put = pl.ds(pl.multiple_of((2 * part + side) * slab, slab), slab)
-                right[band, put, :] = ref[band, part * slab : (part + 1) * slab, :]
-
+    pieces, slab = near_ref.shape[:2]
     for piece in range(2 * pieces):
         ref = far_ref if piece >= pieces else near_ref
         start = pl.multiple_of((index ^ masks[piece]) * slab, slab)
@@ -248,33 +221,76 @@
                 piece % pieces, :, lane * LANES : (lane + 1) * LANES
             ].astype(jnp.float32)
     for lane in range(lane_tiles):
-        wide[lane, pixels : pixels + tile, :] = wide[lane, 0:tile, :]
-
+        wide[lane, pixels:, :] = wide[lane, 0 : wide.shape[1] - pixels, :]
+
+
+def response(wide, whole_ref, q0, band, column, count):
+    lane_tiles = wide.shape[0]
+    pixels = lane_tiles * LANES
+    tile = wide.shape[1] - pixels
+    start = (q0 - shift_by(whole_ref, band, 0)) & (pixels - 1)
+    column = (column - shift_by(whole_ref, band, 1)) & (pixels - 1)
+    rest_lanes = column & (LANES - 1)
+    first = column // LANES
+    turn = (LANES - rest_lanes) & (LANES - 1)
     lanes = lax.broadcasted_iota(jnp.int32, (tile, LANES), 1)
-
-    def response(q0, band, column, count):
-        start = (q0 - shift_of(band, 0)) & (pixels - 1)
-        column = (column - shift_of(band, 1)) & (pixels - 1)
-        rest_lanes = column & (LANES - 1)
-        first = column // LANES
-        turn = (LANES - rest_lanes) & (LANES - 1)
-        turned = [
-            pltpu.roll(wide[(first + i) & (lane_tiles - 1), pl.ds(start, tile), :], turn, 1)
-            for i in range(count + 1)
-        ]
-        return [
-            jnp.where(lanes < LANES - rest_lanes, turned[i], turned[i + 1]) for i in range(count)
-        ]
-
-    side = (chip >> 1) & 1
+    turned = [
+        pltpu.roll(wide[(first + i) & (lane_tiles - 1), pl.ds(start, tile), :], turn, 1)
+        for i in range(count + 1)
+    ]
+    return [jnp.where(lanes < LANES - rest_lanes, turned[i], turned[i + 1]) for i in range(count)]
+
+
+def numer_kernel(
+    columns, masks, own, index_ref, whole_ref, keep_away, got_away, keep_near, got_near, left_ref,
+    near_ref, far_ref, *rest
+):
+    outs = rest[:4]
+    wide, total, right, right_up = rest[4:]
+    pixels = wide.shape[0] * LANES
+    tile = wide.shape[1] - pixels
+    bands, twice, width = keep_away.shape
+    slab = twice // 2
+    tiles = width // LANES
+    half = tiles // 2
+    index = index_ref[0]
+    core = index & 1
+    chip = index >> 1
+    sides = (chip & 1, (chip >> 1) & 1)
+    chosen = sides if own else (1 - sides[0], 1 - sides[1])
+    lower = (keep_near, got_near) if own else (keep_away, got_away)
+
+    @pl.loop(0, bands)
+    def _(band):
+        cut = pl.ds(pl.multiple_of(chosen[1] * (half * LANES), LANES), half * LANES)
+        for which, side in ((0, core), (1, 1 - core)):
+            for part in range(2):
+                put = pl.ds(pl.multiple_of((2 * part + side) * slab, slab), slab)
+                rows = slice(part * slab, (part + 1) * slab)
+                right[band, put, :] = lower[which][band, rows, :]
+                for i, pair in enumerate(((keep_away, got_away), (keep_near, got_near))):
+                    to = slice(i * half * LANES, (i + 1) * half * LANES)
+                    right_up[band, put, to] = pair[which][band, rows, cut]
+
+    widen_otf(wide, masks, index, near_ref, far_ref)
+    steps = pixels // tile // 2
 
     def tile_of(step, upper):
-        q0 = pl.multiple_of((step + upper * (pixels // tile // 2)) * tile, tile)
+        q0 = pl.multiple_of((step + upper * steps) * tile, tile)
         to = pl.ds(pl.multiple_of(step * tile, tile), tile)
-        left = left_ref[step + upper * (pixels // tile // 2)]
+        left = left_ref[step + upper * steps]
         for band in range(bands):
-            product = jnp.dot(left, right[band], preferred_element_type=jnp.float32)
-            weights = response(q0, band, start_column, tiles)
+            product = jnp.dot(
+                left, (right_up if upper else right)[band], preferred_element_type=jnp.float32
+            )
+            if upper:
+                weights = []
+                for side in (1 - sides[0], sides[0]):
+                    column = (2 * core + side) * width + chosen[1] * (half * LANES)
+                    weights += response(wide, whole_ref, q0, band, column, half)
+            else:
+                column = (2 * core + chosen[0]) * width
+                weights = response(wide, whole_ref, q0, band, column, tiles)
             for i in range(tiles):
                 cut = slice(i * LANES, (i + 1) * LANES)
                 for part in range(2):
@@ -285,31 +301,82 @@
                         total[i, part] += value
         for which in range(2):
             out = outs[2 * which + upper]
-            first = (side if which == 1 else 1 - side) * half
+            first = which if upper else (sides[1] if which else 1 - sides[1])
             per_tile = LANES // columns
             for i in range(half):
-                real = total[first + i, 0]
-                imag = total[first + i, 1]
+                real = total[first * half + i, 0]
+                imag = total[first * half + i, 1]
                 for j in range(per_tile):
                     cut = slice(j * columns, (j + 1) * columns)
                     out[i * per_tile + j, to, :] = jnp.concatenate(
                         [real[:, cut], imag[:, cut]], axis=1
                     ).astype(jnp.bfloat16)
-        if with_power:
-            gathered = None
-            for band in range(bands):
-                value = response(q0, band, own_column, 1)[0]
-                value = value * value
-                if band == 0:
-                    gathered = value * float((bands - 1) // others)
-                else:
-                    gathered = gathered + value
-            power_ref[pl.ds(q0, tile), :] = jnp.concatenate(
-                [gathered[:, :columns], gathered[:, :columns]], axis=1
-            )
 
     for upper in range(2):
-        pl.loop(0, pixels // tile // 2)(functools.partial(tile_of, upper=upper))
+        pl.loop(0, steps)(functools.partial(tile_of, upper=upper))
+
+
+def power_kernel(columns, bands, masks, index_ref, whole_ref, near_ref, far_ref, after, power_ref, wide):
+    pixels = power_ref.shape[0]
+    tile = wide.shape[1] - pixels
+    index = index_ref[0]
+    core = index & 1
+    chip = index >> 1
+    levels = (pixels // columns // 2).bit_length() - 1
+    place = sum(((chip >> bit) & 1) << (levels - 1 - bit) for bit in range(levels))
+    own_column = core * (pixels // 2) + place * columns
+    angles = (bands - 1) // (len(MULTIPLES) - 1)
+    widen_otf(wide, masks, index, near_ref, far_ref)
+
+    @pl.loop(0, pixels // tile)
+    def _(step):
+        q0 = pl.multiple_of(step * tile, tile)
+        gathered = None
+        for band in range(bands):
+            value = response(wide, whole_ref, q0, band, own_column, 1)[0]
+            value = value * value
+            gathered = value * float(angles) if band == 0 else gathered + value
+        power_ref[pl.ds(q0, tile), :] = jnp.concatenate(
+            [gathered[:, :columns], gathered[:, :columns]], axis=1
+        )
+
+
+def fold_kernel(bit, index_ref, *refs):
+    *parts, far_ref, stay_ref = refs
+    count = far_ref.shape[0]
+    side = (index_ref[0] >> (bit + 1)) & 1
+    for block in range(count):
+        for out, first in ((far_ref, (1 - side) * count), (stay_ref, side * count)):
+            value = None
+            for ref in parts:
+                one = ref[first + block].astype(jnp.float32)
+                value = one if value is None else value + one
+            out[block] = value.astype(out.dtype)
+
+
+def inverse_kernel(columns, total, numers, *refs):
+    parts = refs[: 2 * numers]
+    *powers, cos_ref, sin_ref, half_ref, ratio = refs[2 * numers :]
+    pixels = half_ref.shape[0]
+    rows = pixels // 2
+    for upper in range(2):
+        here = slice(upper * rows, (upper + 1) * rows)
+        power = powers[0][here, :]
+        for ref in powers[1:]:
+            power = power + ref[here, :]
+        numer = None
+        for ref in parts[upper * numers : (upper + 1) * numers]:
+            one = ref[0].astype(jnp.float32)
+            numer = one if numer is None else numer + one
+        ratio[here, :] = (numer / (WIENER + power / total)).astype(jnp.bfloat16)
+    tile = 256
+    for first in range(0, pixels, tile):
+        here = slice(first, first + tile)
+        by_cos = jnp.dot(cos_ref[here, :], ratio[...], preferred_element_type=jnp.float32)
+        by_sin = jnp.dot(sin_ref[here, :], ratio[...], preferred_element_type=jnp.float32)
+        real = by_cos[:, :columns] - by_sin[:, columns:]
+        imag = by_cos[:, columns:] + by_sin[:, :columns]
+        half_ref[here, :] = jnp.concatenate([real, -imag], axis=1).astype(jnp.bfloat16)
 
 
 def pack_kernel(*refs):
@@ -330,7 +397,7 @@
         rows = []
         for core in range(2):
             start = core * (pixels // 2) + place * columns
-            rows += [cos_ref[start : start + columns, :], sin_ref[start : start + columns, :]]
+            rows += [ref[start : start + columns, :] for ref in (cos_ref, sin_ref)]
         left = jnp.concatenate([back_ref[2 * chip], back_ref[2 * chip + 1]], axis=1)
         value = jnp.dot(left, jnp.concatenate(rows, axis=0), preferred_element_type=jnp.float32)
         total = value if total is None else total + value
@@ -359,7 +426,6 @@
     slices = raw.shape[0] * lax.axis_size("cuts")
     chips = devices // 2
     levels = chips.bit_length() - 1
-    chip = index >> 1
     columns = pixels // devices
     frames = angles * phases
     bands = 1 + angles * (len(MULTIPLES) - 1)
@@ -371,25 +437,16 @@
 
     quarter = pixels // 4
     where = index.astype(jnp.int32).reshape(1)
-    share = unmix.shape[:3]
-    scalars = jnp.concatenate(
-        [
-            unmix,
-            jnp.broadcast_to(phase_order.astype(jnp.float32)[None, :, None, :], share + (phases,)),
-            jnp.broadcast_to(offsets.astype(jnp.float32)[None, :, None, :], share + (2,)),
-        ],
-        axis=3,
-    )
-    table = jax.ShapeDtypeStruct((pixels, pixels), jnp.bfloat16)
-    hbm = pl.BlockSpec(memory_space=pl.ANY)
+    whole = jnp.concatenate([offsets, phase_order], axis=1)
+    hbm = pl.BlockSpec(memory_space=pltpu.HBM)
     part = (bands, 2 * slab, quarter)
     left_shape = (pixels // LANES, 2 * LANES, 4 * slab)
     send_away, send_near, keep_away, keep_near, cosine, sine, left = pl.pallas_call(
         functools.partial(band_kernel, angles, phases),
         out_shape=[jax.ShapeDtypeStruct(part, jnp.bfloat16)] * 4
-        + [table] * 2
+        + [jax.ShapeDtypeStruct((pixels, pixels), jnp.bfloat16)] * 2
         + [jax.ShapeDtypeStruct(left_shape, jnp.bfloat16)],
-        in_specs=[smem()] * 2 + [hbm],
+        in_specs=[smem()] * 3 + [hbm],
         out_specs=[vmem()] * 7,
         scratch_shapes=[
             pltpu.VMEM((frames * slab, pixels), jnp.bfloat16),
@@ -405,9 +462,9 @@
             bytes_accessed=12 << 20,
             transcendentals=0,
         ),
-        compiler_params=pltpu.CompilerParams(vmem_limit_bytes=26 << 20),
+        compiler_params=pltpu.CompilerParams(vmem_limit_bytes=18 << 20),
         name="bands",
-    )(where, scalars, raw.reshape(frames * slab, pixels))
+    )(where, whole, unmix, raw.reshape(frames * slab, pixels))
 
     got_away = swap(send_away, "row", 1)
     own_pieces = pl.pallas_call(
@@ -424,19 +481,19 @@
     other_pieces = swap(own_pieces, "row", 1)
     got_near = swap(send_near, "row", 1)
 
-    def partial(own, other, with_power):
-        half_shape = (chips // 4, pixels // 2, 2 * columns)
-        out_shape = [jax.ShapeDtypeStruct(half_shape, jnp.bfloat16)] * 4
-        if with_power:
-            out_shape = out_shape + [jax.ShapeDtypeStruct((pixels, 2 * columns), jnp.float32)]
+    half_shape = jax.ShapeDtypeStruct((chips // 4, pixels // 2, 2 * columns), jnp.bfloat16)
+    wide_scratch = pltpu.VMEM((pixels // LANES, pixels + LANES, LANES), jnp.float32)
+
+    def partial(own):
         return pl.pallas_call(
-            functools.partial(numer_kernel, slab, bands, columns, masks, with_power),
-            out_shape=out_shape,
-            in_specs=[smem()] * 2 + [vmem()] * 5,
-            out_specs=[vmem()] * len(out_shape),
+            functools.partial(numer_kernel, columns, tuple(masks), own),
+            out_shape=[half_shape] * 4,
+            in_specs=[smem()] * 2 + [vmem()] * 7,
+            out_specs=[vmem()] * 4,
             scratch_shapes=[
-                pltpu.VMEM((pixels // LANES, pixels + LANES, LANES), jnp.float32),
+                wide_scratch,
                 pltpu.VMEM((quarter // LANES, 2, LANES, LANES), jnp.float32),
+                pltpu.VMEM((bands, 4 * slab, quarter), jnp.bfloat16),
                 pltpu.VMEM((bands, 4 * slab, quarter), jnp.bfloat16),
             ],
             cost_estimate=pl.CostEstimate(
@@ -444,51 +501,78 @@
                 bytes_accessed=8 << 20,
                 transcendentals=0,
             ),
-            compiler_params=pltpu.CompilerParams(vmem_limit_bytes=16 << 20),
-        )(where, scalars, own, other, left, own_pieces, other_pieces)
-
-    away = partial(keep_away, got_away, False)
-    moved = [swap(value, "row", 2) for value in away]
-    *kept, power = partial(keep_near, got_near, True)
-
-    def split(blocks, bit):
-        count = blocks.shape[0] // 2
-        side = (chip >> bit) & 1
-        return (
-            lax.dynamic_slice_in_dim(blocks, (1 - side) * count, count, 0),
-            lax.dynamic_slice_in_dim(blocks, side * count, count, 0),
+            compiler_params=pltpu.CompilerParams(vmem_limit_bytes=18 << 20),
+        )(
+            where, whole, keep_away, got_away, keep_near, got_near, left, own_pieces,
+            other_pieces
         )
+
+    away = partial(False)
+    moved = [swap(value, "row", mask) for value, mask in zip(away, (2, 4, 2, 4))]
+    kept = partial(True)
+    power = pl.pallas_call(
+        functools.partial(power_kernel, columns, bands, tuple(masks)),
+        out_shape=jax.ShapeDtypeStruct((pixels, 2 * columns), jnp.float32),
+        in_specs=[smem()] * 2 + [vmem()] * 2 + [pl.BlockSpec(memory_space=pl.ANY)],
+        out_specs=vmem(),
+        scratch_shapes=[wide_scratch],
+        cost_estimate=pl.CostEstimate(
+            flops=16000 * pixels * columns, bytes_accessed=5 << 20, transcendentals=0
+        ),
+        compiler_params=pltpu.CompilerParams(vmem_limit_bytes=12 << 20),
+        name="power",
+    )(where, whole, own_pieces, other_pieces, kept[0])
+
+    def fold(bit, parts):
+        blocks, rows, lanes = parts[0].shape
+        share = (blocks // 2, rows, lanes)
+        return pl.pallas_call(
+            functools.partial(fold_kernel, bit),
+            out_shape=[
+                jax.ShapeDtypeStruct(share, jnp.bfloat16),
+                jax.ShapeDtypeStruct(share, jnp.float32),
+            ],
+            in_specs=[smem()] + [vmem()] * len(parts),
+            out_specs=[vmem()] * 2,
+            cost_estimate=pl.CostEstimate(
+                flops=blocks * rows * lanes * 4, bytes_accessed=1 << 20, transcendentals=0
+            ),
+            compiler_params=pltpu.CompilerParams(vmem_limit_bytes=8 << 20),
+            name="fold",
+        )(where, *parts)
 
     def widen(value):
         return value.astype(jnp.float32)
 
-    fars = [widen(moved[h]) + widen(kept[h]) for h in range(2)]
-    stays = [widen(moved[2 + h]) + widen(kept[2 + h]) for h in range(2)]
+    fars = [(widen(moved[h]) + widen(kept[h])).astype(jnp.bfloat16) for h in range(2)]
+    stays = [[moved[2 + h], kept[2 + h]] for h in range(2)]
     for bit in range(1, levels):
-        got_next = [swap(far.astype(jnp.bfloat16), "row", 2 << bit) for far in fars]
-        stays = [stay + widen(got) for stay, got in zip(stays, got_next)]
-        if bit < levels - 1:
-            fars, stays = zip(*[split(stay, bit + 1) for stay in stays])
-    numer = jnp.concatenate([stay[0] for stay in stays])
-
-    total_power = power
-    moving = power
+        over = (2 << bit, 2) if bit == 1 else (2 << bit, 2 << bit)
+        for h in range(2):
+            stays[h].append(swap(fars[h], "row", over[h]))
+            if bit < levels - 1:
+                fars[h], stay = fold(bit + 1, stays[h])
+                stays[h] = [stay]
+
+    powers = [power]
     cuts = lax.axis_size("cuts")
     for _ in range(cuts - 1):
-        moving = lax.ppermute(moving, "cuts", [(i, (i + 1) % cuts) for i in range(cuts)])
-        total_power = total_power + moving
-    denom = WIENER + total_power / (slices * angles)
-    ratio = (numer / denom).astype(jnp.bfloat16)
-
-    by_cos = jnp.dot(cosine, ratio, preferred_element_type=jnp.float32)
-    by_sin = jnp.dot(sine, ratio, preferred_element_type=jnp.float32)
-    half = jnp.concatenate(
-        [
-            by_cos[:, :columns] - by_sin[:, columns:],
-            -by_cos[:, columns:] - by_sin[:, :columns],
-        ],
-        axis=1,
-    ).astype(jnp.bfloat16)
+        powers.append(
+            lax.ppermute(powers[-1], "cuts", [(i, (i + 1) % cuts) for i in range(cuts)])
+        )
+    parts = stays[0] + stays[1] + powers
+    half = pl.pallas_call(
+        functools.partial(inverse_kernel, columns, float(slices * angles), len(stays[0])),
+        out_shape=jax.ShapeDtypeStruct((pixels, 2 * columns), jnp.bfloat16),
+        in_specs=[vmem()] * (len(parts) + 2),
+        out_specs=vmem(),
+        scratch_shapes=[pltpu.VMEM((pixels, 2 * columns), jnp.bfloat16)],
+        cost_estimate=pl.CostEstimate(
+            flops=8 * pixels * pixels * columns, bytes_accessed=6 << 20, transcendentals=0
+        ),
+        compiler_params=pltpu.CompilerParams(vmem_limit_bytes=12 << 20),
+        name="inverse",
+    )(*parts, cosine, sine)
     back = lax.all_to_all(
         half.reshape(devices, slab, 2 * columns), "row", split_axis=0, concat_axis=0, tiled=True
     )
@@ -500,7 +584,7 @@
         cost_estimate=pl.CostEstimate(
             flops=4 * slab * pixels * pixels, bytes_accessed=6 << 20, transcendentals=0
         ),
-        compiler_params=pltpu.CompilerParams(vmem_limit_bytes=12 << 20),
+        compiler_params=pltpu.CompilerParams(vmem_limit_bytes=8 << 20),
         name="image",
     )(back, cosine, sine)
     return recon.reshape(otf.shape)

time: 127 us -> 124 us (0.976)
  other arithmetic: 5.96 us -> 2 us
  Pallas kernels: 45.4 us -> 49 us
  local copies, waits for them, and re-layouts: 4.11 us -> 1.49 us
  matrix products: 1.65 us -> 0 us
    pallas_call x2 -> x6, Pallas kernels: 25.2 us -> 29.1 us  [the longest x2 21.6 us: partial(): pl.pallas_call(functools.partial(numer_kernel, columns, tuple(masks), own...]
    convert_element_type x5 -> x2, other arithmetic: 3.44 us -> 0.14 us  [shards(): (widen(moved[h]) + widen(kept[h])).astype(jnp.bfloat16)]
    unnamed x11 -> x4, local copies, waits for them, and re-layouts: 3.62 us -> 1.49 us
    dot_general x2 -> x0, matrix products: 1.65 us -> none  [the longest x1 0.83 us: shards(): by_cos = jnp.dot(cosine, ratio, preferred_element_type=jnp.float32)]
  transfers between devices with their start and end apart: 19 -> 19, of which waited for: 7 -> 9; matrix products, arithmetic and copies ran while one was open for 4% -> 2% of each run, Pallas kernels for 35% -> 29%
where the time goes in v4:
time: 124 us; the launch traced here: 123 us
  Pallas kernels  49 us (40%)
  starting transfers between devices  33.4 us (27%)
  waiting for transfers between devices  23.5 us (19%)
  blocking collectives  13.8 us (11%)
  other arithmetic  2 us (2%)
  local copies, waits for them, and re-layouts  1.49 us (1%)
    ppermute x18, starting transfers between devices, swap(): return lax.ppermute(value, axis, [(i, i ^ mask) for i in range(size)])  31.9 us
    ppermute x18, waiting for transfers between devices, swap(): return lax.ppermute(value, axis, [(i, i ^ mask) for i in range(size)])  22.5 us
    pallas_call x2, Pallas kernels, partial(): pl.pallas_call(functools.partial(numer_kernel, columns, tuple(masks), own...  21.6 us
    pallas_call x1, Pallas kernels, shards(): pl.pallas_call(functools.partial(band_kernel, angles, phases), out_shape=...  18.3 us
    all_to_all x1, blocking collectives, shards(): lax.all_to_all(half.reshape(devices, slab, 2 * columns), 'row', split_axi...  13.8 us
    pallas_call x1, Pallas kernels, shards(): pl.pallas_call(functools.partial(power_kernel, columns, bands, tuple(mask...  5.86 us
  transfers between devices with their start and end apart: 19, of which 9 were waited for; matrix products, arithmetic and copies ran while one was open for 2% of the time, Pallas kernels for 29%

profile of v4, /device:TPU:0, one launch (start us, length us, event | category | flops | bytes accessed | tf_op | source)
XLA Modules:
  0.0 123.2 jit_solution(18203292596652477307)
XLA Ops:
  0.0 0.0 copy-start
  0.0 1.1 convert_bitcast_fusion.refs_0_
  1.1 6.1 %collective-permute-start.8 = (bf16[64,1024]{1,0:T(8,128)(2,1)S(1)}, bf16[64,1024]{1,0:T(8,128)(2,1)S(1)}, u32[]{:S(2)}, u32[]{:S(2)}) collective-permute-start(bf16[64,1024]{1,0:T(8,128)(2,1)S(1)} %convert_bitcast_fusion.refs_0_), channel_id=1, source_target_pairs={{0,14},{1,15},{2,12},{3,13},{4,10},{5,11},{6,8},{7,9},{8,6},{9,7},... | collective-permute-start | bytes 393224 | tf_op jit(solution)/shard_map/ppermute | solution.py:417
  7.2 0.2 collective-permute-start.7
  7.4 0.7 collective-permute-start.6
  8.2 2.0 %collective-permute-start.5 = (bf16[64,1024]{1,0:T(8,128)(2,1)S(1)}, bf16[64,1024]{1,0:T(8,128)(2,1)S(1)}, u32[]{:S(2)}, u32[]{:S(2)}) collective-permute-start(bf16[64,1024]{1,0:T(8,128)(2,1)S(1)} %convert_bitcast_fusion.refs_0_), channel_id=1, source_target_pairs={{0,8},{1,9},{2,10},{3,11},{4,12},{5,13},{6,14},{7,15},{8,0},{9,1},... | collective-permute-start | bytes 393224 | tf_op jit(solution)/shard_map/ppermute | solution.py:417
  10.2 2.3 %collective-permute-start.4 = (bf16[64,1024]{1,0:T(8,128)(2,1)S(1)}, bf16[64,1024]{1,0:T(8,128)(2,1)S(1)}, u32[]{:S(2)}, u32[]{:S(2)}) collective-permute-start(bf16[64,1024]{1,0:T(8,128)(2,1)S(1)} %convert_bitcast_fusion.refs_0_), channel_id=1, source_target_pairs={{0,6},{1,7},{2,4},{3,5},{4,2},{5,3},{6,0},{7,1},{8,14},{9,15},{10,... | collective-permute-start | bytes 393224 | tf_op jit(solution)/shard_map/ppermute | solution.py:417
  12.5 0.0 collective-permute-done.8.refs_7_
  12.5 10.4 %collective-permute-start.3 = (bf16[64,1024]{1,0:T(8,128)(2,1)S(1)}, bf16[64,1024]{1,0:T(8,128)(2,1)S(1)}, u32[]{:S(2)}, u32[]{:S(2)}) collective-permute-start(bf16[64,1024]{1,0:T(8,128)(2,1)S(1)} %convert_bitcast_fusion.refs_0_), channel_id=1, source_target_pairs={{0,4},{1,5},{2,6},{3,7},{4,0},{5,1},{6,2},{7,3},{8,12},{9,13},{10,... | collective-permute-start | bytes 393224 | tf_op jit(solution)/shard_map/ppermute | solution.py:417
  22.9 0.0 collective-permute-done.7.refs_6_
  22.9 1.3 %collective-permute-start.2 = (bf16[64,1024]{1,0:T(8,128)(2,1)S(1)}, bf16[64,1024]{1,0:T(8,128)(2,1)S(1)}, u32[]{:S(2)}, u32[]{:S(2)}) collective-permute-start(bf16[64,1024]{1,0:T(8,128)(2,1)S(1)} %convert_bitcast_fusion.refs_0_), channel_id=1, source_target_pairs={{0,2},{1,3},{2,0},{3,1},{4,6},{5,7},{6,4},{7,5},{8,10},{9,11},{10,... | collective-permute-start | bytes 393224 | tf_op jit(solution)/shard_map/ppermute | solution.py:417
  24.3 0.8 copy.6
  25.0 0.7 copy.7.unmix_ref
  25.8 0.8 pad_add_fusion.whole_ref
  26.5 1.2 %collective-permute-done.6.refs_5_ = bf16[64,1024]{1,0:T(8,128)(2,1)S(1)} collective-permute-done((bf16[64,1024]{1,0:T(8,128)(2,1)S(1)}, bf16[64,1024]{1,0:T(8,128)(2,1)S(1)}, u32[]{:S(2)}, u32[]{:S(2)}) %collective-permute-start.6) | collective-permute-done | bytes 131104 | tf_op jit(solution)/shard_map/ppermute | solution.py:417
  27.8 1.9 %collective-permute-done.5.refs_4_ = bf16[64,1024]{1,0:T(8,128)(2,1)S(1)} collective-permute-done((bf16[64,1024]{1,0:T(8,128)(2,1)S(1)}, bf16[64,1024]{1,0:T(8,128)(2,1)S(1)}, u32[]{:S(2)}, u32[]{:S(2)}) %collective-permute-start.5) | collective-permute-done | bytes 131104 | tf_op jit(solution)/shard_map/ppermute | solution.py:417
  29.6 0.0 collective-permute-done.4.refs_3_
  29.6 1.1 collective-permute-done.3.refs_2_
  30.8 0.0 collective-permute-done.2.refs_1_
  30.8 0.1 pack.1.near_ref
  30.8 0.1 collective-permute-start.9
  30.9 0.0 copy-done
  30.9 18.3 %bands.1 = (bf16[13,128,256]{2,1,0:T(8,128)(2,1)S(1)}, bf16[13,128,256]{2,1,0:T(8,128)(2,1)S(1)}, bf16[13,128,256]{2,1,0:T(8,128)(2,1)S(1)}, bf16[13,128,256]{2,...) custom-call(s32[1]{0:T(128)} %bitcast.index_ref, ...), custom_call_target="tpu_custom_call" | custom-call | flops 8053063680 | bytes 12582912 | tf_op jit(solution)/shard_map/bands/pallas_call | solution.py:444
  49.2 0.5 collective-permute-start
  49.8 0.1 collective-permute-start.1
  49.8 1.9 %collective-permute-done.got_away = bf16[13,128,256]{2,1,0:T(8,128)(2,1)S(1)} collective-permute-done((bf16[13,128,256]{2,1,0:T(8,128)(2,1)S(1)}, bf16[13,128,256]{2,1,0:T(8,128)(2,1)S(1)}, u32[]{:S(2)}, u32[]{:S(2)}) %collective-permute-start) | collective-permute-done | bytes 852000 | tf_op jit(solution)/shard_map/ppermute | solution.py:417
  51.8 1.2 collective-permute-done.1.got_near
  53.0 0.0 collective-permute-done.9.far_ref
  53.0 10.8 %shard_map.55 = (bf16[2,512,128]{2,1,0:T(8,128)(2,1)S(1)}, bf16[2,512,128]{2,1,0:T(8,128)(2,1)S(1)}, bf16[2,512,128]{2,1,0:T(8,128)(2,1)S(1)}, bf16[2,512,128]{2,1,0:T(8,128)(2,1)S(1)}) custom-call(s32[1]{0:T(128)} %bitcast.index_ref, s32[3,7]{1,0:T(4,128)S(1)} %pad_add_fusion.whole_ref, bf16[13,128,256]{2,1,0:T(8,128)(2,1)S(1)} %get-tuple-element.24.keep_away, ...), custom_call_target="tpu_custom_call" | custom-call | flops 3489660928 | bytes 8388608 | tf_op jit(solution)/shard_map/pallas_call | solution.py:488
  63.8 0.7 collective-permute-start.10
  64.5 1.3 %collective-permute-start.11 = (bf16[2,512,128]{2,1,0:T(8,128)(2,1)S(1)}, bf16[2,512,128]{2,1,0:T(8,128)(2,1)S(1)}, u32[]{:S(2)}, u32[]{:S(2)}) collective-permute-start(bf16[2,512,128]{2,1,0:T(8,128)(2,1)S(1)} %get-tuple-element.31), channel_id=1, source_target_pairs={{0,2},{1,3},{2,0},{3,1},{4,6},{5,7},{6,4},{7,5},{8,10},{9,11},{10,... | collective-permute-start | bytes 786440 | tf_op jit(solution)/shard_map/ppermute | solution.py:417
  65.9 0.0 collective-permute-start.14
  65.9 2.0 %collective-permute-start.15 = (bf16[2,512,128]{2,1,0:T(8,128)(2,1)S(1)}, bf16[2,512,128]{2,1,0:T(8,128)(2,1)S(1)}, u32[]{:S(2)}, u32[]{:S(2)}) collective-permute-start(bf16[2,512,128]{2,1,0:T(8,128)(2,1)S(1)} %get-tuple-element.37), channel_id=1, source_target_pairs={{0,4},{1,5},{2,6},{3,7},{4,0},{5,1},{6,2},{7,3},{8,12},{9,13},{10,... | collective-permute-start | bytes 786440 | tf_op jit(solution)/shard_map/ppermute | solution.py:417
  67.9 10.8 %shard_map.56 = (bf16[2,512,128]{2,1,0:T(8,128)(2,1)S(1)}, bf16[2,512,128]{2,1,0:T(8,128)(2,1)S(1)}, bf16[2,512,128]{2,1,0:T(8,128)(2,1)S(1)}, bf16[2,512,128]{2,1,0:T(8,128)(2,1)S(1)}) custom-call(s32[1]{0:T(128)} %bitcast.index_ref, s32[3,7]{1,0:T(4,128)S(1)} %pad_add_fusion.whole_ref, bf16[13,128,256]{2,1,0:T(8,128)(2,1)S(1)} %get-tuple-element.24.keep_away, ...), custom_call_target="tpu_custom_call" | custom-call | flops 3489660928 | bytes 8388608 | tf_op jit(solution)/shard_map/pallas_call | solution.py:488
  78.7 5.9 %power.1.refs_4_ = f32[1024,128]{1,0:T(8,128)S(1)} custom-call(s32[1]{0:T(128)} %bitcast.index_ref, s32[3,7]{1,0:T(4,128)S(1)} %pad_add_fusion.whole_ref, bf16[8,64,1024]{2,1,0:T(8,128)(2,1)S(1)} %pack.1.near_ref, bf16[8,64,1024]{2,1,0:T(8,128)(2,1)S(1)} %collective-permute-done.9.far_ref, bf16[2,512,128]{2,1,0:T(8,128)(2,1)S(1)} %get-tuple-element.32.after), custom_call_target="tpu_custom_call" | custom-call | flops 1048576000 | bytes 5242880 | tf_op jit(solution)/shard_map/power/pallas_call | solution.py:513
  84.6 1.6 %collective-permute-start.18 = (f32[1024,128]{1,0:T(8,128)S(1)}, f32[1024,128]{1,0:T(8,128)S(1)}, u32[]{:S(2)}, u32[]{:S(2)}) collective-permute-start(f32[1024,128]{1,0:T(8,128)S(1)} %power.1.refs_4_), channel_id=1, source_target_pairs={{0,16},{16,0},{1,17},{17,1},{2,18},{18,2},{3,19},{19,3},{4,20},{20... | collective-permute-start | bytes 1572872 | tf_op jit(solution)/shard_map/ppermute | solution.py:561
  86.1 0.0 collective-permute-done.11
  86.1 0.1 add_convert_fusion.1
  86.2 0.1 collective-permute-start.12
  86.3 0.0 collective-permute-done.15
  86.3 0.1 add_convert_fusion
  86.4 0.7 collective-permute-start.16
  87.1 0.0 collective-permute-done.10.refs_0_
  87.1 6.3 %collective-permute-done.12.refs_2_ = bf16[2,512,128]{2,1,0:T(8,128)(2,1)S(1)} collective-permute-done((bf16[2,512,128]{2,1,0:T(8,128)(2,1)S(1)}, bf16[2,512,128]{2,1,0:T(8,128)(2,1)S(1)}, u32[]{:S(2)}, u32[]{:S(2)}) %collective-permute-start.12) | collective-permute-done | bytes 262176 | tf_op jit(solution)/shard_map/ppermute | solution.py:417
  93.5 0.1 fold.2
  93.6 1.2 collective-permute-start.13
  94.7 0.0 collective-permute-done.14.refs_0_
  94.7 0.0 collective-permute-done.16.refs_2_
  94.7 0.1 fold.3
  94.8 1.9 %collective-permute-start.17 = (bf16[1,512,128]{2,1,0:T(8,128)(2,1)S(1)}, bf16[1,512,128]{2,1,0:T(8,128)(2,1)S(1)}, u32[]{:S(2)}, u32[]{:S(2)}) collective-permute-start(bf16[1,512,128]{2,1,0:T(8,128)(2,1)S(1)} %get-tuple-element.40), channel_id=1, source_target_pairs={{0,8},{1,9},{2,10},{3,11},{4,12},{5,13},{6,14},{7,15},{8,0},{9,1},... | collective-permute-start | bytes 393224 | tf_op jit(solution)/shard_map/ppermute | solution.py:417
  96.7 1.0 collective-permute-done.18.refs_5_
  97.7 6.8 %collective-permute-done.13.refs_1_ = bf16[1,512,128]{2,1,0:T(8,128)(2,1)S(1)} collective-permute-done((bf16[1,512,128]{2,1,0:T(8,128)(2,1)S(1)}, bf16[1,512,128]{2,1,0:T(8,128)(2,1)S(1)}, u32[]{:S(2)}, u32[]{:S(2)}) %collective-permute-start.13) | collective-permute-done | bytes 131104 | tf_op jit(solution)/shard_map/ppermute | solution.py:417
  104.5 2.0 %collective-permute-done.17.refs_3_ = bf16[1,512,128]{2,1,0:T(8,128)(2,1)S(1)} collective-permute-done((bf16[1,512,128]{2,1,0:T(8,128)(2,1)S(1)}, bf16[1,512,128]{2,1,0:T(8,128)(2,1)S(1)}, u32[]{:S(2)}, u32[]{:S(2)}) %collective-permute-start.17) | collective-permute-done | bytes 131104 | tf_op jit(solution)/shard_map/ppermute | solution.py:417
  106.5 1.4 %inverse.1 = bf16[1024,128]{1,0:T(8,128)(2,1)S(1)} custom-call(f32[1,512,128]{2,1,0:T(8,128)S(1)} %get-tuple-element.33.refs_0_, bf16[1,512,128]{2,1,0:T(8,128)(2,1)S(1)} %collective-permute-done.13.refs_1_, f32[1,512,128]{2,1,0:T(8,128)S(1)} %get-tuple-element.39.refs_2_, bf16[1,512,128]{2,1,0:T(8,128)(2,1)S(1)} %collective-permute-done.17.refs_3_, ...), custom_call_target="tpu_custom_call" | custom-call | flops 536870912 | bytes 6291456 | tf_op jit(solution)/shard_map/inverse/pallas_call | solution.py:564
  107.9 13.8 %all_to_all.5.back_ref = bf16[16,64,128]{2,1,0:T(8,128)(2,1)S(1)} all-to-all(bf16[16,64,128]{2,1,0:T(8,128)(2,1)S(1)} %bitcast.6), channel_id=1, replica_groups=mesh['cuts'=2,'row'=16] {'row'}, dimensions={0} | all-to-all | bytes 524288 | tf_op jit(solution)/shard_map/all_to_all | solution.py:576
  121.7 1.5 %image.1 = f32[64,1024]{1,0:T(8,128)} custom-call(bf16[16,64,128]{2,1,0:T(8,128)(2,1)S(1)} %all_to_all.5.back_ref, bf16[1024,1024]{1,0:T(8,128)(2,1)S(1)} %get-tuple-element.41.refs_6_.cos_ref, bf16[1024,1024]{1,0:T(8,128)(2,1)S(1)} %get-tuple-element.42.refs_7_.sin_ref), custom_call_target="tpu_custom_call" | custom-call | flops 268435456 | bytes 6291456 | tf_op jit(solution)/shard_map/image/pallas_call | solution.py:579
Async XLA Ops:
  0.0 30.9 %copy-start = (bf16[1,3,5,64,1024]{4,3,2,1,0:T(8,128)(2,1)S(1)}, bf16[1,3,5,64,1024]{4,3,2,1,0:T(8,128)(2,1)}, u32[]{:S(2)}) copy-start(bf16[1,3,5,64,1024]{4,3,2,1,0:T(8,128)(2,1)} %param.5) | copy-start | bytes 5898244
  1.1 11.4 %collective-permute-start.8 = (bf16[64,1024]{1,0:T(8,128)(2,1)S(1)}, bf16[64,1024]{1,0:T(8,128)(2,1)S(1)}, u32[]{:S(2)}, u32[]{:S(2)}) collective-permute-start(bf16[64,1024]{1,0:T(8,128)(2,1)S(1)} %convert_bitcast_fusion.refs_0_), channel_id=1, source_target_pairs={{0,14},{1,15},{2,12},{3,13},{4,10},{5,11},{6,8},{7,9},{8,6},{9,7},... | collective-permute-start | bytes 393224 | tf_op jit(solution)/shard_map/ppermute | solution.py:417
  7.2 15.7 %collective-permute-start.7 = (bf16[64,1024]{1,0:T(8,128)(2,1)S(1)}, bf16[64,1024]{1,0:T(8,128)(2,1)S(1)}, u32[]{:S(2)}, u32[]{:S(2)}) collective-permute-start(bf16[64,1024]{1,0:T(8,128)(2,1)S(1)} %convert_bitcast_fusion.refs_0_), channel_id=1, source_target_pairs={{0,12},{1,13},{2,14},{3,15},{4,8},{5,9},{6,10},{7,11},{8,4},{9,5},... | collective-permute-start | bytes 393224 | tf_op jit(solution)/shard_map/ppermute | solution.py:417
  7.4 20.3 %collective-permute-start.6 = (bf16[64,1024]{1,0:T(8,128)(2,1)S(1)}, bf16[64,1024]{1,0:T(8,128)(2,1)S(1)}, u32[]{:S(2)}, u32[]{:S(2)}) collective-permute-start(bf16[64,1024]{1,0:T(8,128)(2,1)S(1)} %convert_bitcast_fusion.refs_0_), channel_id=1, source_target_pairs={{0,10},{1,11},{2,8},{3,9},{4,14},{5,15},{6,12},{7,13},{8,2},{9,3},... | collective-permute-start | bytes 393224 | tf_op jit(solution)/shard_map/ppermute | solution.py:417
  8.2 21.5 %collective-permute-start.5 = (bf16[64,1024]{1,0:T(8,128)(2,1)S(1)}, bf16[64,1024]{1,0:T(8,128)(2,1)S(1)}, u32[]{:S(2)}, u32[]{:S(2)}) collective-permute-start(bf16[64,1024]{1,0:T(8,128)(2,1)S(1)} %convert_bitcast_fusion.refs_0_), channel_id=1, source_target_pairs={{0,8},{1,9},{2,10},{3,11},{4,12},{5,13},{6,14},{7,15},{8,0},{9,1},... | collective-permute-start | bytes 393224 | tf_op jit(solution)/shard_map/ppermute | solution.py:417
  10.2 19.4 %collective-permute-start.4 = (bf16[64,1024]{1,0:T(8,128)(2,1)S(1)}, bf16[64,1024]{1,0:T(8,128)(2,1)S(1)}, u32[]{:S(2)}, u32[]{:S(2)}) collective-permute-start(bf16[64,1024]{1,0:T(8,128)(2,1)S(1)} %convert_bitcast_fusion.refs_0_), channel_id=1, source_target_pairs={{0,6},{1,7},{2,4},{3,5},{4,2},{5,3},{6,0},{7,1},{8,14},{9,15},{10,... | collective-permute-start | bytes 393224 | tf_op jit(solution)/shard_map/ppermute | solution.py:417
  12.5 18.3 %collective-permute-start.3 = (bf16[64,1024]{1,0:T(8,128)(2,1)S(1)}, bf16[64,1024]{1,0:T(8,128)(2,1)S(1)}, u32[]{:S(2)}, u32[]{:S(2)}) collective-permute-start(bf16[64,1024]{1,0:T(8,128)(2,1)S(1)} %convert_bitcast_fusion.refs_0_), channel_id=1, source_target_pairs={{0,4},{1,5},{2,6},{3,7},{4,0},{5,1},{6,2},{7,3},{8,12},{9,13},{10,... | collective-permute-start | bytes 393224 | tf_op jit(solution)/shard_map/ppermute | solution.py:417
  22.9 7.8 %collective-permute-start.2 = (bf16[64,1024]{1,0:T(8,128)(2,1)S(1)}, bf16[64,1024]{1,0:T(8,128)(2,1)S(1)}, u32[]{:S(2)}, u32[]{:S(2)}) collective-permute-start(bf16[64,1024]{1,0:T(8,128)(2,1)S(1)} %convert_bitcast_fusion.refs_0_), channel_id=1, source_target_pairs={{0,2},{1,3},{2,0},{3,1},{4,6},{5,7},{6,4},{7,5},{8,10},{9,11},{10,... | collective-permute-start | bytes 393224 | tf_op jit(solution)/shard_map/ppermute | solution.py:417
  30.8 22.1 %collective-permute-start.9 = (bf16[8,64,1024]{2,1,0:T(8,128)(2,1)S(1)}, bf16[8,64,1024]{2,1,0:T(8,128)(2,1)S(1)}, u32[]{:S(2)}, u32[]{:S(2)}) collective-permute-start(bf16[8,64,1024]{2,1,0:T(8,128)(2,1)S(1)} %pack.1.near_ref), channel_id=1, source_target_pairs={{0,1},{1,0},{2,3},{3,2},{4,5},{5,4},{6,7},{7,6},{8,9},{9,8},{10,11... | collective-permute-start | bytes 3145736 | tf_op jit(solution)/shard_map/ppermute | solution.py:417
  49.2 2.6 %collective-permute-start = (bf16[13,128,256]{2,1,0:T(8,128)(2,1)S(1)}, bf16[13,128,256]{2,1,0:T(8,128)(2,1)S(1)}, u32[]{:S(2)}, u32[]{:S(2)}) collective-permute-start(bf16[13,128,256]{2,1,0:T(8,128)(2,1)S(1)} %get-tuple-element.25), channel_id=1, source_target_pairs={{0,1},{1,0},{2,3},{3,2},{4,5},{5,4},{6,7},{7,6},{8,9},{9,8},{10,11... | collective-permute-start | bytes 2555912 | tf_op jit(solution)/shard_map/ppermute | solution.py:417
  49.8 3.2 %collective-permute-start.1 = (bf16[13,128,256]{2,1,0:T(8,128)(2,1)S(1)}, bf16[13,128,256]{2,1,0:T(8,128)(2,1)S(1)}, u32[]{:S(2)}, u32[]{:S(2)}) collective-permute-start(bf16[13,128,256]{2,1,0:T(8,128)(2,1)S(1)} %get-tuple-element.27), channel_id=1, source_target_pairs={{0,1},{1,0},{2,3},{3,2},{4,5},{5,4},{6,7},{7,6},{8,9},{9,8},{10,11... | collective-permute-start | bytes 2555912 | tf_op jit(solution)/shard_map/ppermute | solution.py:417
  63.8 23.4 %collective-permute-start.10 = (bf16[2,512,128]{2,1,0:T(8,128)(2,1)S(1)}, bf16[2,512,128]{2,1,0:T(8,128)(2,1)S(1)}, u32[]{:S(2)}, u32[]{:S(2)}) collective-permute-start(bf16[2,512,128]{2,1,0:T(8,128)(2,1)S(1)} %get-tuple-element.29), channel_id=1, source_target_pairs={{0,2},{1,3},{2,0},{3,1},{4,6},{5,7},{6,4},{7,5},{8,10},{9,11},{10,... | collective-permute-start | bytes 786440 | tf_op jit(solution)/shard_map/ppermute | solution.py:417
  64.5 21.6 %collective-permute-start.11 = (bf16[2,512,128]{2,1,0:T(8,128)(2,1)S(1)}, bf16[2,512,128]{2,1,0:T(8,128)(2,1)S(1)}, u32[]{:S(2)}, u32[]{:S(2)}) collective-permute-start(bf16[2,512,128]{2,1,0:T(8,128)(2,1)S(1)} %get-tuple-element.31), channel_id=1, source_target_pairs={{0,2},{1,3},{2,0},{3,1},{4,6},{5,7},{6,4},{7,5},{8,10},{9,11},{10,... | collective-permute-start | bytes 786440 | tf_op jit(solution)/shard_map/ppermute | solution.py:417
  65.9 28.9 %collective-permute-start.14 = (bf16[2,512,128]{2,1,0:T(8,128)(2,1)S(1)}, bf16[2,512,128]{2,1,0:T(8,128)(2,1)S(1)}, u32[]{:S(2)}, u32[]{:S(2)}) collective-permute-start(bf16[2,512,128]{2,1,0:T(8,128)(2,1)S(1)} %get-tuple-element.35), channel_id=1, source_target_pairs={{0,4},{1,5},{2,6},{3,7},{4,0},{5,1},{6,2},{7,3},{8,12},{9,13},{10,... | collective-permute-start | bytes 786440 | tf_op jit(solution)/shard_map/ppermute | solution.py:417
  65.9 20.4 %collective-permute-start.15 = (bf16[2,512,128]{2,1,0:T(8,128)(2,1)S(1)}, bf16[2,512,128]{2,1,0:T(8,128)(2,1)S(1)}, u32[]{:S(2)}, u32[]{:S(2)}) collective-permute-start(bf16[2,512,128]{2,1,0:T(8,128)(2,1)S(1)} %get-tuple-element.37), channel_id=1, source_target_pairs={{0,4},{1,5},{2,6},{3,7},{4,0},{5,1},{6,2},{7,3},{8,12},{9,13},{10,... | collective-permute-start | bytes 786440 | tf_op jit(solution)/shard_map/ppermute | solution.py:417
  84.6 13.1 %collective-permute-start.18 = (f32[1024,128]{1,0:T(8,128)S(1)}, f32[1024,128]{1,0:T(8,128)S(1)}, u32[]{:S(2)}, u32[]{:S(2)}) collective-permute-start(f32[1024,128]{1,0:T(8,128)S(1)} %power.1.refs_4_), channel_id=1, source_target_pairs={{0,16},{16,0},{1,17},{17,1},{2,18},{18,2},{3,19},{19,3},{4,20},{20... | collective-permute-start | bytes 1572872 | tf_op jit(solution)/shard_map/ppermute | solution.py:561
  86.2 7.3 %collective-permute-start.12 = (bf16[2,512,128]{2,1,0:T(8,128)(2,1)S(1)}, bf16[2,512,128]{2,1,0:T(8,128)(2,1)S(1)}, u32[]{:S(2)}, u32[]{:S(2)}) collective-permute-start(bf16[2,512,128]{2,1,0:T(8,128)(2,1)S(1)} %add_convert_fusion.1), channel_id=1, source_target_pairs={{0,4},{1,5},{2,6},{3,7},{4,0},{5,1},{6,2},{7,3},{8,12},{9,13},{10,... | collective-permute-start | bytes 786440 | tf_op jit(solution)/shard_map/ppermute | solution.py:417
  86.4 8.3 %collective-permute-start.16 = (bf16[2,512,128]{2,1,0:T(8,128)(2,1)S(1)}, bf16[2,512,128]{2,1,0:T(8,128)(2,1)S(1)}, u32[]{:S(2)}, u32[]{:S(2)}) collective-permute-start(bf16[2,512,128]{2,1,0:T(8,128)(2,1)S(1)} %add_convert_fusion), channel_id=1, source_target_pairs={{0,2},{1,3},{2,0},{3,1},{4,6},{5,7},{6,4},{7,5},{8,10},{9,11},{10,... | collective-permute-start | bytes 786440 | tf_op jit(solution)/shard_map/ppermute | solution.py:417
  93.6 11.0 %collective-permute-start.13 = (bf16[1,512,128]{2,1,0:T(8,128)(2,1)S(1)}, bf16[1,512,128]{2,1,0:T(8,128)(2,1)S(1)}, u32[]{:S(2)}, u32[]{:S(2)}) collective-permute-start(bf16[1,512,128]{2,1,0:T(8,128)(2,1)S(1)} %get-tuple-element.34), channel_id=1, source_target_pairs={{0,8},{1,9},{2,10},{3,11},{4,12},{5,13},{6,14},{7,15},{8,0},{9,1},... | collective-permute-start | bytes 393224 | tf_op jit(solution)/shard_map/ppermute | solution.py:417
  94.8 11.6 %collective-permute-start.17 = (bf16[1,512,128]{2,1,0:T(8,128)(2,1)S(1)}, bf16[1,512,128]{2,1,0:T(8,128)(2,1)S(1)}, u32[]{:S(2)}, u32[]{:S(2)}) collective-permute-start(bf16[1,512,128]{2,1,0:T(8,128)(2,1)S(1)} %get-tuple-element.40), channel_id=1, source_target_pairs={{0,8},{1,9},{2,10},{3,11},{4,12},{5,13},{6,14},{7,15},{8,0},{9,1},... | collective-permute-start | bytes 393224 | tf_op jit(solution)/shard_map/ppermute | solution.py:417

commit v5 on v4

--- a/solution.py
+++ b/solution.py
@@ -26,28 +26,11 @@
     return cosine, sine * angle
 
 
-def band_kernel(
-    angles, phases, index_ref, whole_ref, unmix_ref, raw_hbm, *rest
-):
-    parts = rest[:4]
-    cos_ref, sin_ref, left_ref, raw_ref, low, spec, turned_even, turned_odd, phase, sem = rest[4:]
-    frames = angles * phases
-    slab = raw_ref.shape[0] // frames
+def spectra_kernel(slab, index_ref, raw_ref, spec, cos_ref, sin_ref, left_ref, low):
     pixels = raw_ref.shape[1]
-    lane_tiles = pixels // LANES
     tile = 256
-    others = len(MULTIPLES) - 1
-    index = index_ref[0]
-    core = index & 1
-    chip = index >> 1
-    near = chip & 1
+    chip = index_ref[0] >> 1
     pair = 2 * slab
-
-    def offset(which, axis):
-        return whole_ref[which, axis]
-
-    fetch = pltpu.make_async_copy(raw_hbm, raw_ref, sem)
-    fetch.start()
 
     column = lax.broadcasted_iota(jnp.int32, (LANES, LANES), 1)
     unit = 2.0 * math.pi / pixels
@@ -80,7 +63,6 @@
     per_tile = tile // LANES
     for tab in range(per_tile):
         build(tab)
-    fetch.wait()
     for step in range(pixels // tile):
         cut = slice(step * tile, (step + 1) * tile)
         spec[0, :, cut] = jnp.dot(raw_ref[...], cos_ref[:, cut], preferred_element_type=jnp.float32)
@@ -106,6 +88,24 @@
         left_ref[step, LANES:, 0:pair] = -mine[1]
         left_ref[step, LANES:, pair:] = mine[0]
 
+
+def band_kernel(
+    angles, phases, index_ref, shift_ref, unmix_ref, spec, *rest
+):
+    parts = rest[:4]
+    turned_even, turned_odd, phase = rest[4:]
+    frames = angles * phases
+    slab = spec.shape[1] // frames
+    pixels = spec.shape[2]
+    lane_tiles = pixels // LANES
+    others = len(MULTIPLES) - 1
+    index = index_ref[0]
+    core = index & 1
+    near = (index >> 1) & 1
+
+    def offset(which, axis):
+        return shift_ref[axis, which]
+
     image_row = index * slab + lax.broadcasted_iota(jnp.int32, (slab, LANES), 0)
     for which in range(angles):
         for m in range(1, others + 1):
@@ -119,8 +119,8 @@
     quarter_tiles = lane_tiles // 4
 
     def weight(which, m, j):
-        column = whole_ref[which, 2 + j]
-        return unmix_ref[0, which, m, column], unmix_ref[1, which, m, column]
+        column = shift_ref[2 + which, j]
+        return unmix_ref[which, m, 0, column], unmix_ref[which, m, 1, column]
 
     def combine(terms, rows, slot):
         for tab in range(lane_tiles):
@@ -202,20 +202,20 @@
         put_out(angles * others, rows, turned_even, shift_of(angles * others))
 
 
-def shift_by(whole_ref, band, axis):
+def shift_by(shift_ref, band, axis):
     if band == 0:
         return 0
     which, m = divmod(band - 1, len(MULTIPLES) - 1)
-    return MULTIPLES[m + 1] * whole_ref[which, axis]
-
-
-def widen_otf(wide, masks, index, near_ref, far_ref):
+    return MULTIPLES[m + 1] * shift_ref[axis, which]
+
+
+def widen_otf(wide, masks, index, refs):
     lane_tiles = wide.shape[0]
     pixels = lane_tiles * LANES
-    pieces, slab = near_ref.shape[:2]
-    for piece in range(2 * pieces):
-        ref = far_ref if piece >= pieces else near_ref
-        start = pl.multiple_of((index ^ masks[piece]) * slab, slab)
+    pieces, slab = refs[0].shape[:2]
+    for piece, mask in enumerate(masks):
+        ref = refs[piece // pieces]
+        start = pl.multiple_of((index ^ mask) * slab, slab)
         for lane in range(lane_tiles):
             wide[lane, pl.ds(start, slab), :] = ref[
                 piece % pieces, :, lane * LANES : (lane + 1) * LANES
@@ -224,12 +224,12 @@
         wide[lane, pixels:, :] = wide[lane, 0 : wide.shape[1] - pixels, :]
 
 
-def response(wide, whole_ref, q0, band, column, count):
+def response(wide, shift_ref, q0, band, column, count):
     lane_tiles = wide.shape[0]
     pixels = lane_tiles * LANES
     tile = wide.shape[1] - pixels
-    start = (q0 - shift_by(whole_ref, band, 0)) & (pixels - 1)
-    column = (column - shift_by(whole_ref, band, 1)) & (pixels - 1)
+    start = (q0 - shift_by(shift_ref, band, 0)) & (pixels - 1)
+    column = (column - shift_by(shift_ref, band, 1)) & (pixels - 1)
     rest_lanes = column & (LANES - 1)
     first = column // LANES
     turn = (LANES - rest_lanes) & (LANES - 1)
@@ -242,11 +242,12 @@
 
 
 def numer_kernel(
-    columns, masks, own, index_ref, whole_ref, keep_away, got_away, keep_near, got_near, left_ref,
-    near_ref, far_ref, *rest
+    columns, masks, own, index_ref, shift_ref, keep_away, got_away, keep_near, got_near, left_ref,
+    *rest
 ):
-    outs = rest[:4]
-    wide, total, right, right_up = rest[4:]
+    otf_refs = rest[:4]
+    outs = rest[4:8]
+    wide, total, right, right_up = rest[8:]
     pixels = wide.shape[0] * LANES
     tile = wide.shape[1] - pixels
     bands, twice, width = keep_away.shape
@@ -272,7 +273,7 @@
                     to = slice(i * half * LANES, (i + 1) * half * LANES)
                     right_up[band, put, to] = pair[which][band, rows, cut]
 
-    widen_otf(wide, masks, index, near_ref, far_ref)
+    widen_otf(wide, masks, index, otf_refs)
     steps = pixels // tile // 2
 
     def tile_of(step, upper):
@@ -287,10 +288,10 @@
                 weights = []
                 for side in (1 - sides[0], sides[0]):
                     column = (2 * core + side) * width + chosen[1] * (half * LANES)
-                    weights += response(wide, whole_ref, q0, band, column, half)
+                    weights += response(wide, shift_ref, q0, band, column, half)
             else:
                 column = (2 * core + chosen[0]) * width
-                weights = response(wide, whole_ref, q0, band, column, tiles)
+                weights = response(wide, shift_ref, q0, band, column, tiles)
             for i in range(tiles):
                 cut = slice(i * LANES, (i + 1) * LANES)
                 for part in range(2):
@@ -316,7 +317,8 @@
         pl.loop(0, steps)(functools.partial(tile_of, upper=upper))
 
 
-def power_kernel(columns, bands, masks, index_ref, whole_ref, near_ref, far_ref, after, power_ref, wide):
+def power_kernel(columns, bands, masks, index_ref, shift_ref, *rest):
+    *otf_refs, _, power_ref, wide = rest
     pixels = power_ref.shape[0]
     tile = wide.shape[1] - pixels
     index = index_ref[0]
@@ -326,14 +328,14 @@
     place = sum(((chip >> bit) & 1) << (levels - 1 - bit) for bit in range(levels))
     own_column = core * (pixels // 2) + place * columns
     angles = (bands - 1) // (len(MULTIPLES) - 1)
-    widen_otf(wide, masks, index, near_ref, far_ref)
+    widen_otf(wide, masks, index, otf_refs)
 
     @pl.loop(0, pixels // tile)
     def _(step):
         q0 = pl.multiple_of(step * tile, tile)
         gathered = None
         for band in range(bands):
-            value = response(wide, whole_ref, q0, band, own_column, 1)[0]
+            value = response(wide, shift_ref, q0, band, own_column, 1)[0]
             value = value * value
             gathered = value * float(angles) if band == 0 else gathered + value
         power_ref[pl.ds(q0, tile), :] = jnp.concatenate(
@@ -379,6 +381,11 @@
         half_ref[here, :] = jnp.concatenate([real, -imag], axis=1).astype(jnp.bfloat16)
 
 
+def join_kernel(head_ref, tail_ref, out_ref):
+    out_ref[0] = head_ref[...]
+    out_ref[1:] = tail_ref[...]
+
+
 def pack_kernel(*refs):
     out_ref = refs[-1]
     for index, ref in enumerate(refs[:-1]):
@@ -431,55 +438,90 @@
     bands = 1 + angles * (len(MULTIPLES) - 1)
 
     mine = otf.reshape(slab, pixels).astype(jnp.bfloat16)
-    masks = list(range(0, devices, 2))
-    pieces = [mine] + [swap(mine, "row", mask) for mask in masks[1:]]
+    masks = list(range(0, devices, 4))
+    far = [swap(mine, "row", mask) for mask in masks[1:]]
+    across = swap(mine, "row", 2)
+    masks += [mask | 2 for mask in masks]
     masks += [mask | 1 for mask in masks]
 
     quarter = pixels // 4
     where = index.astype(jnp.int32).reshape(1)
-    whole = jnp.concatenate([offsets, phase_order], axis=1)
-    hbm = pl.BlockSpec(memory_space=pltpu.HBM)
+    longer = [(0, 0), (0, phases - angles)]
+    shifts = jnp.concatenate([jnp.pad(offsets.T, longer), phase_order], axis=0)
+    matrices = jnp.transpose(unmix, (1, 2, 0, 3))
     part = (bands, 2 * slab, quarter)
     left_shape = (pixels // LANES, 2 * LANES, 4 * slab)
-    send_away, send_near, keep_away, keep_near, cosine, sine, left = pl.pallas_call(
-        functools.partial(band_kernel, angles, phases),
-        out_shape=[jax.ShapeDtypeStruct(part, jnp.bfloat16)] * 4
+    spec, cosine, sine, left = pl.pallas_call(
+        functools.partial(spectra_kernel, slab),
+        out_shape=[jax.ShapeDtypeStruct((2, frames * slab, pixels), jnp.float32)]
         + [jax.ShapeDtypeStruct((pixels, pixels), jnp.bfloat16)] * 2
         + [jax.ShapeDtypeStruct(left_shape, jnp.bfloat16)],
-        in_specs=[smem()] * 3 + [hbm],
-        out_specs=[vmem()] * 7,
+        in_specs=[smem(), vmem()],
+        out_specs=[vmem()] * 4,
+        scratch_shapes=[pltpu.VMEM((2, pixels, LANES), jnp.float32)],
+        cost_estimate=pl.CostEstimate(
+            flops=4 * frames * slab * pixels * pixels,
+            bytes_accessed=12 << 20,
+            transcendentals=0,
+        ),
+        compiler_params=pltpu.CompilerParams(vmem_limit_bytes=20 << 20),
+        name="spectra",
+    )(where, raw.reshape(frames * slab, pixels))
+
+    def join(head, tail):
+        return pl.pallas_call(
+            join_kernel,
+            out_shape=jax.ShapeDtypeStruct((tail.shape[0] + 1, slab, pixels), jnp.bfloat16),
+            in_specs=[vmem()] * 2,
+            out_specs=vmem(),
+            compiler_params=pltpu.CompilerParams(vmem_limit_bytes=8 << 20),
+            cost_estimate=pl.CostEstimate(
+                flops=slab * pixels, bytes_accessed=2 << 20, transcendentals=0
+            ),
+            name="join",
+        )(head[0], tail)
+
+    def pack(parts):
+        return pl.pallas_call(
+            pack_kernel,
+            out_shape=jax.ShapeDtypeStruct((len(parts), slab, pixels), jnp.bfloat16),
+            in_specs=[vmem()] * len(parts),
+            out_specs=vmem(),
+            compiler_params=pltpu.CompilerParams(vmem_limit_bytes=8 << 20),
+            cost_estimate=pl.CostEstimate(
+                flops=len(parts) * slab * pixels, bytes_accessed=2 << 20, transcendentals=0
+            ),
+            name="pack",
+        )(*parts)
+
+    first = pack([mine] + far)
+    forwarded = swap(pack(far), "row", 2)
+    first_other = swap(first, "row", 1)
+
+    send_away, send_near, keep_away, keep_near = pl.pallas_call(
+        functools.partial(band_kernel, angles, phases),
+        out_shape=[jax.ShapeDtypeStruct(part, jnp.bfloat16)] * 4,
+        in_specs=[smem()] * 3 + [vmem()],
+        out_specs=[vmem()] * 4,
         scratch_shapes=[
-            pltpu.VMEM((frames * slab, pixels), jnp.bfloat16),
-            pltpu.VMEM((2, pixels, LANES), jnp.float32),
-            pltpu.VMEM((2, frames * slab, pixels), jnp.float32),
             pltpu.VMEM((2, pixels // LANES, GROUP, LANES), jnp.float32),
             pltpu.VMEM((2, pixels // LANES, GROUP, LANES), jnp.float32),
             pltpu.VMEM((bands - 1, 2, slab, LANES), jnp.float32),
-            pltpu.SemaphoreType.DMA,
         ],
         cost_estimate=pl.CostEstimate(
-            flops=8 * frames * slab * pixels * pixels,
+            flops=4 * frames * slab * pixels * pixels,
             bytes_accessed=12 << 20,
             transcendentals=0,
         ),
-        compiler_params=pltpu.CompilerParams(vmem_limit_bytes=18 << 20),
+        compiler_params=pltpu.CompilerParams(vmem_limit_bytes=14 << 20),
         name="bands",
-    )(where, whole, unmix, raw.reshape(frames * slab, pixels))
-
+    )(where, shifts, matrices, spec)
+
+    second = join([across], forwarded)
+    second_other = swap(second, "row", 1)
     got_away = swap(send_away, "row", 1)
-    own_pieces = pl.pallas_call(
-        pack_kernel,
-        out_shape=jax.ShapeDtypeStruct((chips, slab, pixels), jnp.bfloat16),
-        in_specs=[vmem()] * chips,
-        out_specs=vmem(),
-        compiler_params=pltpu.CompilerParams(vmem_limit_bytes=8 << 20),
-        cost_estimate=pl.CostEstimate(
-            flops=chips * slab * pixels, bytes_accessed=2 << 20, transcendentals=0
-        ),
-        name="pack",
-    )(*pieces)
-    other_pieces = swap(own_pieces, "row", 1)
     got_near = swap(send_near, "row", 1)
+    pieces = [first, second, first_other, second_other]
 
     half_shape = jax.ShapeDtypeStruct((chips // 4, pixels // 2, 2 * columns), jnp.bfloat16)
     wide_scratch = pltpu.VMEM((pixels // LANES, pixels + LANES, LANES), jnp.float32)
@@ -488,7 +530,7 @@
         return pl.pallas_call(
             functools.partial(numer_kernel, columns, tuple(masks), own),
             out_shape=[half_shape] * 4,
-            in_specs=[smem()] * 2 + [vmem()] * 7,
+            in_specs=[smem()] * 2 + [vmem()] * 9,
             out_specs=[vmem()] * 4,
             scratch_shapes=[
                 wide_scratch,
@@ -503,8 +545,7 @@
             ),
             compiler_params=pltpu.CompilerParams(vmem_limit_bytes=18 << 20),
         )(
-            where, whole, keep_away, got_away, keep_near, got_near, left, own_pieces,
-            other_pieces
+            where, shifts, keep_away, got_away, keep_near, got_near, left, *pieces
         )
 
     away = partial(False)
@@ -513,7 +554,7 @@
     power = pl.pallas_call(
         functools.partial(power_kernel, columns, bands, tuple(masks)),
         out_shape=jax.ShapeDtypeStruct((pixels, 2 * columns), jnp.float32),
-        in_specs=[smem()] * 2 + [vmem()] * 2 + [pl.BlockSpec(memory_space=pl.ANY)],
+        in_specs=[smem()] * 2 + [vmem()] * 4 + [pl.BlockSpec(memory_space=pl.ANY)],
         out_specs=vmem(),
         scratch_shapes=[wide_scratch],
         cost_estimate=pl.CostEstimate(
@@ -521,7 +562,7 @@
         ),
         compiler_params=pltpu.CompilerParams(vmem_limit_bytes=12 << 20),
         name="power",
-    )(where, whole, own_pieces, other_pieces, kept[0])
+    )(where, shifts, *pieces, kept[0])
 
     def fold(bit, parts):
         blocks, rows, lanes = parts[0].shape

time: 124 us -> 109 us (0.88)
  starting transfers between devices: 33.4 us -> 19.9 us
    ppermute x18 -> x17, starting transfers between devices: 31.9 us -> 18.3 us  [swap(): return lax.ppermute(value, axis, [(i, i ^ mask) for i in range(size)])]
    pallas_call x1, Pallas kernels: 18.3 us -> 11.7 us  [shards(): pl.pallas_call(functools.partial(band_kernel, angles, phases), out_shape=...]
    pallas_call x1 -> x4, Pallas kernels: 0.07 us -> 6.16 us  [the longest x1 6.06 us: shards(): pl.pallas_call(functools.partial(spectra_kernel, slab), out_shape=[jax.Sh...]
    ppermute x18 -> x17, waiting for transfers between devices: 22.5 us -> 22.7 us  [swap(): return lax.ppermute(value, axis, [(i, i ^ mask) for i in range(size)])]
  transfers between devices with their start and end apart: 19 -> 18, of which waited for: 9 -> 7; matrix products, arithmetic and copies ran while one was open for 2% -> 0% of each run, Pallas kernels for 29% -> 32%
where the time goes in v5:
time: 109 us
  Pallas kernels  48.6 us (45%)
  waiting for transfers between devices  23.7 us (22%)
  starting transfers between devices  19.9 us (18%)
  blocking collectives  13.7 us (13%)
  local copies, waits for them, and re-layouts  1.56 us (1%)
  other arithmetic  1.12 us (1%)
    ppermute x17, waiting for transfers between devices, swap(): return lax.ppermute(value, axis, [(i, i ^ mask) for i in range(size)])  22.7 us
    pallas_call x2, Pallas kernels, partial(): pl.pallas_call(functools.partial(numer_kernel, columns, tuple(masks), own...  21.7 us
    ppermute x17, starting transfers between devices, swap(): return lax.ppermute(value, axis, [(i, i ^ mask) for i in range(size)])  18.3 us
    all_to_all x1, blocking collectives, shards(): lax.all_to_all(half.reshape(devices, slab, 2 * columns), 'row', split_axi...  13.7 us
    pallas_call x1, Pallas kernels, shards(): pl.pallas_call(functools.partial(band_kernel, angles, phases), out_shape=...  11.7 us
    pallas_call x1, Pallas kernels, shards(): pl.pallas_call(functools.partial(spectra_kernel, slab), out_shape=[jax.Sh...  6.06 us
    pallas_call x1, Pallas kernels, shards(): pl.pallas_call(functools.partial(power_kernel, columns, bands, tuple(mask...  5.9 us
  transfers between devices with their start and end apart: 18, of which 7 were waited for; matrix products, arithmetic and copies ran while one was open for 0% of the time, Pallas kernels for 32%

profile of v5, /device:TPU:0, one launch (start us, length us, event | category | flops | bytes accessed | tf_op | source)
XLA Modules:
  0.0 108.8 jit_solution(7908571908070048667)
XLA Ops:
  0.0 1.0 convert_bitcast_fusion.refs_0_
  1.0 3.1 %collective-permute-start.2 = (bf16[64,1024]{1,0:T(8,128)(2,1)S(1)}, bf16[64,1024]{1,0:T(8,128)(2,1)S(1)}, u32[]{:S(2)}, u32[]{:S(2)}) collective-permute-start(bf16[64,1024]{1,0:T(8,128)(2,1)S(1)} %convert_bitcast_fusion.refs_0_), channel_id=1, source_target_pairs={{0,4},{1,5},{2,6},{3,7},{4,0},{5,1},{6,2},{7,3},{8,12},{9,13},{10,... | collective-permute-start | bytes 393224 | tf_op jit(solution)/shard_map/ppermute | solution.py:424
  4.1 2.6 %collective-permute-start.3 = (bf16[64,1024]{1,0:T(8,128)(2,1)S(1)}, bf16[64,1024]{1,0:T(8,128)(2,1)S(1)}, u32[]{:S(2)}, u32[]{:S(2)}) collective-permute-start(bf16[64,1024]{1,0:T(8,128)(2,1)S(1)} %convert_bitcast_fusion.refs_0_), channel_id=1, source_target_pairs={{0,8},{1,9},{2,10},{3,11},{4,12},{5,13},{6,14},{7,15},{8,0},{9,1},... | collective-permute-start | bytes 393224 | tf_op jit(solution)/shard_map/ppermute | solution.py:424
  6.7 0.0 collective-permute-start.4
  6.7 0.0 copy-start
  6.7 1.5 %copy-done = bf16[1,3,5,64,1024]{4,3,2,1,0:T(8,128)(2,1)S(1)} copy-done((bf16[1,3,5,64,1024]{4,3,2,1,0:T(8,128)(2,1)S(1)}, bf16[1,3,5,64,1024]{4,3,2,1,0:T(8,128)(2,1)}, u32[]{:S(2)}) %copy-start) | copy-done | bytes 1966104
  8.2 0.0 copy-start.2
  8.2 0.0 copy-start.3
  8.2 0.0 copy-start.1
  8.2 6.1 %spectra.1 = (f32[2,960,1024]{2,1,0:T(8,128)S(1)}, bf16[1024,1024]{1,0:T(8,128)(2,1)S(1)}, bf16[1024,1024]{1,0:T(8,128)(2,1)S(1)}, bf16[8,256,256]{2,1,0:T(8,128)(2,1)S(1)}) custom-call(s32[1]{0:T(128)} %bitcast.index_ref, bf16[960,1024]{1,0:T(8,128)(2,1)S(1)} %bitcast.9), custom_call_target="tpu_custom_call" | custom-call | flops 4026531840 | bytes 12582912 | tf_op jit(solution)/shard_map/spectra/pallas_call | solution.py:454
  14.3 0.0 copy-done.2
  14.3 0.0 copy-done.3
  14.3 0.0 collective-permute-done.2.refs_1_.refs_0_
  14.3 2.6 %collective-permute-done.3.refs_2_.refs_1_ = bf16[64,1024]{1,0:T(8,128)(2,1)S(1)} collective-permute-done((bf16[64,1024]{1,0:T(8,128)(2,1)S(1)}, bf16[64,1024]{1,0:T(8,128)(2,1)S(1)}, u32[]{:S(2)}, u32[]{:S(2)}) %collective-permute-start.3) | collective-permute-done | bytes 131104 | tf_op jit(solution)/shard_map/ppermute | solution.py:424
  17.0 0.0 collective-permute-done.4.refs_3_.refs_2_
  17.0 1.6 %collective-permute-start.6 = (bf16[3,64,1024]{2,1,0:T(8,128)(2,1)S(1)}, bf16[3,64,1024]{2,1,0:T(8,128)(2,1)S(1)}, u32[]{:S(2)}, u32[]{:S(2)}) collective-permute-start(bf16[3,64,1024]{2,1,0:T(8,128)(2,1)S(1)} %pack.3), channel_id=1, source_target_pairs={{0,2},{1,3},{2,0},{3,1},{4,6},{5,7},{6,4},{7,5},{8,10},{9,11},{10,... | collective-permute-start | bytes 1179656 | tf_op jit(solution)/shard_map/ppermute | solution.py:424
  18.6 0.0 copy-done.1
  18.6 11.7 %bands.1 = (bf16[13,128,256]{2,1,0:T(8,128)(2,1)S(1)}, bf16[13,128,256]{2,1,0:T(8,128)(2,1)S(1)}, bf16[13,128,256]{2,1,0:T(8,128)(2,1)S(1)}, bf16[13,128,256]{2,1,0:T(8,128)(2,1)S(1)}) custom-call(s32[1]{0:T(128)} %bitcast.index_ref, s32[5,5]{1,0:T(8,128)S(1)} %pad_add_fusion.shift_ref, f32[3,5,2,5]{3,2,1,0:T(2,128)S(1)} %bitcast.10, ...), custom_call_target="tpu_custom_call" | custom-call | flops 4026531840 | bytes 12582912 | tf_op jit(solution)/shard_map/bands/pallas_call | solution.py:501
  30.3 0.1 collective-permute-start
  30.4 0.5 collective-permute-start.1
  30.9 0.5 collective-permute-start.5
  31.4 0.1 collective-permute-start.7
  31.5 4.9 %collective-permute-done.5.head_ref = bf16[64,1024]{1,0:T(8,128)(2,1)S(1)} collective-permute-done((bf16[64,1024]{1,0:T(8,128)(2,1)S(1)}, bf16[64,1024]{1,0:T(8,128)(2,1)S(1)}, u32[]{:S(2)}, u32[]{:S(2)}) %collective-permute-start.5) | collective-permute-done | bytes 131104 | tf_op jit(solution)/shard_map/ppermute | solution.py:424
  36.4 0.0 collective-permute-done.6.tail_ref
  36.4 0.1 collective-permute-start.8
  36.5 0.0 collective-permute-done.7.rest_2_
  36.5 0.0 collective-permute-done.got_away
  36.5 0.0 collective-permute-done.1.got_near
  36.5 1.9 %collective-permute-done.8.rest_3_ = bf16[4,64,1024]{2,1,0:T(8,128)(2,1)S(1)} collective-permute-done((bf16[4,64,1024]{2,1,0:T(8,128)(2,1)S(1)}, bf16[4,64,1024]{2,1,0:T(8,128)(2,1)S(1)}, u32[]{:S(2)}, u32[]{:S(2)}) %collective-permute-start.8) | collective-permute-done | bytes 524320 | tf_op jit(solution)/shard_map/ppermute | solution.py:424
  38.4 10.9 %shard_map.55 = (bf16[2,512,128]{2,1,0:T(8,128)(2,1)S(1)}, bf16[2,512,128]{2,1,0:T(8,128)(2,1)S(1)}, bf16[2,512,128]{2,1,0:T(8,128)(2,1)S(1)}, bf16[2,512,128]{2,1,0:T(8,128)(2,1)S(1)}) custom-call(s32[1]{0:T(128)} %bitcast.index_ref, s32[5,5]{1,0:T(8,128)S(1)} %pad_add_fusion.shift_ref, bf16[13,128,256]{2,1,0:T(8,128)(2,1)S(1)} %get-tuple-element.26.keep_away, ...), custom_call_target="tpu_custom_call" | custom-call | flops 3489660928 | bytes 8388608 | tf_op jit(solution)/shard_map/pallas_call | solution.py:530
  49.2 0.6 collective-permute-start.9
  49.8 1.5 %collective-permute-start.10 = (bf16[2,512,128]{2,1,0:T(8,128)(2,1)S(1)}, bf16[2,512,128]{2,1,0:T(8,128)(2,1)S(1)}, u32[]{:S(2)}, u32[]{:S(2)}) collective-permute-start(bf16[2,512,128]{2,1,0:T(8,128)(2,1)S(1)} %get-tuple-element.33), channel_id=1, source_target_pairs={{0,2},{1,3},{2,0},{3,1},{4,6},{5,7},{6,4},{7,5},{8,10},{9,11},{10,... | collective-permute-start | bytes 786440 | tf_op jit(solution)/shard_map/ppermute | solution.py:424
  51.3 2.0 %collective-permute-start.13 = (bf16[2,512,128]{2,1,0:T(8,128)(2,1)S(1)}, bf16[2,512,128]{2,1,0:T(8,128)(2,1)S(1)}, u32[]{:S(2)}, u32[]{:S(2)}) collective-permute-start(bf16[2,512,128]{2,1,0:T(8,128)(2,1)S(1)} %get-tuple-element.37), channel_id=1, source_target_pairs={{0,4},{1,5},{2,6},{3,7},{4,0},{5,1},{6,2},{7,3},{8,12},{9,13},{10,... | collective-permute-start | bytes 786440 | tf_op jit(solution)/shard_map/ppermute | solution.py:424
  53.3 0.0 collective-permute-start.14
  53.4 10.8 %shard_map.56 = (bf16[2,512,128]{2,1,0:T(8,128)(2,1)S(1)}, bf16[2,512,128]{2,1,0:T(8,128)(2,1)S(1)}, bf16[2,512,128]{2,1,0:T(8,128)(2,1)S(1)}, bf16[2,512,128]{2,1,0:T(8,128)(2,1)S(1)}) custom-call(s32[1]{0:T(128)} %bitcast.index_ref, s32[5,5]{1,0:T(8,128)S(1)} %pad_add_fusion.shift_ref, bf16[13,128,256]{2,1,0:T(8,128)(2,1)S(1)} %get-tuple-element.26.keep_away, ...), custom_call_target="tpu_custom_call" | custom-call | flops 3489660928 | bytes 8388608 | tf_op jit(solution)/shard_map/pallas_call | solution.py:530
  64.2 5.9 %power.1.refs_4_ = f32[1024,128]{1,0:T(8,128)S(1)} custom-call(s32[1]{0:T(128)} %bitcast.index_ref, s32[5,5]{1,0:T(8,128)S(1)} %pad_add_fusion.shift_ref, bf16[4,64,1024]{2,1,0:T(8,128)(2,1)S(1)} %pack.2.rest_0_, bf16[4,64,1024]{2,1,0:T(8,128)(2,1)S(1)} %join.1.rest_1_, bf16[4,64,1024]{2,1,0:T(8,128)(2,1)S(1)} %collective-permute-done.7.rest_2_, ...), custom_call_target="tpu_custom_call" | custom-call | flops 1048576000 | bytes 5242880 | tf_op jit(solution)/shard_map/power/pallas_call | solution.py:554
  70.1 1.6 %collective-permute-start.17 = (f32[1024,128]{1,0:T(8,128)S(1)}, f32[1024,128]{1,0:T(8,128)S(1)}, u32[]{:S(2)}, u32[]{:S(2)}) collective-permute-start(f32[1024,128]{1,0:T(8,128)S(1)} %power.1.refs_4_), channel_id=1, source_target_pairs={{0,16},{16,0},{1,17},{17,1},{2,18},{18,2},{3,19},{19,3},{4,20},{20... | collective-permute-start | bytes 1572872 | tf_op jit(solution)/shard_map/ppermute | solution.py:602
  71.7 0.0 collective-permute-done.10
  71.7 0.1 add_convert_fusion.1
  71.7 2.1 %collective-permute-start.11 = (bf16[2,512,128]{2,1,0:T(8,128)(2,1)S(1)}, bf16[2,512,128]{2,1,0:T(8,128)(2,1)S(1)}, u32[]{:S(2)}, u32[]{:S(2)}) collective-permute-start(bf16[2,512,128]{2,1,0:T(8,128)(2,1)S(1)} %add_convert_fusion.1), channel_id=1, source_target_pairs={{0,4},{1,5},{2,6},{3,7},{4,0},{5,1},{6,2},{7,3},{8,12},{9,13},{10,... | collective-permute-start | bytes 786440 | tf_op jit(solution)/shard_map/ppermute | solution.py:424
  73.8 0.0 collective-permute-done.14
  73.8 0.1 add_convert_fusion
  73.9 0.6 collective-permute-start.15
  74.5 0.0 collective-permute-done.9.refs_0_
  74.5 4.6 %collective-permute-done.11.refs_2_ = bf16[2,512,128]{2,1,0:T(8,128)(2,1)S(1)} collective-permute-done((bf16[2,512,128]{2,1,0:T(8,128)(2,1)S(1)}, bf16[2,512,128]{2,1,0:T(8,128)(2,1)S(1)}, u32[]{:S(2)}, u32[]{:S(2)}) %collective-permute-start.11) | collective-permute-done | bytes 262176 | tf_op jit(solution)/shard_map/ppermute | solution.py:424
  79.0 0.1 fold.2
  79.1 2.8 %collective-permute-start.12 = (bf16[1,512,128]{2,1,0:T(8,128)(2,1)S(1)}, bf16[1,512,128]{2,1,0:T(8,128)(2,1)S(1)}, u32[]{:S(2)}, u32[]{:S(2)}) collective-permute-start(bf16[1,512,128]{2,1,0:T(8,128)(2,1)S(1)} %get-tuple-element.36), channel_id=1, source_target_pairs={{0,8},{1,9},{2,10},{3,11},{4,12},{5,13},{6,14},{7,15},{8,0},{9,1},... | collective-permute-start | bytes 393224 | tf_op jit(solution)/shard_map/ppermute | solution.py:424
  81.9 0.0 collective-permute-done.13.refs_0_
  81.9 0.0 collective-permute-done.15.refs_2_
  81.9 0.1 fold.3
  82.0 0.3 collective-permute-start.16
  82.3 1.0 collective-permute-done.17.refs_5_
  83.3 6.9 %collective-permute-done.12.refs_1_ = bf16[1,512,128]{2,1,0:T(8,128)(2,1)S(1)} collective-permute-done((bf16[1,512,128]{2,1,0:T(8,128)(2,1)S(1)}, bf16[1,512,128]{2,1,0:T(8,128)(2,1)S(1)}, u32[]{:S(2)}, u32[]{:S(2)}) %collective-permute-start.12) | collective-permute-done | bytes 131104 | tf_op jit(solution)/shard_map/ppermute | solution.py:424
  90.2 1.8 %collective-permute-done.16.refs_3_ = bf16[1,512,128]{2,1,0:T(8,128)(2,1)S(1)} collective-permute-done((bf16[1,512,128]{2,1,0:T(8,128)(2,1)S(1)}, bf16[1,512,128]{2,1,0:T(8,128)(2,1)S(1)}, u32[]{:S(2)}, u32[]{:S(2)}) %collective-permute-start.16) | collective-permute-done | bytes 131104 | tf_op jit(solution)/shard_map/ppermute | solution.py:424
  92.1 1.5 %inverse.1 = bf16[1024,128]{1,0:T(8,128)(2,1)S(1)} custom-call(f32[1,512,128]{2,1,0:T(8,128)S(1)} %get-tuple-element.35.refs_0_, bf16[1,512,128]{2,1,0:T(8,128)(2,1)S(1)} %collective-permute-done.12.refs_1_, f32[1,512,128]{2,1,0:T(8,128)S(1)} %get-tuple-element.41.refs_2_, bf16[1,512,128]{2,1,0:T(8,128)(2,1)S(1)} %collective-permute-done.16.refs_3_, ...), custom_call_target="tpu_custom_call" | custom-call | flops 536870912 | bytes 6291456 | tf_op jit(solution)/shard_map/inverse/pallas_call | solution.py:605
  93.5 13.7 %all_to_all.5.back_ref = bf16[16,64,128]{2,1,0:T(8,128)(2,1)S(1)} all-to-all(bf16[16,64,128]{2,1,0:T(8,128)(2,1)S(1)} %bitcast.8), channel_id=1, replica_groups=mesh['cuts'=2,'row'=16] {'row'}, dimensions={0} | all-to-all | bytes 524288 | tf_op jit(solution)/shard_map/all_to_all | solution.py:617
  107.2 1.6 %image.1 = f32[64,1024]{1,0:T(8,128)} custom-call(bf16[16,64,128]{2,1,0:T(8,128)(2,1)S(1)} %all_to_all.5.back_ref, bf16[1024,1024]{1,0:T(8,128)(2,1)S(1)} %get-tuple-element.43.refs_6_.cos_ref, bf16[1024,1024]{1,0:T(8,128)(2,1)S(1)} %get-tuple-element.44.refs_7_.sin_ref), custom_call_target="tpu_custom_call" | custom-call | flops 268435456 | bytes 6291456 | tf_op jit(solution)/shard_map/image/pallas_call | solution.py:620
  (4 shorter events, 0.1 us)
Async XLA Ops:
  1.0 13.4 %collective-permute-start.2 = (bf16[64,1024]{1,0:T(8,128)(2,1)S(1)}, bf16[64,1024]{1,0:T(8,128)(2,1)S(1)}, u32[]{:S(2)}, u32[]{:S(2)}) collective-permute-start(bf16[64,1024]{1,0:T(8,128)(2,1)S(1)} %convert_bitcast_fusion.refs_0_), channel_id=1, source_target_pairs={{0,4},{1,5},{2,6},{3,7},{4,0},{5,1},{6,2},{7,3},{8,12},{9,13},{10,... | collective-permute-start | bytes 393224 | tf_op jit(solution)/shard_map/ppermute | solution.py:424
  4.1 12.9 %collective-permute-start.3 = (bf16[64,1024]{1,0:T(8,128)(2,1)S(1)}, bf16[64,1024]{1,0:T(8,128)(2,1)S(1)}, u32[]{:S(2)}, u32[]{:S(2)}) collective-permute-start(bf16[64,1024]{1,0:T(8,128)(2,1)S(1)} %convert_bitcast_fusion.refs_0_), channel_id=1, source_target_pairs={{0,8},{1,9},{2,10},{3,11},{4,12},{5,13},{6,14},{7,15},{8,0},{9,1},... | collective-permute-start | bytes 393224 | tf_op jit(solution)/shard_map/ppermute | solution.py:424
  6.7 10.3 %collective-permute-start.4 = (bf16[64,1024]{1,0:T(8,128)(2,1)S(1)}, bf16[64,1024]{1,0:T(8,128)(2,1)S(1)}, u32[]{:S(2)}, u32[]{:S(2)}) collective-permute-start(bf16[64,1024]{1,0:T(8,128)(2,1)S(1)} %convert_bitcast_fusion.refs_0_), channel_id=1, source_target_pairs={{0,12},{1,13},{2,14},{3,15},{4,8},{5,9},{6,10},{7,11},{8,4},{9,5},... | collective-permute-start | bytes 393224 | tf_op jit(solution)/shard_map/ppermute | solution.py:424
  6.7 1.5 %copy-start = (bf16[1,3,5,64,1024]{4,3,2,1,0:T(8,128)(2,1)S(1)}, bf16[1,3,5,64,1024]{4,3,2,1,0:T(8,128)(2,1)}, u32[]{:S(2)}) copy-start(bf16[1,3,5,64,1024]{4,3,2,1,0:T(8,128)(2,1)} %param.5) | copy-start | bytes 5898244
  8.2 6.1 %copy-start.2 = (s32[3,5]{1,0:T(4,128)S(1)}, s32[3,5]{1,0:T(4,128)}, u32[]{:S(2)}) copy-start(s32[3,5]{1,0:T(4,128)} %param.8) | copy-start | bytes 184
  8.2 6.1 %copy-start.3 = (s32[3,2]{0,1:T(2,128)S(1)}, s32[3,2]{0,1:T(2,128)}, u32[]{:S(2)}) copy-start(s32[3,2]{0,1:T(2,128)} %param.7) | copy-start | bytes 76
  8.2 10.4 %copy-start.1 = (f32[2,3,5,5]{3,0,2,1:T(2,128)S(1)}, f32[2,3,5,5]{3,0,2,1:T(2,128)}, u32[]{:S(2)}) copy-start(f32[2,3,5,5]{3,0,2,1:T(2,128)} %param.9) | copy-start | bytes 1804
  17.0 19.4 %collective-permute-start.6 = (bf16[3,64,1024]{2,1,0:T(8,128)(2,1)S(1)}, bf16[3,64,1024]{2,1,0:T(8,128)(2,1)S(1)}, u32[]{:S(2)}, u32[]{:S(2)}) collective-permute-start(bf16[3,64,1024]{2,1,0:T(8,128)(2,1)S(1)} %pack.3), channel_id=1, source_target_pairs={{0,2},{1,3},{2,0},{3,1},{4,6},{5,7},{6,4},{7,5},{8,10},{9,11},{10,... | collective-permute-start | bytes 1179656 | tf_op jit(solution)/shard_map/ppermute | solution.py:424
  30.3 6.2 %collective-permute-start = (bf16[13,128,256]{2,1,0:T(8,128)(2,1)S(1)}, bf16[13,128,256]{2,1,0:T(8,128)(2,1)S(1)}, u32[]{:S(2)}, u32[]{:S(2)}) collective-permute-start(bf16[13,128,256]{2,1,0:T(8,128)(2,1)S(1)} %get-tuple-element.27), channel_id=1, source_target_pairs={{0,1},{1,0},{2,3},{3,2},{4,5},{5,4},{6,7},{7,6},{8,9},{9,8},{10,11... | collective-permute-start | bytes 2555912 | tf_op jit(solution)/shard_map/ppermute | solution.py:424
  30.4 6.1 %collective-permute-start.1 = (bf16[13,128,256]{2,1,0:T(8,128)(2,1)S(1)}, bf16[13,128,256]{2,1,0:T(8,128)(2,1)S(1)}, u32[]{:S(2)}, u32[]{:S(2)}) collective-permute-start(bf16[13,128,256]{2,1,0:T(8,128)(2,1)S(1)} %get-tuple-element.29), channel_id=1, source_target_pairs={{0,1},{1,0},{2,3},{3,2},{4,5},{5,4},{6,7},{7,6},{8,9},{9,8},{10,11... | collective-permute-start | bytes 2555912 | tf_op jit(solution)/shard_map/ppermute | solution.py:424
  30.9 5.5 %collective-permute-start.5 = (bf16[64,1024]{1,0:T(8,128)(2,1)S(1)}, bf16[64,1024]{1,0:T(8,128)(2,1)S(1)}, u32[]{:S(2)}, u32[]{:S(2)}) collective-permute-start(bf16[64,1024]{1,0:T(8,128)(2,1)S(1)} %convert_bitcast_fusion.refs_0_), channel_id=1, source_target_pairs={{0,2},{1,3},{2,0},{3,1},{4,6},{5,7},{6,4},{7,5},{8,10},{9,11},{10,... | collective-permute-start | bytes 393224 | tf_op jit(solution)/shard_map/ppermute | solution.py:424
  31.4 5.1 %collective-permute-start.7 = (bf16[4,64,1024]{2,1,0:T(8,128)(2,1)S(1)}, bf16[4,64,1024]{2,1,0:T(8,128)(2,1)S(1)}, u32[]{:S(2)}, u32[]{:S(2)}) collective-permute-start(bf16[4,64,1024]{2,1,0:T(8,128)(2,1)S(1)} %pack.2.rest_0_), channel_id=1, source_target_pairs={{0,1},{1,0},{2,3},{3,2},{4,5},{5,4},{6,7},{7,6},{8,9},{9,8},{10,11... | collective-permute-start | bytes 1572872 | tf_op jit(solution)/shard_map/ppermute | solution.py:424
  36.4 2.0 %collective-permute-start.8 = (bf16[4,64,1024]{2,1,0:T(8,128)(2,1)S(1)}, bf16[4,64,1024]{2,1,0:T(8,128)(2,1)S(1)}, u32[]{:S(2)}, u32[]{:S(2)}) collective-permute-start(bf16[4,64,1024]{2,1,0:T(8,128)(2,1)S(1)} %join.1.rest_1_), channel_id=1, source_target_pairs={{0,1},{1,0},{2,3},{3,2},{4,5},{5,4},{6,7},{7,6},{8,9},{9,8},{10,11... | collective-permute-start | bytes 1572872 | tf_op jit(solution)/shard_map/ppermute | solution.py:424
  49.2 25.2 %collective-permute-start.9 = (bf16[2,512,128]{2,1,0:T(8,128)(2,1)S(1)}, bf16[2,512,128]{2,1,0:T(8,128)(2,1)S(1)}, u32[]{:S(2)}, u32[]{:S(2)}) collective-permute-start(bf16[2,512,128]{2,1,0:T(8,128)(2,1)S(1)} %get-tuple-element.31), channel_id=1, source_target_pairs={{0,2},{1,3},{2,0},{3,1},{4,6},{5,7},{6,4},{7,5},{8,10},{9,11},{10,... | collective-permute-start | bytes 786440 | tf_op jit(solution)/shard_map/ppermute | solution.py:424
  49.8 21.8 %collective-permute-start.10 = (bf16[2,512,128]{2,1,0:T(8,128)(2,1)S(1)}, bf16[2,512,128]{2,1,0:T(8,128)(2,1)S(1)}, u32[]{:S(2)}, u32[]{:S(2)}) collective-permute-start(bf16[2,512,128]{2,1,0:T(8,128)(2,1)S(1)} %get-tuple-element.33), channel_id=1, source_target_pairs={{0,2},{1,3},{2,0},{3,1},{4,6},{5,7},{6,4},{7,5},{8,10},{9,11},{10,... | collective-permute-start | bytes 786440 | tf_op jit(solution)/shard_map/ppermute | solution.py:424
  51.3 30.6 %collective-permute-start.13 = (bf16[2,512,128]{2,1,0:T(8,128)(2,1)S(1)}, bf16[2,512,128]{2,1,0:T(8,128)(2,1)S(1)}, u32[]{:S(2)}, u32[]{:S(2)}) collective-permute-start(bf16[2,512,128]{2,1,0:T(8,128)(2,1)S(1)} %get-tuple-element.37), channel_id=1, source_target_pairs={{0,4},{1,5},{2,6},{3,7},{4,0},{5,1},{6,2},{7,3},{8,12},{9,13},{10,... | collective-permute-start | bytes 786440 | tf_op jit(solution)/shard_map/ppermute | solution.py:424
  53.3 20.5 %collective-permute-start.14 = (bf16[2,512,128]{2,1,0:T(8,128)(2,1)S(1)}, bf16[2,512,128]{2,1,0:T(8,128)(2,1)S(1)}, u32[]{:S(2)}, u32[]{:S(2)}) collective-permute-start(bf16[2,512,128]{2,1,0:T(8,128)(2,1)S(1)} %get-tuple-element.39), channel_id=1, source_target_pairs={{0,4},{1,5},{2,6},{3,7},{4,0},{5,1},{6,2},{7,3},{8,12},{9,13},{10,... | collective-permute-start | bytes 786440 | tf_op jit(solution)/shard_map/ppermute | solution.py:424
  70.1 13.2 %collective-permute-start.17 = (f32[1024,128]{1,0:T(8,128)S(1)}, f32[1024,128]{1,0:T(8,128)S(1)}, u32[]{:S(2)}, u32[]{:S(2)}) collective-permute-start(f32[1024,128]{1,0:T(8,128)S(1)} %power.1.refs_4_), channel_id=1, source_target_pairs={{0,16},{16,0},{1,17},{17,1},{2,18},{18,2},{3,19},{19,3},{4,20},{20... | collective-permute-start | bytes 1572872 | tf_op jit(solution)/shard_map/ppermute | solution.py:602
  71.7 7.3 %collective-permute-start.11 = (bf16[2,512,128]{2,1,0:T(8,128)(2,1)S(1)}, bf16[2,512,128]{2,1,0:T(8,128)(2,1)S(1)}, u32[]{:S(2)}, u32[]{:S(2)}) collective-permute-start(bf16[2,512,128]{2,1,0:T(8,128)(2,1)S(1)} %add_convert_fusion.1), channel_id=1, source_target_pairs={{0,4},{1,5},{2,6},{3,7},{4,0},{5,1},{6,2},{7,3},{8,12},{9,13},{10,... | collective-permute-start | bytes 786440 | tf_op jit(solution)/shard_map/ppermute | solution.py:424
  73.9 8.0 %collective-permute-start.15 = (bf16[2,512,128]{2,1,0:T(8,128)(2,1)S(1)}, bf16[2,512,128]{2,1,0:T(8,128)(2,1)S(1)}, u32[]{:S(2)}, u32[]{:S(2)}) collective-permute-start(bf16[2,512,128]{2,1,0:T(8,128)(2,1)S(1)} %add_convert_fusion), channel_id=1, source_target_pairs={{0,2},{1,3},{2,0},{3,1},{4,6},{5,7},{6,4},{7,5},{8,10},{9,11},{10,... | collective-permute-start | bytes 786440 | tf_op jit(solution)/shard_map/ppermute | solution.py:424
  79.1 11.1 %collective-permute-start.12 = (bf16[1,512,128]{2,1,0:T(8,128)(2,1)S(1)}, bf16[1,512,128]{2,1,0:T(8,128)(2,1)S(1)}, u32[]{:S(2)}, u32[]{:S(2)}) collective-permute-start(bf16[1,512,128]{2,1,0:T(8,128)(2,1)S(1)} %get-tuple-element.36), channel_id=1, source_target_pairs={{0,8},{1,9},{2,10},{3,11},{4,12},{5,13},{6,14},{7,15},{8,0},{9,1},... | collective-permute-start | bytes 393224 | tf_op jit(solution)/shard_map/ppermute | solution.py:424
  82.0 10.0 %collective-permute-start.16 = (bf16[1,512,128]{2,1,0:T(8,128)(2,1)S(1)}, bf16[1,512,128]{2,1,0:T(8,128)(2,1)S(1)}, u32[]{:S(2)}, u32[]{:S(2)}) collective-permute-start(bf16[1,512,128]{2,1,0:T(8,128)(2,1)S(1)} %get-tuple-element.42), channel_id=1, source_target_pairs={{0,8},{1,9},{2,10},{3,11},{4,12},{5,13},{6,14},{7,15},{8,0},{9,1},... | collective-permute-start | bytes 393224 | tf_op jit(solution)/shard_map/ppermute | solution.py:424

commit v6 on v5

--- a/solution.py
+++ b/solution.py
@@ -26,7 +26,9 @@
     return cosine, sine * angle
 
 
-def spectra_kernel(slab, index_ref, raw_ref, spec, cos_ref, sin_ref, left_ref, low):
+def spectra_kernel(slab, index_ref, raw_hbm, spec, cos_ref, sin_ref, left_ref, low, raw_ref, sem):
+    fetch = pltpu.make_async_copy(raw_hbm, raw_ref, sem)
+    fetch.start()
     pixels = raw_ref.shape[1]
     tile = 256
     chip = index_ref[0] >> 1
@@ -63,6 +65,7 @@
     per_tile = tile // LANES
     for tab in range(per_tile):
         build(tab)
+    fetch.wait()
     for step in range(pixels // tile):
         cut = slice(step * tile, (step + 1) * tile)
         spec[0, :, cut] = jnp.dot(raw_ref[...], cos_ref[:, cut], preferred_element_type=jnp.float32)
@@ -89,11 +92,9 @@
         left_ref[step, LANES:, pair:] = mine[0]
 
 
-def band_kernel(
-    angles, phases, index_ref, shift_ref, unmix_ref, spec, *rest
-):
-    parts = rest[:4]
-    turned_even, turned_odd, phase = rest[4:]
+def plain_kernel(angles, phases, index_ref, shift_ref, unmix_ref, spec, phase, *rest):
+    outs = rest[:4]
+    held = rest[4]
     frames = angles * phases
     slab = spec.shape[1] // frames
     pixels = spec.shape[2]
@@ -102,6 +103,7 @@
     index = index_ref[0]
     core = index & 1
     near = (index >> 1) & 1
+    quarter_tiles = lane_tiles // 4
 
     def offset(which, axis):
         return shift_ref[axis, which]
@@ -114,6 +116,62 @@
             cosine, sine = turn_of(around.astype(jnp.float32) * (2.0 * math.pi / pixels))
             phase[which * others + m - 1, 0] = cosine
             phase[which * others + m - 1, 1] = sine
+
+    @pl.loop(0, slab // GROUP)
+    def _(step):
+        rows = step * GROUP
+        terms = []
+        for which in range(angles):
+            for j in range(phases):
+                column = shift_ref[2 + which, j]
+                here = pl.ds(
+                    pl.multiple_of((which * phases + j) * slab + rows, GROUP), GROUP
+                )
+                terms.append(
+                    (here, unmix_ref[which, 0, 0, column], unmix_ref[which, 0, 1, column])
+                )
+        for tab in range(lane_tiles):
+            cut = slice(tab * LANES, (tab + 1) * LANES)
+            real = imag = None
+            for here, weight_re, weight_im in terms:
+                cosine_sum = spec[0, here, cut]
+                sine_sum = spec[1, here, cut]
+                add_re = weight_re * cosine_sum + weight_im * sine_sum
+                add_im = weight_im * cosine_sum - weight_re * sine_sum
+                real = add_re if real is None else real + add_re
+                imag = add_im if imag is None else imag + add_im
+            held[0, tab] = real
+            held[1, tab] = imag
+        for which, out in enumerate(outs):
+            side = (1 - core) if which < 2 else core
+            half = (1 - near) if which % 2 == 0 else near
+            first = (2 * side + half) * quarter_tiles
+            for part in range(2):
+                put = pl.ds(pl.multiple_of(part * slab + rows, GROUP), GROUP)
+                for i in range(quarter_tiles):
+                    out[put, i * LANES : (i + 1) * LANES] = held[part, first + i].astype(
+                        jnp.bfloat16
+                    )
+
+
+def band_kernel(
+    angles, phases, index_ref, shift_ref, unmix_ref, spec, *rest
+):
+    phase = rest[0]
+    plain = rest[1:5]
+    parts = rest[5:9]
+    turned_even, turned_odd = rest[9:]
+    frames = angles * phases
+    slab = spec.shape[1] // frames
+    pixels = spec.shape[2]
+    lane_tiles = pixels // LANES
+    others = len(MULTIPLES) - 1
+    index = index_ref[0]
+    core = index & 1
+    near = (index >> 1) & 1
+
+    def offset(which, axis):
+        return shift_ref[axis, which]
 
     lane = lax.broadcasted_iota(jnp.int32, (GROUP, LANES), 1)
     quarter_tiles = lane_tiles // 4
@@ -181,25 +239,26 @@
         mult = jnp.where(m <= 2, 1, 2) * jnp.where(m % 2 == 1, 1, -1)
         return jnp.where(band == 0, 0, mult * offset(which, 1))
 
+    count = angles * others
+    for ref, out in zip(plain, parts):
+        out[0] = ref[...]
+
     @pl.loop(0, slab // GROUP)
     def _(step):
         rows = step * GROUP
-        terms = [
-            (which * phases + j, *weight(which, 0, j))
-            for which in range(angles)
-            for j in range(phases)
-        ]
-        combine(terms, rows, turned_even)
-
-        @pl.loop(0, angles * others // 2)
+        combine(terms_of(0, rows), rows, turned_odd)
+
+        @pl.loop(0, count // 2 - 1)
         def _(pair_index):
-            band = 2 * pair_index
-            combine(terms_of(band, rows), rows, turned_odd)
-            put_out(band, rows, turned_even, shift_of(band))
-            combine(terms_of(band + 1, rows), rows, turned_even)
-            put_out(band + 1, rows, turned_odd, shift_of(band + 1))
-
-        put_out(angles * others, rows, turned_even, shift_of(angles * others))
+            band = 2 * pair_index + 1
+            combine(terms_of(band, rows), rows, turned_even)
+            put_out(band, rows, turned_odd, shift_of(band))
+            combine(terms_of(band + 1, rows), rows, turned_odd)
+            put_out(band + 1, rows, turned_even, shift_of(band + 1))
+
+        combine(terms_of(count - 1, rows), rows, turned_even)
+        put_out(count - 1, rows, turned_odd, shift_of(count - 1))
+        put_out(count, rows, turned_even, shift_of(count))
 
 
 def shift_by(shift_ref, band, axis):
@@ -456,9 +515,13 @@
         out_shape=[jax.ShapeDtypeStruct((2, frames * slab, pixels), jnp.float32)]
         + [jax.ShapeDtypeStruct((pixels, pixels), jnp.bfloat16)] * 2
         + [jax.ShapeDtypeStruct(left_shape, jnp.bfloat16)],
-        in_specs=[smem(), vmem()],
+        in_specs=[smem(), pl.BlockSpec(memory_space=pltpu.HBM)],
         out_specs=[vmem()] * 4,
-        scratch_shapes=[pltpu.VMEM((2, pixels, LANES), jnp.float32)],
+        scratch_shapes=[
+            pltpu.VMEM((2, pixels, LANES), jnp.float32),
+            pltpu.VMEM((frames * slab, pixels), jnp.bfloat16),
+            pltpu.SemaphoreType.DMA,
+        ],
         cost_estimate=pl.CostEstimate(
             flops=4 * frames * slab * pixels * pixels,
             bytes_accessed=12 << 20,
@@ -466,7 +529,7 @@
         ),
         compiler_params=pltpu.CompilerParams(vmem_limit_bytes=20 << 20),
         name="spectra",
-    )(where, raw.reshape(frames * slab, pixels))
+    )(where, pltpu.with_memory_space_constraint(raw.reshape(frames * slab, pixels), pltpu.HBM))
 
     def join(head, tail):
         return pl.pallas_call(
@@ -494,6 +557,22 @@
             name="pack",
         )(*parts)
 
+    phase, *plain = pl.pallas_call(
+        functools.partial(plain_kernel, angles, phases),
+        out_shape=[jax.ShapeDtypeStruct((bands - 1, 2, slab, LANES), jnp.float32)]
+        + [jax.ShapeDtypeStruct(part[1:], jnp.bfloat16)] * 4,
+        in_specs=[smem()] * 3 + [vmem()],
+        out_specs=[vmem()] * 5,
+        scratch_shapes=[pltpu.VMEM((2, pixels // LANES, GROUP, LANES), jnp.float32)],
+        cost_estimate=pl.CostEstimate(
+            flops=frames * slab * pixels * pixels,
+            bytes_accessed=8 << 20,
+            transcendentals=0,
+        ),
+        compiler_params=pltpu.CompilerParams(vmem_limit_bytes=12 << 20),
+        name="plain",
+    )(where, shifts, matrices, spec)
+
     first = pack([mine] + far)
     forwarded = swap(pack(far), "row", 2)
     first_other = swap(first, "row", 1)
@@ -501,12 +580,11 @@
     send_away, send_near, keep_away, keep_near = pl.pallas_call(
         functools.partial(band_kernel, angles, phases),
         out_shape=[jax.ShapeDtypeStruct(part, jnp.bfloat16)] * 4,
-        in_specs=[smem()] * 3 + [vmem()],
+        in_specs=[smem()] * 3 + [vmem()] * 6,
         out_specs=[vmem()] * 4,
         scratch_shapes=[
             pltpu.VMEM((2, pixels // LANES, GROUP, LANES), jnp.float32),
             pltpu.VMEM((2, pixels // LANES, GROUP, LANES), jnp.float32),
-            pltpu.VMEM((bands - 1, 2, slab, LANES), jnp.float32),
         ],
         cost_estimate=pl.CostEstimate(
             flops=4 * frames * slab * pixels * pixels,
@@ -515,7 +593,7 @@
         ),
         compiler_params=pltpu.CompilerParams(vmem_limit_bytes=14 << 20),
         name="bands",
-    )(where, shifts, matrices, spec)
+    )(where, shifts, matrices, spec, phase, *plain)
 
     second = join([across], forwarded)
     second_other = swap(second, "row", 1)

time: 109 us -> 112 us (1.028)
  waiting for transfers between devices: 23.7 us -> 26.6 us
  local copies, waits for them, and re-layouts: 1.56 us -> 0.01 us
    ppermute x17, waiting for transfers between devices: 22.7 us -> 26.6 us  [swap(): return lax.ppermute(value, axis, [(i, i ^ mask) for i in range(size)])]
    pallas_call x0 -> x1, Pallas kernels: none -> 2.75 us  [shards(): pl.pallas_call(functools.partial(plain_kernel, angles, phases), out_shape...]
    pallas_call x1, Pallas kernels: 11.7 us -> 9 us  [shards(): pl.pallas_call(functools.partial(band_kernel, angles, phases), out_shape=...]
    unnamed x8 -> x6, local copies, waits for them, and re-layouts: 1.56 us -> 0.01 us
where the time goes in v6:
time: 112 us; the launch traced here: 111 us
  Pallas kernels  49.2 us (44%)
  waiting for transfers between devices  26.6 us (24%)
  starting transfers between devices  19.9 us (18%)
  blocking collectives  14.5 us (13%)
  other arithmetic  1.12 us (1%)
    ppermute x17, waiting for transfers between devices, swap(): return lax.ppermute(value, axis, [(i, i ^ mask) for i in range(size)])  26.6 us
    pallas_call x2, Pallas kernels, partial(): pl.pallas_call(functools.partial(numer_kernel, columns, tuple(masks), own...  21.7 us
    ppermute x17, starting transfers between devices, swap(): return lax.ppermute(value, axis, [(i, i ^ mask) for i in range(size)])  18.3 us
    all_to_all x1, blocking collectives, shards(): lax.all_to_all(half.reshape(devices, slab, 2 * columns), 'row', split_axi...  14.5 us
    pallas_call x1, Pallas kernels, shards(): pl.pallas_call(functools.partial(band_kernel, angles, phases), out_shape=...  9 us
    pallas_call x1, Pallas kernels, shards(): pl.pallas_call(functools.partial(spectra_kernel, slab), out_shape=[jax.Sh...  6.57 us
    pallas_call x1, Pallas kernels, shards(): pl.pallas_call(functools.partial(power_kernel, columns, bands, tuple(mask...  5.9 us
    pallas_call x1, Pallas kernels, shards(): pl.pallas_call(functools.partial(plain_kernel, angles, phases), out_shape...  2.75 us
  transfers between devices with their start and end apart: 18, of which 7 were waited for; matrix products, arithmetic and copies ran while one was open for 0% of the time, Pallas kernels for 32%

profile of v6, /device:TPU:0, one launch (start us, length us, event | category | flops | bytes accessed | tf_op | source)
XLA Modules:
  0.0 111.5 jit_solution(11650923270658971080)
XLA Ops:
  0.0 1.0 convert_bitcast_fusion.refs_0_
  1.0 3.1 %collective-permute-start.2 = (bf16[64,1024]{1,0:T(8,128)(2,1)S(1)}, bf16[64,1024]{1,0:T(8,128)(2,1)S(1)}, u32[]{:S(2)}, u32[]{:S(2)}) collective-permute-start(bf16[64,1024]{1,0:T(8,128)(2,1)S(1)} %convert_bitcast_fusion.refs_0_), channel_id=1, source_target_pairs={{0,4},{1,5},{2,6},{3,7},{4,0},{5,1},{6,2},{7,3},{8,12},{9,13},{10,... | collective-permute-start | bytes 393224 | tf_op jit(solution)/shard_map/ppermute | solution.py:483
  4.1 2.6 %collective-permute-start.3 = (bf16[64,1024]{1,0:T(8,128)(2,1)S(1)}, bf16[64,1024]{1,0:T(8,128)(2,1)S(1)}, u32[]{:S(2)}, u32[]{:S(2)}) collective-permute-start(bf16[64,1024]{1,0:T(8,128)(2,1)S(1)} %convert_bitcast_fusion.refs_0_), channel_id=1, source_target_pairs={{0,8},{1,9},{2,10},{3,11},{4,12},{5,13},{6,14},{7,15},{8,0},{9,1},... | collective-permute-start | bytes 393224 | tf_op jit(solution)/shard_map/ppermute | solution.py:483
  6.7 0.0 collective-permute-start.4
  6.7 0.0 copy-start.1
  6.7 0.0 copy-start.2
  6.7 0.0 copy-start
  6.7 6.6 %spectra.1 = (f32[2,960,1024]{2,1,0:T(8,128)S(1)}, bf16[1024,1024]{1,0:T(8,128)(2,1)S(1)}, bf16[1024,1024]{1,0:T(8,128)(2,1)S(1)}, bf16[8,256,256]{2,1,0:T(8,128)(2,1)S(1)}) custom-call(s32[1]{0:T(128)} %bitcast.index_ref, bf16[960,1024]{1,0:T(8,128)(2,1)} %bitcast.12), custom_call_target="tpu_custom_call" | custom-call | flops 4026531840 | bytes 12582912 | tf_op jit(solution)/shard_map/spectra/pallas_call | solution.py:513
  13.3 0.0 copy-done.1
  13.3 0.0 copy-done.2
  13.3 0.0 copy-done
  13.3 2.7 %plain.1 = (f32[12,2,64,128]{3,2,1,0:T(8,128)S(1)}, bf16[128,256]{1,0:T(8,128)(2,1)S(1)}, bf16[128,256]{1,0:T(8,128)(2,1)S(1)}, bf16[128,256]{1,0:T(8,128)(2,1)S(1)}, bf16[128,256]{1,0:T(8,128)(2,1)S(1)}) custom-call(s32[1]{0:T(128)} %bitcast.index_ref, s32[5,5]{1,0:T(8,128)S(1)} %pad_add_fusion.shift_ref, f32[3,5,2,5]{3,2,1,0:T(2,128)S(1)} %bitcast.9, ...), custom_call_target="tpu_custom_call" | custom-call | flops 1006632960 | bytes 8388608 | tf_op jit(solution)/shard_map/plain/pallas_call | solution.py:560
  16.1 0.0 collective-permute-done.2.refs_1_.refs_0_
  16.1 0.9 collective-permute-done.3.refs_2_.refs_1_
  17.0 0.0 collective-permute-done.4.refs_3_.refs_2_
  17.0 1.6 %collective-permute-start.6 = (bf16[3,64,1024]{2,1,0:T(8,128)(2,1)S(1)}, bf16[3,64,1024]{2,1,0:T(8,128)(2,1)S(1)}, u32[]{:S(2)}, u32[]{:S(2)}) collective-permute-start(bf16[3,64,1024]{2,1,0:T(8,128)(2,1)S(1)} %pack.3), channel_id=1, source_target_pairs={{0,2},{1,3},{2,0},{3,1},{4,6},{5,7},{6,4},{7,5},{8,10},{9,11},{10,... | collective-permute-start | bytes 1179656 | tf_op jit(solution)/shard_map/ppermute | solution.py:483
  18.6 9.0 %bands.1 = (bf16[13,128,256]{2,1,0:T(8,128)(2,1)S(1)}, bf16[13,128,256]{2,1,0:T(8,128)(2,1)S(1)}, bf16[13,128,256]{2,1,0:T(8,128)(2,1)S(1)}, bf16[13,128,256]{2,1,0:T(8,128)(2,1)S(1)}) custom-call(s32[1]{0:T(128)} %bitcast.index_ref, s32[5,5]{1,0:T(8,128)S(1)} %pad_add_fusion.shift_ref, f32[3,5,2,5]{3,2,1,0:T(2,128)S(1)} %bitcast.10, ...), custom_call_target="tpu_custom_call" | custom-call | flops 4026531840 | bytes 12582912 | tf_op jit(solution)/shard_map/bands/pallas_call | solution.py:580
  27.6 0.1 collective-permute-start
  27.7 0.5 collective-permute-start.1
  28.2 0.5 collective-permute-start.5
  28.7 0.1 collective-permute-start.7
  28.8 4.9 %collective-permute-done.5.head_ref = bf16[64,1024]{1,0:T(8,128)(2,1)S(1)} collective-permute-done((bf16[64,1024]{1,0:T(8,128)(2,1)S(1)}, bf16[64,1024]{1,0:T(8,128)(2,1)S(1)}, u32[]{:S(2)}, u32[]{:S(2)}) %collective-permute-start.5) | collective-permute-done | bytes 131104 | tf_op jit(solution)/shard_map/ppermute | solution.py:483
  33.7 0.0 collective-permute-done.6.tail_ref
  33.7 0.1 collective-permute-start.8
  33.8 0.0 collective-permute-done.7.rest_2_
  33.8 0.0 collective-permute-done.got_away
  33.8 0.0 collective-permute-done.1.got_near
  33.8 1.9 %collective-permute-done.8.rest_3_ = bf16[4,64,1024]{2,1,0:T(8,128)(2,1)S(1)} collective-permute-done((bf16[4,64,1024]{2,1,0:T(8,128)(2,1)S(1)}, bf16[4,64,1024]{2,1,0:T(8,128)(2,1)S(1)}, u32[]{:S(2)}, u32[]{:S(2)}) %collective-permute-start.8) | collective-permute-done | bytes 524320 | tf_op jit(solution)/shard_map/ppermute | solution.py:483
  35.7 10.8 %shard_map.55 = (bf16[2,512,128]{2,1,0:T(8,128)(2,1)S(1)}, bf16[2,512,128]{2,1,0:T(8,128)(2,1)S(1)}, bf16[2,512,128]{2,1,0:T(8,128)(2,1)S(1)}, bf16[2,512,128]{2,1,0:T(8,128)(2,1)S(1)}) custom-call(s32[1]{0:T(128)} %bitcast.index_ref, s32[5,5]{1,0:T(8,128)S(1)} %pad_add_fusion.shift_ref, bf16[13,128,256]{2,1,0:T(8,128)(2,1)S(1)} %get-tuple-element.36.keep_away, ...), custom_call_target="tpu_custom_call" | custom-call | flops 3489660928 | bytes 8388608 | tf_op jit(solution)/shard_map/pallas_call | solution.py:608
  46.5 2.1 %collective-permute-start.14 = (bf16[2,512,128]{2,1,0:T(8,128)(2,1)S(1)}, bf16[2,512,128]{2,1,0:T(8,128)(2,1)S(1)}, u32[]{:S(2)}, u32[]{:S(2)}) collective-permute-start(bf16[2,512,128]{2,1,0:T(8,128)(2,1)S(1)} %get-tuple-element.49), channel_id=1, source_target_pairs={{0,4},{1,5},{2,6},{3,7},{4,0},{5,1},{6,2},{7,3},{8,12},{9,13},{10,... | collective-permute-start | bytes 786440 | tf_op jit(solution)/shard_map/ppermute | solution.py:483
  48.6 0.5 collective-permute-start.10
  49.1 10.8 %shard_map.56 = (bf16[2,512,128]{2,1,0:T(8,128)(2,1)S(1)}, bf16[2,512,128]{2,1,0:T(8,128)(2,1)S(1)}, bf16[2,512,128]{2,1,0:T(8,128)(2,1)S(1)}, bf16[2,512,128]{2,1,0:T(8,128)(2,1)S(1)}) custom-call(s32[1]{0:T(128)} %bitcast.index_ref, s32[5,5]{1,0:T(8,128)S(1)} %pad_add_fusion.shift_ref, bf16[13,128,256]{2,1,0:T(8,128)(2,1)S(1)} %get-tuple-element.36.keep_away, ...), custom_call_target="tpu_custom_call" | custom-call | flops 3489660928 | bytes 8388608 | tf_op jit(solution)/shard_map/pallas_call | solution.py:608
  60.0 5.9 %power.1.refs_4_ = f32[1024,128]{1,0:T(8,128)S(1)} custom-call(s32[1]{0:T(128)} %bitcast.index_ref, s32[5,5]{1,0:T(8,128)S(1)} %pad_add_fusion.shift_ref, bf16[4,64,1024]{2,1,0:T(8,128)(2,1)S(1)} %pack.2.rest_0_, bf16[4,64,1024]{2,1,0:T(8,128)(2,1)S(1)} %join.1.rest_1_, bf16[4,64,1024]{2,1,0:T(8,128)(2,1)S(1)} %collective-permute-done.7.rest_2_, ...), custom_call_target="tpu_custom_call" | custom-call | flops 1048576000 | bytes 5242880 | tf_op jit(solution)/shard_map/power/pallas_call | solution.py:632
  65.9 1.6 %collective-permute-start.17 = (f32[1024,128]{1,0:T(8,128)S(1)}, f32[1024,128]{1,0:T(8,128)S(1)}, u32[]{:S(2)}, u32[]{:S(2)}) collective-permute-start(f32[1024,128]{1,0:T(8,128)S(1)} %power.1.refs_4_), channel_id=1, source_target_pairs={{0,16},{16,0},{1,17},{17,1},{2,18},{18,2},{3,19},{19,3},{4,20},{20... | collective-permute-start | bytes 1572872 | tf_op jit(solution)/shard_map/ppermute | solution.py:680
  67.4 0.1 collective-permute-start.13
  67.5 1.5 %collective-permute-start.9 = (bf16[2,512,128]{2,1,0:T(8,128)(2,1)S(1)}, bf16[2,512,128]{2,1,0:T(8,128)(2,1)S(1)}, u32[]{:S(2)}, u32[]{:S(2)}) collective-permute-start(bf16[2,512,128]{2,1,0:T(8,128)(2,1)S(1)} %get-tuple-element.41), channel_id=1, source_target_pairs={{0,2},{1,3},{2,0},{3,1},{4,6},{5,7},{6,4},{7,5},{8,10},{9,11},{10,... | collective-permute-start | bytes 786440 | tf_op jit(solution)/shard_map/ppermute | solution.py:483
  69.0 0.0 collective-permute-done.14
  69.0 0.1 add_convert_fusion
  69.1 0.6 collective-permute-start.15
  69.7 0.0 collective-permute-done.10
  69.7 0.1 add_convert_fusion.1
  69.7 2.0 %collective-permute-start.11 = (bf16[2,512,128]{2,1,0:T(8,128)(2,1)S(1)}, bf16[2,512,128]{2,1,0:T(8,128)(2,1)S(1)}, u32[]{:S(2)}, u32[]{:S(2)}) collective-permute-start(bf16[2,512,128]{2,1,0:T(8,128)(2,1)S(1)} %add_convert_fusion.1), channel_id=1, source_target_pairs={{0,4},{1,5},{2,6},{3,7},{4,0},{5,1},{6,2},{7,3},{8,12},{9,13},{10,... | collective-permute-start | bytes 786440 | tf_op jit(solution)/shard_map/ppermute | solution.py:483
  71.8 4.8 %collective-permute-done.13.refs_0_ = bf16[2,512,128]{2,1,0:T(8,128)(2,1)S(1)} collective-permute-done((bf16[2,512,128]{2,1,0:T(8,128)(2,1)S(1)}, bf16[2,512,128]{2,1,0:T(8,128)(2,1)S(1)}, u32[]{:S(2)}, u32[]{:S(2)}) %collective-permute-start.13) | collective-permute-done | bytes 262176 | tf_op jit(solution)/shard_map/ppermute | solution.py:483
  76.6 4.0 %collective-permute-done.15.refs_2_ = bf16[2,512,128]{2,1,0:T(8,128)(2,1)S(1)} collective-permute-done((bf16[2,512,128]{2,1,0:T(8,128)(2,1)S(1)}, bf16[2,512,128]{2,1,0:T(8,128)(2,1)S(1)}, u32[]{:S(2)}, u32[]{:S(2)}) %collective-permute-start.15) | collective-permute-done | bytes 262176 | tf_op jit(solution)/shard_map/ppermute | solution.py:483
  80.6 0.1 fold.3
  80.7 2.7 %collective-permute-start.16 = (bf16[1,512,128]{2,1,0:T(8,128)(2,1)S(1)}, bf16[1,512,128]{2,1,0:T(8,128)(2,1)S(1)}, u32[]{:S(2)}, u32[]{:S(2)}) collective-permute-start(bf16[1,512,128]{2,1,0:T(8,128)(2,1)S(1)} %get-tuple-element.52), channel_id=1, source_target_pairs={{0,8},{1,9},{2,10},{3,11},{4,12},{5,13},{6,14},{7,15},{8,0},{9,1},... | collective-permute-start | bytes 393224 | tf_op jit(solution)/shard_map/ppermute | solution.py:483
  83.4 0.0 collective-permute-done.9.refs_0_
  83.5 0.0 collective-permute-done.11.refs_2_
  83.5 0.1 fold.2
  83.6 0.3 collective-permute-start.12
  83.9 0.0 collective-permute-done.17.refs_5_
  83.9 8.2 %collective-permute-done.16.refs_3_ = bf16[1,512,128]{2,1,0:T(8,128)(2,1)S(1)} collective-permute-done((bf16[1,512,128]{2,1,0:T(8,128)(2,1)S(1)}, bf16[1,512,128]{2,1,0:T(8,128)(2,1)S(1)}, u32[]{:S(2)}, u32[]{:S(2)}) %collective-permute-start.16) | collective-permute-done | bytes 131104 | tf_op jit(solution)/shard_map/ppermute | solution.py:483
  92.1 1.9 %collective-permute-done.12.refs_1_ = bf16[1,512,128]{2,1,0:T(8,128)(2,1)S(1)} collective-permute-done((bf16[1,512,128]{2,1,0:T(8,128)(2,1)S(1)}, bf16[1,512,128]{2,1,0:T(8,128)(2,1)S(1)}, u32[]{:S(2)}, u32[]{:S(2)}) %collective-permute-start.12) | collective-permute-done | bytes 131104 | tf_op jit(solution)/shard_map/ppermute | solution.py:483
  93.9 1.5 %inverse.1 = bf16[1024,128]{1,0:T(8,128)(2,1)S(1)} custom-call(f32[1,512,128]{2,1,0:T(8,128)S(1)} %get-tuple-element.45.refs_0_, bf16[1,512,128]{2,1,0:T(8,128)(2,1)S(1)} %collective-permute-done.12.refs_1_, f32[1,512,128]{2,1,0:T(8,128)S(1)} %get-tuple-element.51.refs_2_, bf16[1,512,128]{2,1,0:T(8,128)(2,1)S(1)} %collective-permute-done.16.refs_3_, ...), custom_call_target="tpu_custom_call" | custom-call | flops 536870912 | bytes 6291456 | tf_op jit(solution)/shard_map/inverse/pallas_call | solution.py:683
  95.4 14.5 %all_to_all.5.back_ref = bf16[16,64,128]{2,1,0:T(8,128)(2,1)S(1)} all-to-all(bf16[16,64,128]{2,1,0:T(8,128)(2,1)S(1)} %bitcast.8), channel_id=1, replica_groups=mesh['cuts'=2,'row'=16] {'row'}, dimensions={0} | all-to-all | bytes 524288 | tf_op jit(solution)/shard_map/all_to_all | solution.py:695
  109.9 1.6 %image.1 = f32[64,1024]{1,0:T(8,128)} custom-call(bf16[16,64,128]{2,1,0:T(8,128)(2,1)S(1)} %all_to_all.5.back_ref, bf16[1024,1024]{1,0:T(8,128)(2,1)S(1)} %get-tuple-element.53.refs_6_.cos_ref, bf16[1024,1024]{1,0:T(8,128)(2,1)S(1)} %get-tuple-element.54.refs_7_.sin_ref), custom_call_target="tpu_custom_call" | custom-call | flops 268435456 | bytes 6291456 | tf_op jit(solution)/shard_map/image/pallas_call | solution.py:698
  (4 shorter events, 0.1 us)
Async XLA Ops:
  1.0 15.1 %collective-permute-start.2 = (bf16[64,1024]{1,0:T(8,128)(2,1)S(1)}, bf16[64,1024]{1,0:T(8,128)(2,1)S(1)}, u32[]{:S(2)}, u32[]{:S(2)}) collective-permute-start(bf16[64,1024]{1,0:T(8,128)(2,1)S(1)} %convert_bitcast_fusion.refs_0_), channel_id=1, source_target_pairs={{0,4},{1,5},{2,6},{3,7},{4,0},{5,1},{6,2},{7,3},{8,12},{9,13},{10,... | collective-permute-start | bytes 393224 | tf_op jit(solution)/shard_map/ppermute | solution.py:483
  4.1 12.9 %collective-permute-start.3 = (bf16[64,1024]{1,0:T(8,128)(2,1)S(1)}, bf16[64,1024]{1,0:T(8,128)(2,1)S(1)}, u32[]{:S(2)}, u32[]{:S(2)}) collective-permute-start(bf16[64,1024]{1,0:T(8,128)(2,1)S(1)} %convert_bitcast_fusion.refs_0_), channel_id=1, source_target_pairs={{0,8},{1,9},{2,10},{3,11},{4,12},{5,13},{6,14},{7,15},{8,0},{9,1},... | collective-permute-start | bytes 393224 | tf_op jit(solution)/shard_map/ppermute | solution.py:483
  6.7 10.3 %collective-permute-start.4 = (bf16[64,1024]{1,0:T(8,128)(2,1)S(1)}, bf16[64,1024]{1,0:T(8,128)(2,1)S(1)}, u32[]{:S(2)}, u32[]{:S(2)}) collective-permute-start(bf16[64,1024]{1,0:T(8,128)(2,1)S(1)} %convert_bitcast_fusion.refs_0_), channel_id=1, source_target_pairs={{0,12},{1,13},{2,14},{3,15},{4,8},{5,9},{6,10},{7,11},{8,4},{9,5},... | collective-permute-start | bytes 393224 | tf_op jit(solution)/shard_map/ppermute | solution.py:483
  6.7 6.6 %copy-start.1 = (s32[3,5]{1,0:T(4,128)S(1)}, s32[3,5]{1,0:T(4,128)}, u32[]{:S(2)}) copy-start(s32[3,5]{1,0:T(4,128)} %param.8) | copy-start | bytes 184
  6.7 6.6 %copy-start.2 = (s32[3,2]{0,1:T(2,128)S(1)}, s32[3,2]{0,1:T(2,128)}, u32[]{:S(2)}) copy-start(s32[3,2]{0,1:T(2,128)} %param.7) | copy-start | bytes 76
  6.7 6.6 %copy-start = (f32[2,3,5,5]{3,0,2,1:T(2,128)S(1)}, f32[2,3,5,5]{3,0,2,1:T(2,128)}, u32[]{:S(2)}) copy-start(f32[2,3,5,5]{3,0,2,1:T(2,128)} %param.9) | copy-start | bytes 1804
  17.0 16.7 %collective-permute-start.6 = (bf16[3,64,1024]{2,1,0:T(8,128)(2,1)S(1)}, bf16[3,64,1024]{2,1,0:T(8,128)(2,1)S(1)}, u32[]{:S(2)}, u32[]{:S(2)}) collective-permute-start(bf16[3,64,1024]{2,1,0:T(8,128)(2,1)S(1)} %pack.3), channel_id=1, source_target_pairs={{0,2},{1,3},{2,0},{3,1},{4,6},{5,7},{6,4},{7,5},{8,10},{9,11},{10,... | collective-permute-start | bytes 1179656 | tf_op jit(solution)/shard_map/ppermute | solution.py:483
  27.6 6.2 %collective-permute-start = (bf16[13,128,256]{2,1,0:T(8,128)(2,1)S(1)}, bf16[13,128,256]{2,1,0:T(8,128)(2,1)S(1)}, u32[]{:S(2)}, u32[]{:S(2)}) collective-permute-start(bf16[13,128,256]{2,1,0:T(8,128)(2,1)S(1)} %get-tuple-element.37), channel_id=1, source_target_pairs={{0,1},{1,0},{2,3},{3,2},{4,5},{5,4},{6,7},{7,6},{8,9},{9,8},{10,11... | collective-permute-start | bytes 2555912 | tf_op jit(solution)/shard_map/ppermute | solution.py:483
  27.7 6.1 %collective-permute-start.1 = (bf16[13,128,256]{2,1,0:T(8,128)(2,1)S(1)}, bf16[13,128,256]{2,1,0:T(8,128)(2,1)S(1)}, u32[]{:S(2)}, u32[]{:S(2)}) collective-permute-start(bf16[13,128,256]{2,1,0:T(8,128)(2,1)S(1)} %get-tuple-element.39), channel_id=1, source_target_pairs={{0,1},{1,0},{2,3},{3,2},{4,5},{5,4},{6,7},{7,6},{8,9},{9,8},{10,11... | collective-permute-start | bytes 2555912 | tf_op jit(solution)/shard_map/ppermute | solution.py:483
  28.2 5.5 %collective-permute-start.5 = (bf16[64,1024]{1,0:T(8,128)(2,1)S(1)}, bf16[64,1024]{1,0:T(8,128)(2,1)S(1)}, u32[]{:S(2)}, u32[]{:S(2)}) collective-permute-start(bf16[64,1024]{1,0:T(8,128)(2,1)S(1)} %convert_bitcast_fusion.refs_0_), channel_id=1, source_target_pairs={{0,2},{1,3},{2,0},{3,1},{4,6},{5,7},{6,4},{7,5},{8,10},{9,11},{10,... | collective-permute-start | bytes 393224 | tf_op jit(solution)/shard_map/ppermute | solution.py:483
  28.7 5.1 %collective-permute-start.7 = (bf16[4,64,1024]{2,1,0:T(8,128)(2,1)S(1)}, bf16[4,64,1024]{2,1,0:T(8,128)(2,1)S(1)}, u32[]{:S(2)}, u32[]{:S(2)}) collective-permute-start(bf16[4,64,1024]{2,1,0:T(8,128)(2,1)S(1)} %pack.2.rest_0_), channel_id=1, source_target_pairs={{0,1},{1,0},{2,3},{3,2},{4,5},{5,4},{6,7},{7,6},{8,9},{9,8},{10,11... | collective-permute-start | bytes 1572872 | tf_op jit(solution)/shard_map/ppermute | solution.py:483
  33.7 2.0 %collective-permute-start.8 = (bf16[4,64,1024]{2,1,0:T(8,128)(2,1)S(1)}, bf16[4,64,1024]{2,1,0:T(8,128)(2,1)S(1)}, u32[]{:S(2)}, u32[]{:S(2)}) collective-permute-start(bf16[4,64,1024]{2,1,0:T(8,128)(2,1)S(1)} %join.1.rest_1_), channel_id=1, source_target_pairs={{0,1},{1,0},{2,3},{3,2},{4,5},{5,4},{6,7},{7,6},{8,9},{9,8},{10,11... | collective-permute-start | bytes 1572872 | tf_op jit(solution)/shard_map/ppermute | solution.py:483
  46.5 22.5 %collective-permute-start.14 = (bf16[2,512,128]{2,1,0:T(8,128)(2,1)S(1)}, bf16[2,512,128]{2,1,0:T(8,128)(2,1)S(1)}, u32[]{:S(2)}, u32[]{:S(2)}) collective-permute-start(bf16[2,512,128]{2,1,0:T(8,128)(2,1)S(1)} %get-tuple-element.49), channel_id=1, source_target_pairs={{0,4},{1,5},{2,6},{3,7},{4,0},{5,1},{6,2},{7,3},{8,12},{9,13},{10,... | collective-permute-start | bytes 786440 | tf_op jit(solution)/shard_map/ppermute | solution.py:483
  48.6 21.1 %collective-permute-start.10 = (bf16[2,512,128]{2,1,0:T(8,128)(2,1)S(1)}, bf16[2,512,128]{2,1,0:T(8,128)(2,1)S(1)}, u32[]{:S(2)}, u32[]{:S(2)}) collective-permute-start(bf16[2,512,128]{2,1,0:T(8,128)(2,1)S(1)} %get-tuple-element.43), channel_id=1, source_target_pairs={{0,2},{1,3},{2,0},{3,1},{4,6},{5,7},{6,4},{7,5},{8,10},{9,11},{10,... | collective-permute-start | bytes 786440 | tf_op jit(solution)/shard_map/ppermute | solution.py:483
  65.9 18.0 %collective-permute-start.17 = (f32[1024,128]{1,0:T(8,128)S(1)}, f32[1024,128]{1,0:T(8,128)S(1)}, u32[]{:S(2)}, u32[]{:S(2)}) collective-permute-start(f32[1024,128]{1,0:T(8,128)S(1)} %power.1.refs_4_), channel_id=1, source_target_pairs={{0,16},{16,0},{1,17},{17,1},{2,18},{18,2},{3,19},{19,3},{4,20},{20... | collective-permute-start | bytes 1572872 | tf_op jit(solution)/shard_map/ppermute | solution.py:680
  67.4 9.2 %collective-permute-start.13 = (bf16[2,512,128]{2,1,0:T(8,128)(2,1)S(1)}, bf16[2,512,128]{2,1,0:T(8,128)(2,1)S(1)}, u32[]{:S(2)}, u32[]{:S(2)}) collective-permute-start(bf16[2,512,128]{2,1,0:T(8,128)(2,1)S(1)} %get-tuple-element.47), channel_id=1, source_target_pairs={{0,4},{1,5},{2,6},{3,7},{4,0},{5,1},{6,2},{7,3},{8,12},{9,13},{10,... | collective-permute-start | bytes 786440 | tf_op jit(solution)/shard_map/ppermute | solution.py:483
  67.5 16.0 %collective-permute-start.9 = (bf16[2,512,128]{2,1,0:T(8,128)(2,1)S(1)}, bf16[2,512,128]{2,1,0:T(8,128)(2,1)S(1)}, u32[]{:S(2)}, u32[]{:S(2)}) collective-permute-start(bf16[2,512,128]{2,1,0:T(8,128)(2,1)S(1)} %get-tuple-element.41), channel_id=1, source_target_pairs={{0,2},{1,3},{2,0},{3,1},{4,6},{5,7},{6,4},{7,5},{8,10},{9,11},{10,... | collective-permute-start | bytes 786440 | tf_op jit(solution)/shard_map/ppermute | solution.py:483
  69.1 11.5 %collective-permute-start.15 = (bf16[2,512,128]{2,1,0:T(8,128)(2,1)S(1)}, bf16[2,512,128]{2,1,0:T(8,128)(2,1)S(1)}, u32[]{:S(2)}, u32[]{:S(2)}) collective-permute-start(bf16[2,512,128]{2,1,0:T(8,128)(2,1)S(1)} %add_convert_fusion), channel_id=1, source_target_pairs={{0,2},{1,3},{2,0},{3,1},{4,6},{5,7},{6,4},{7,5},{8,10},{9,11},{10,... | collective-permute-start | bytes 786440 | tf_op jit(solution)/shard_map/ppermute | solution.py:483
  69.7 13.7 %collective-permute-start.11 = (bf16[2,512,128]{2,1,0:T(8,128)(2,1)S(1)}, bf16[2,512,128]{2,1,0:T(8,128)(2,1)S(1)}, u32[]{:S(2)}, u32[]{:S(2)}) collective-permute-start(bf16[2,512,128]{2,1,0:T(8,128)(2,1)S(1)} %add_convert_fusion.1), channel_id=1, source_target_pairs={{0,4},{1,5},{2,6},{3,7},{4,0},{5,1},{6,2},{7,3},{8,12},{9,13},{10,... | collective-permute-start | bytes 786440 | tf_op jit(solution)/shard_map/ppermute | solution.py:483
  80.7 11.3 %collective-permute-start.16 = (bf16[1,512,128]{2,1,0:T(8,128)(2,1)S(1)}, bf16[1,512,128]{2,1,0:T(8,128)(2,1)S(1)}, u32[]{:S(2)}, u32[]{:S(2)}) collective-permute-start(bf16[1,512,128]{2,1,0:T(8,128)(2,1)S(1)} %get-tuple-element.52), channel_id=1, source_target_pairs={{0,8},{1,9},{2,10},{3,11},{4,12},{5,13},{6,14},{7,15},{8,0},{9,1},... | collective-permute-start | bytes 393224 | tf_op jit(solution)/shard_map/ppermute | solution.py:483
  83.6 10.4 %collective-permute-start.12 = (bf16[1,512,128]{2,1,0:T(8,128)(2,1)S(1)}, bf16[1,512,128]{2,1,0:T(8,128)(2,1)S(1)}, u32[]{:S(2)}, u32[]{:S(2)}) collective-permute-start(bf16[1,512,128]{2,1,0:T(8,128)(2,1)S(1)} %get-tuple-element.46), channel_id=1, source_target_pairs={{0,8},{1,9},{2,10},{3,11},{4,12},{5,13},{6,14},{7,15},{8,0},{9,1},... | collective-permute-start | bytes 393224 | tf_op jit(solution)/shard_map/ppermute | solution.py:483

commit v7 on v6

--- a/solution.py
+++ b/solution.py
@@ -378,7 +378,7 @@
 
 def power_kernel(columns, bands, masks, index_ref, shift_ref, *rest):
     *otf_refs, _, power_ref, wide = rest
-    pixels = power_ref.shape[0]
+    pixels = 2 * power_ref.shape[0]
     tile = wide.shape[1] - pixels
     index = index_ref[0]
     core = index & 1
@@ -389,16 +389,19 @@
     angles = (bands - 1) // (len(MULTIPLES) - 1)
     widen_otf(wide, masks, index, otf_refs)
 
-    @pl.loop(0, pixels // tile)
+    @pl.loop(0, pixels // tile // 2)
     def _(step):
-        q0 = pl.multiple_of(step * tile, tile)
-        gathered = None
-        for band in range(bands):
-            value = response(wide, shift_ref, q0, band, own_column, 1)[0]
-            value = value * value
-            gathered = value * float(angles) if band == 0 else gathered + value
-        power_ref[pl.ds(q0, tile), :] = jnp.concatenate(
-            [gathered[:, :columns], gathered[:, :columns]], axis=1
+        halves = []
+        for upper in range(2):
+            q0 = pl.multiple_of(step * tile + upper * (pixels // 2), tile)
+            gathered = None
+            for band in range(bands):
+                value = response(wide, shift_ref, q0, band, own_column, 1)[0]
+                value = value * value
+                gathered = value * float(angles) if band == 0 else gathered + value
+            halves.append(gathered[:, :columns])
+        power_ref[pl.ds(pl.multiple_of(step * tile, tile), tile), :] = jnp.concatenate(
+            halves, axis=1
         )
 
 
@@ -422,9 +425,11 @@
     rows = pixels // 2
     for upper in range(2):
         here = slice(upper * rows, (upper + 1) * rows)
-        power = powers[0][here, :]
+        cut = slice(upper * columns, (upper + 1) * columns)
+        power = powers[0][:, cut]
         for ref in powers[1:]:
-            power = power + ref[here, :]
+            power = power + ref[:, cut]
+        power = jnp.concatenate([power, power], axis=1)
         numer = None
         for ref in parts[upper * numers : (upper + 1) * numers]:
             one = ref[0].astype(jnp.float32)
@@ -627,11 +632,12 @@
         )
 
     away = partial(False)
-    moved = [swap(value, "row", mask) for value, mask in zip(away, (2, 4, 2, 4))]
+    moved = [swap(value, "row", mask) for value, mask in zip(away[:2], (2, 4))]
+    moved += [swap(value, "row", mask) for value, mask in zip(away[2:], (2, 4))]
     kept = partial(True)
     power = pl.pallas_call(
         functools.partial(power_kernel, columns, bands, tuple(masks)),
-        out_shape=jax.ShapeDtypeStruct((pixels, 2 * columns), jnp.float32),
+        out_shape=jax.ShapeDtypeStruct((pixels // 2, 2 * columns), jnp.float32),
         in_specs=[smem()] * 2 + [vmem()] * 4 + [pl.BlockSpec(memory_space=pl.ANY)],
         out_specs=vmem(),
         scratch_shapes=[wide_scratch],
@@ -676,9 +682,7 @@
     powers = [power]
     cuts = lax.axis_size("cuts")
     for _ in range(cuts - 1):
-        powers.append(
-            lax.ppermute(powers[-1], "cuts", [(i, (i + 1) % cuts) for i in range(cuts)])
-        )
+        powers.append(lax.ppermute(powers[-1], "cuts", [(i, (i + 1) % cuts) for i in range(cuts)]))
     parts = stays[0] + stays[1] + powers
     half = pl.pallas_call(
         functools.partial(inverse_kernel, columns, float(slices * angles), len(stays[0])),

time: 112 us -> 102 us (0.911)
  waiting for transfers between devices: 26.6 us -> 17.3 us
    ppermute x17, waiting for transfers between devices: 26.6 us -> 15.4 us  [swap(): return lax.ppermute(value, axis, [(i, i ^ mask) for i in range(size)])]
    ppermute x1, waiting for transfers between devices: 0.01 us -> 1.92 us  [shards(): lax.ppermute(powers[-1], 'cuts', [(i, (i + 1) % cuts) for i in range(cuts)])]
  transfers between devices with their start and end apart: 18 -> 18, of which waited for: 7 -> 6; matrix products, arithmetic and copies ran while one was open for 0% -> 0% of each run, Pallas kernels for 32% -> 34%
where the time goes in v7:
time: 102 us
  Pallas kernels  48.6 us (48%)
  starting transfers between devices  19.9 us (20%)
  waiting for transfers between devices  17.3 us (17%)
  blocking collectives  14.7 us (14%)
  other arithmetic  1.12 us (1%)
    pallas_call x2, Pallas kernels, partial(): pl.pallas_call(functools.partial(numer_kernel, columns, tuple(masks), own...  21.7 us
    ppermute x17, starting transfers between devices, swap(): return lax.ppermute(value, axis, [(i, i ^ mask) for i in range(size)])  18.3 us
    ppermute x17, waiting for transfers between devices, swap(): return lax.ppermute(value, axis, [(i, i ^ mask) for i in range(size)])  15.4 us
    all_to_all x1, blocking collectives, shards(): lax.all_to_all(half.reshape(devices, slab, 2 * columns), 'row', split_axi...  14.7 us
    pallas_call x1, Pallas kernels, shards(): pl.pallas_call(functools.partial(band_kernel, angles, phases), out_shape=...  9 us
    pallas_call x1, Pallas kernels, shards(): pl.pallas_call(functools.partial(spectra_kernel, slab), out_shape=[jax.Sh...  6.57 us
    pallas_call x1, Pallas kernels, shards(): pl.pallas_call(functools.partial(power_kernel, columns, bands, tuple(mask...  5.22 us
    pallas_call x1, Pallas kernels, shards(): pl.pallas_call(functools.partial(plain_kernel, angles, phases), out_shape...  2.75 us
  transfers between devices with their start and end apart: 18, of which 6 were waited for; matrix products, arithmetic and copies ran while one was open for 0% of the time, Pallas kernels for 34%

profile of v7, /device:TPU:0, one launch (start us, length us, event | category | flops | bytes accessed | tf_op | source)
XLA Modules:
  0.0 101.8 jit_solution(8407090446130110490)
XLA Ops:
  0.0 1.0 convert_bitcast_fusion.refs_0_
  1.0 3.1 %collective-permute-start.2 = (bf16[64,1024]{1,0:T(8,128)(2,1)S(1)}, bf16[64,1024]{1,0:T(8,128)(2,1)S(1)}, u32[]{:S(2)}, u32[]{:S(2)}) collective-permute-start(bf16[64,1024]{1,0:T(8,128)(2,1)S(1)} %convert_bitcast_fusion.refs_0_), channel_id=1, source_target_pairs={{0,4},{1,5},{2,6},{3,7},{4,0},{5,1},{6,2},{7,3},{8,12},{9,13},{10,... | collective-permute-start | bytes 393224 | tf_op jit(solution)/shard_map/ppermute | solution.py:488
  4.1 2.6 %collective-permute-start.3 = (bf16[64,1024]{1,0:T(8,128)(2,1)S(1)}, bf16[64,1024]{1,0:T(8,128)(2,1)S(1)}, u32[]{:S(2)}, u32[]{:S(2)}) collective-permute-start(bf16[64,1024]{1,0:T(8,128)(2,1)S(1)} %convert_bitcast_fusion.refs_0_), channel_id=1, source_target_pairs={{0,8},{1,9},{2,10},{3,11},{4,12},{5,13},{6,14},{7,15},{8,0},{9,1},... | collective-permute-start | bytes 393224 | tf_op jit(solution)/shard_map/ppermute | solution.py:488
  6.7 0.0 collective-permute-start.4
  6.7 0.0 copy-start.1
  6.7 0.0 copy-start.2
  6.7 0.0 copy-start
  6.7 6.6 %spectra.1 = (f32[2,960,1024]{2,1,0:T(8,128)S(1)}, bf16[1024,1024]{1,0:T(8,128)(2,1)S(1)}, bf16[1024,1024]{1,0:T(8,128)(2,1)S(1)}, bf16[8,256,256]{2,1,0:T(8,128)(2,1)S(1)}) custom-call(s32[1]{0:T(128)} %bitcast.index_ref, bf16[960,1024]{1,0:T(8,128)(2,1)} %bitcast.12), custom_call_target="tpu_custom_call" | custom-call | flops 4026531840 | bytes 12582912 | tf_op jit(solution)/shard_map/spectra/pallas_call | solution.py:518
  13.3 0.0 copy-done.1
  13.3 0.0 copy-done.2
  13.3 0.0 copy-done
  13.3 2.7 %plain.1 = (f32[12,2,64,128]{3,2,1,0:T(8,128)S(1)}, bf16[128,256]{1,0:T(8,128)(2,1)S(1)}, bf16[128,256]{1,0:T(8,128)(2,1)S(1)}, bf16[128,256]{1,0:T(8,128)(2,1)S(1)}, bf16[128,256]{1,0:T(8,128)(2,1)S(1)}) custom-call(s32[1]{0:T(128)} %bitcast.index_ref, s32[5,5]{1,0:T(8,128)S(1)} %pad_add_fusion.shift_ref, f32[3,5,2,5]{3,2,1,0:T(2,128)S(1)} %bitcast.9, ...), custom_call_target="tpu_custom_call" | custom-call | flops 1006632960 | bytes 8388608 | tf_op jit(solution)/shard_map/plain/pallas_call | solution.py:565
  16.1 0.0 collective-permute-done.2.refs_1_.refs_0_
  16.1 0.9 collective-permute-done.3.refs_2_.refs_1_
  17.0 0.0 collective-permute-done.4.refs_3_.refs_2_
  17.0 1.6 %collective-permute-start.6 = (bf16[3,64,1024]{2,1,0:T(8,128)(2,1)S(1)}, bf16[3,64,1024]{2,1,0:T(8,128)(2,1)S(1)}, u32[]{:S(2)}, u32[]{:S(2)}) collective-permute-start(bf16[3,64,1024]{2,1,0:T(8,128)(2,1)S(1)} %pack.3), channel_id=1, source_target_pairs={{0,2},{1,3},{2,0},{3,1},{4,6},{5,7},{6,4},{7,5},{8,10},{9,11},{10,... | collective-permute-start | bytes 1179656 | tf_op jit(solution)/shard_map/ppermute | solution.py:488
  18.6 9.0 %bands.1 = (bf16[13,128,256]{2,1,0:T(8,128)(2,1)S(1)}, bf16[13,128,256]{2,1,0:T(8,128)(2,1)S(1)}, bf16[13,128,256]{2,1,0:T(8,128)(2,1)S(1)}, bf16[13,128,256]{2,1,0:T(8,128)(2,1)S(1)}) custom-call(s32[1]{0:T(128)} %bitcast.index_ref, s32[5,5]{1,0:T(8,128)S(1)} %pad_add_fusion.shift_ref, f32[3,5,2,5]{3,2,1,0:T(2,128)S(1)} %bitcast.10, ...), custom_call_target="tpu_custom_call" | custom-call | flops 4026531840 | bytes 12582912 | tf_op jit(solution)/shard_map/bands/pallas_call | solution.py:585
  27.6 0.1 collective-permute-start
  27.7 0.5 collective-permute-start.1
  28.2 0.5 collective-permute-start.5
  28.7 0.1 collective-permute-start.7
  28.8 4.9 %collective-permute-done.5.head_ref = bf16[64,1024]{1,0:T(8,128)(2,1)S(1)} collective-permute-done((bf16[64,1024]{1,0:T(8,128)(2,1)S(1)}, bf16[64,1024]{1,0:T(8,128)(2,1)S(1)}, u32[]{:S(2)}, u32[]{:S(2)}) %collective-permute-start.5) | collective-permute-done | bytes 131104 | tf_op jit(solution)/shard_map/ppermute | solution.py:488
  33.7 0.0 collective-permute-done.6.tail_ref
  33.7 0.1 collective-permute-start.8
  33.8 0.0 collective-permute-done.7.rest_2_
  33.8 0.0 collective-permute-done.got_away
  33.8 0.0 collective-permute-done.1.got_near
  33.8 1.9 %collective-permute-done.8.rest_3_ = bf16[4,64,1024]{2,1,0:T(8,128)(2,1)S(1)} collective-permute-done((bf16[4,64,1024]{2,1,0:T(8,128)(2,1)S(1)}, bf16[4,64,1024]{2,1,0:T(8,128)(2,1)S(1)}, u32[]{:S(2)}, u32[]{:S(2)}) %collective-permute-start.8) | collective-permute-done | bytes 524320 | tf_op jit(solution)/shard_map/ppermute | solution.py:488
  35.7 10.8 %shard_map.55 = (bf16[2,512,128]{2,1,0:T(8,128)(2,1)S(1)}, bf16[2,512,128]{2,1,0:T(8,128)(2,1)S(1)}, bf16[2,512,128]{2,1,0:T(8,128)(2,1)S(1)}, bf16[2,512,128]{2,1,0:T(8,128)(2,1)S(1)}) custom-call(s32[1]{0:T(128)} %bitcast.index_ref, s32[5,5]{1,0:T(8,128)S(1)} %pad_add_fusion.shift_ref, bf16[13,128,256]{2,1,0:T(8,128)(2,1)S(1)} %get-tuple-element.36.keep_away, ...), custom_call_target="tpu_custom_call" | custom-call | flops 3489660928 | bytes 8388608 | tf_op jit(solution)/shard_map/pallas_call | solution.py:613
  46.5 2.1 %collective-permute-start.14 = (bf16[2,512,128]{2,1,0:T(8,128)(2,1)S(1)}, bf16[2,512,128]{2,1,0:T(8,128)(2,1)S(1)}, u32[]{:S(2)}, u32[]{:S(2)}) collective-permute-start(bf16[2,512,128]{2,1,0:T(8,128)(2,1)S(1)} %get-tuple-element.49), channel_id=1, source_target_pairs={{0,4},{1,5},{2,6},{3,7},{4,0},{5,1},{6,2},{7,3},{8,12},{9,13},{10,... | collective-permute-start | bytes 786440 | tf_op jit(solution)/shard_map/ppermute | solution.py:488
  48.6 0.1 collective-permute-start.13
  48.7 0.5 collective-permute-start.10
  49.2 1.5 %collective-permute-start.9 = (bf16[2,512,128]{2,1,0:T(8,128)(2,1)S(1)}, bf16[2,512,128]{2,1,0:T(8,128)(2,1)S(1)}, u32[]{:S(2)}, u32[]{:S(2)}) collective-permute-start(bf16[2,512,128]{2,1,0:T(8,128)(2,1)S(1)} %get-tuple-element.41), channel_id=1, source_target_pairs={{0,2},{1,3},{2,0},{3,1},{4,6},{5,7},{6,4},{7,5},{8,10},{9,11},{10,... | collective-permute-start | bytes 786440 | tf_op jit(solution)/shard_map/ppermute | solution.py:488
  50.7 10.8 %shard_map.56 = (bf16[2,512,128]{2,1,0:T(8,128)(2,1)S(1)}, bf16[2,512,128]{2,1,0:T(8,128)(2,1)S(1)}, bf16[2,512,128]{2,1,0:T(8,128)(2,1)S(1)}, bf16[2,512,128]{2,1,0:T(8,128)(2,1)S(1)}) custom-call(s32[1]{0:T(128)} %bitcast.index_ref, s32[5,5]{1,0:T(8,128)S(1)} %pad_add_fusion.shift_ref, bf16[13,128,256]{2,1,0:T(8,128)(2,1)S(1)} %get-tuple-element.36.keep_away, ...), custom_call_target="tpu_custom_call" | custom-call | flops 3489660928 | bytes 8388608 | tf_op jit(solution)/shard_map/pallas_call | solution.py:613
  61.5 0.0 collective-permute-done.14
  61.6 0.1 add_convert_fusion
  61.6 0.6 collective-permute-start.15
  62.2 0.0 collective-permute-done.10
  62.2 0.1 add_convert_fusion.1
  62.3 2.0 %collective-permute-start.11 = (bf16[2,512,128]{2,1,0:T(8,128)(2,1)S(1)}, bf16[2,512,128]{2,1,0:T(8,128)(2,1)S(1)}, u32[]{:S(2)}, u32[]{:S(2)}) collective-permute-start(bf16[2,512,128]{2,1,0:T(8,128)(2,1)S(1)} %add_convert_fusion.1), channel_id=1, source_target_pairs={{0,4},{1,5},{2,6},{3,7},{4,0},{5,1},{6,2},{7,3},{8,12},{9,13},{10,... | collective-permute-start | bytes 786440 | tf_op jit(solution)/shard_map/ppermute | solution.py:488
  64.3 5.2 %power.1.refs_4_ = f32[512,128]{1,0:T(8,128)S(1)} custom-call(s32[1]{0:T(128)} %bitcast.index_ref, s32[5,5]{1,0:T(8,128)S(1)} %pad_add_fusion.shift_ref, bf16[4,64,1024]{2,1,0:T(8,128)(2,1)S(1)} %pack.2.rest_0_, bf16[4,64,1024]{2,1,0:T(8,128)(2,1)S(1)} %join.1.rest_1_, bf16[4,64,1024]{2,1,0:T(8,128)(2,1)S(1)} %collective-permute-done.7.rest_2_, ...), custom_call_target="tpu_custom_call" | custom-call | flops 1048576000 | bytes 5242880 | tf_op jit(solution)/shard_map/power/pallas_call | solution.py:638
  69.5 1.6 %collective-permute-start.17 = (f32[512,128]{1,0:T(8,128)S(1)}, f32[512,128]{1,0:T(8,128)S(1)}, u32[]{:S(2)}, u32[]{:S(2)}) collective-permute-start(f32[512,128]{1,0:T(8,128)S(1)} %power.1.refs_4_), channel_id=1, source_target_pairs={{0,16},{16,0},{1,17},{17,1},{2,18},{18,2},{3,19},{19,3},{4,20},{20... | collective-permute-start | bytes 786440 | tf_op jit(solution)/shard_map/ppermute | solution.py:685
  71.1 0.0 collective-permute-done.13.refs_0_
  71.1 0.0 collective-permute-done.15.refs_2_
  71.1 0.1 fold.3
  71.2 1.6 %collective-permute-start.16 = (bf16[1,512,128]{2,1,0:T(8,128)(2,1)S(1)}, bf16[1,512,128]{2,1,0:T(8,128)(2,1)S(1)}, u32[]{:S(2)}, u32[]{:S(2)}) collective-permute-start(bf16[1,512,128]{2,1,0:T(8,128)(2,1)S(1)} %get-tuple-element.52), channel_id=1, source_target_pairs={{0,8},{1,9},{2,10},{3,11},{4,12},{5,13},{6,14},{7,15},{8,0},{9,1},... | collective-permute-start | bytes 393224 | tf_op jit(solution)/shard_map/ppermute | solution.py:488
  72.8 0.0 collective-permute-done.9.refs_0_
  72.8 0.0 collective-permute-done.11.refs_2_
  72.8 0.1 fold.2
  72.9 1.5 %collective-permute-start.12 = (bf16[1,512,128]{2,1,0:T(8,128)(2,1)S(1)}, bf16[1,512,128]{2,1,0:T(8,128)(2,1)S(1)}, u32[]{:S(2)}, u32[]{:S(2)}) collective-permute-start(bf16[1,512,128]{2,1,0:T(8,128)(2,1)S(1)} %get-tuple-element.46), channel_id=1, source_target_pairs={{0,8},{1,9},{2,10},{3,11},{4,12},{5,13},{6,14},{7,15},{8,0},{9,1},... | collective-permute-start | bytes 393224 | tf_op jit(solution)/shard_map/ppermute | solution.py:488
  74.3 1.9 %collective-permute-done.17.refs_5_ = f32[512,128]{1,0:T(8,128)S(1)} collective-permute-done((f32[512,128]{1,0:T(8,128)S(1)}, f32[512,128]{1,0:T(8,128)S(1)}, u32[]{:S(2)}, u32[]{:S(2)}) %collective-permute-start.17) | collective-permute-done | bytes 262176 | tf_op jit(solution)/shard_map/ppermute | solution.py:685
  76.3 6.1 %collective-permute-done.16.refs_3_ = bf16[1,512,128]{2,1,0:T(8,128)(2,1)S(1)} collective-permute-done((bf16[1,512,128]{2,1,0:T(8,128)(2,1)S(1)}, bf16[1,512,128]{2,1,0:T(8,128)(2,1)S(1)}, u32[]{:S(2)}, u32[]{:S(2)}) %collective-permute-start.16) | collective-permute-done | bytes 131104 | tf_op jit(solution)/shard_map/ppermute | solution.py:488
  82.4 1.6 %collective-permute-done.12.refs_1_ = bf16[1,512,128]{2,1,0:T(8,128)(2,1)S(1)} collective-permute-done((bf16[1,512,128]{2,1,0:T(8,128)(2,1)S(1)}, bf16[1,512,128]{2,1,0:T(8,128)(2,1)S(1)}, u32[]{:S(2)}, u32[]{:S(2)}) %collective-permute-start.12) | collective-permute-done | bytes 131104 | tf_op jit(solution)/shard_map/ppermute | solution.py:488
  84.0 1.5 %inverse.1 = bf16[1024,128]{1,0:T(8,128)(2,1)S(1)} custom-call(f32[1,512,128]{2,1,0:T(8,128)S(1)} %get-tuple-element.45.refs_0_, bf16[1,512,128]{2,1,0:T(8,128)(2,1)S(1)} %collective-permute-done.12.refs_1_, f32[1,512,128]{2,1,0:T(8,128)S(1)} %get-tuple-element.51.refs_2_, bf16[1,512,128]{2,1,0:T(8,128)(2,1)S(1)} %collective-permute-done.16.refs_3_, ...), custom_call_target="tpu_custom_call" | custom-call | flops 536870912 | bytes 6291456 | tf_op jit(solution)/shard_map/inverse/pallas_call | solution.py:687
  85.5 14.7 %all_to_all.5.back_ref = bf16[16,64,128]{2,1,0:T(8,128)(2,1)S(1)} all-to-all(bf16[16,64,128]{2,1,0:T(8,128)(2,1)S(1)} %bitcast.8), channel_id=1, replica_groups=mesh['cuts'=2,'row'=16] {'row'}, dimensions={0} | all-to-all | bytes 524288 | tf_op jit(solution)/shard_map/all_to_all | solution.py:699
  100.2 1.6 %image.1 = f32[64,1024]{1,0:T(8,128)} custom-call(bf16[16,64,128]{2,1,0:T(8,128)(2,1)S(1)} %all_to_all.5.back_ref, bf16[1024,1024]{1,0:T(8,128)(2,1)S(1)} %get-tuple-element.53.refs_6_.cos_ref, bf16[1024,1024]{1,0:T(8,128)(2,1)S(1)} %get-tuple-element.54.refs_7_.sin_ref), custom_call_target="tpu_custom_call" | custom-call | flops 268435456 | bytes 6291456 | tf_op jit(solution)/shard_map/image/pallas_call | solution.py:702
  (4 shorter events, 0.1 us)
Async XLA Ops:
  1.0 15.1 %collective-permute-start.2 = (bf16[64,1024]{1,0:T(8,128)(2,1)S(1)}, bf16[64,1024]{1,0:T(8,128)(2,1)S(1)}, u32[]{:S(2)}, u32[]{:S(2)}) collective-permute-start(bf16[64,1024]{1,0:T(8,128)(2,1)S(1)} %convert_bitcast_fusion.refs_0_), channel_id=1, source_target_pairs={{0,4},{1,5},{2,6},{3,7},{4,0},{5,1},{6,2},{7,3},{8,12},{9,13},{10,... | collective-permute-start | bytes 393224 | tf_op jit(solution)/shard_map/ppermute | solution.py:488
  4.1 12.9 %collective-permute-start.3 = (bf16[64,1024]{1,0:T(8,128)(2,1)S(1)}, bf16[64,1024]{1,0:T(8,128)(2,1)S(1)}, u32[]{:S(2)}, u32[]{:S(2)}) collective-permute-start(bf16[64,1024]{1,0:T(8,128)(2,1)S(1)} %convert_bitcast_fusion.refs_0_), channel_id=1, source_target_pairs={{0,8},{1,9},{2,10},{3,11},{4,12},{5,13},{6,14},{7,15},{8,0},{9,1},... | collective-permute-start | bytes 393224 | tf_op jit(solution)/shard_map/ppermute | solution.py:488
  6.7 10.3 %collective-permute-start.4 = (bf16[64,1024]{1,0:T(8,128)(2,1)S(1)}, bf16[64,1024]{1,0:T(8,128)(2,1)S(1)}, u32[]{:S(2)}, u32[]{:S(2)}) collective-permute-start(bf16[64,1024]{1,0:T(8,128)(2,1)S(1)} %convert_bitcast_fusion.refs_0_), channel_id=1, source_target_pairs={{0,12},{1,13},{2,14},{3,15},{4,8},{5,9},{6,10},{7,11},{8,4},{9,5},... | collective-permute-start | bytes 393224 | tf_op jit(solution)/shard_map/ppermute | solution.py:488
  6.7 6.6 %copy-start.1 = (s32[3,5]{1,0:T(4,128)S(1)}, s32[3,5]{1,0:T(4,128)}, u32[]{:S(2)}) copy-start(s32[3,5]{1,0:T(4,128)} %param.8) | copy-start | bytes 184
  6.7 6.6 %copy-start.2 = (s32[3,2]{0,1:T(2,128)S(1)}, s32[3,2]{0,1:T(2,128)}, u32[]{:S(2)}) copy-start(s32[3,2]{0,1:T(2,128)} %param.7) | copy-start | bytes 76
  6.7 6.6 %copy-start = (f32[2,3,5,5]{3,0,2,1:T(2,128)S(1)}, f32[2,3,5,5]{3,0,2,1:T(2,128)}, u32[]{:S(2)}) copy-start(f32[2,3,5,5]{3,0,2,1:T(2,128)} %param.9) | copy-start | bytes 1804
  17.0 16.7 %collective-permute-start.6 = (bf16[3,64,1024]{2,1,0:T(8,128)(2,1)S(1)}, bf16[3,64,1024]{2,1,0:T(8,128)(2,1)S(1)}, u32[]{:S(2)}, u32[]{:S(2)}) collective-permute-start(bf16[3,64,1024]{2,1,0:T(8,128)(2,1)S(1)} %pack.3), channel_id=1, source_target_pairs={{0,2},{1,3},{2,0},{3,1},{4,6},{5,7},{6,4},{7,5},{8,10},{9,11},{10,... | collective-permute-start | bytes 1179656 | tf_op jit(solution)/shard_map/ppermute | solution.py:488
  27.6 6.2 %collective-permute-start = (bf16[13,128,256]{2,1,0:T(8,128)(2,1)S(1)}, bf16[13,128,256]{2,1,0:T(8,128)(2,1)S(1)}, u32[]{:S(2)}, u32[]{:S(2)}) collective-permute-start(bf16[13,128,256]{2,1,0:T(8,128)(2,1)S(1)} %get-tuple-element.37), channel_id=1, source_target_pairs={{0,1},{1,0},{2,3},{3,2},{4,5},{5,4},{6,7},{7,6},{8,9},{9,8},{10,11... | collective-permute-start | bytes 2555912 | tf_op jit(solution)/shard_map/ppermute | solution.py:488
  27.7 6.1 %collective-permute-start.1 = (bf16[13,128,256]{2,1,0:T(8,128)(2,1)S(1)}, bf16[13,128,256]{2,1,0:T(8,128)(2,1)S(1)}, u32[]{:S(2)}, u32[]{:S(2)}) collective-permute-start(bf16[13,128,256]{2,1,0:T(8,128)(2,1)S(1)} %get-tuple-element.39), channel_id=1, source_target_pairs={{0,1},{1,0},{2,3},{3,2},{4,5},{5,4},{6,7},{7,6},{8,9},{9,8},{10,11... | collective-permute-start | bytes 2555912 | tf_op jit(solution)/shard_map/ppermute | solution.py:488
  28.2 5.5 %collective-permute-start.5 = (bf16[64,1024]{1,0:T(8,128)(2,1)S(1)}, bf16[64,1024]{1,0:T(8,128)(2,1)S(1)}, u32[]{:S(2)}, u32[]{:S(2)}) collective-permute-start(bf16[64,1024]{1,0:T(8,128)(2,1)S(1)} %convert_bitcast_fusion.refs_0_), channel_id=1, source_target_pairs={{0,2},{1,3},{2,0},{3,1},{4,6},{5,7},{6,4},{7,5},{8,10},{9,11},{10,... | collective-permute-start | bytes 393224 | tf_op jit(solution)/shard_map/ppermute | solution.py:488
  28.7 5.1 %collective-permute-start.7 = (bf16[4,64,1024]{2,1,0:T(8,128)(2,1)S(1)}, bf16[4,64,1024]{2,1,0:T(8,128)(2,1)S(1)}, u32[]{:S(2)}, u32[]{:S(2)}) collective-permute-start(bf16[4,64,1024]{2,1,0:T(8,128)(2,1)S(1)} %pack.2.rest_0_), channel_id=1, source_target_pairs={{0,1},{1,0},{2,3},{3,2},{4,5},{5,4},{6,7},{7,6},{8,9},{9,8},{10,11... | collective-permute-start | bytes 1572872 | tf_op jit(solution)/shard_map/ppermute | solution.py:488
  33.7 2.0 %collective-permute-start.8 = (bf16[4,64,1024]{2,1,0:T(8,128)(2,1)S(1)}, bf16[4,64,1024]{2,1,0:T(8,128)(2,1)S(1)}, u32[]{:S(2)}, u32[]{:S(2)}) collective-permute-start(bf16[4,64,1024]{2,1,0:T(8,128)(2,1)S(1)} %join.1.rest_1_), channel_id=1, source_target_pairs={{0,1},{1,0},{2,3},{3,2},{4,5},{5,4},{6,7},{7,6},{8,9},{9,8},{10,11... | collective-permute-start | bytes 1572872 | tf_op jit(solution)/shard_map/ppermute | solution.py:488
  46.5 15.0 %collective-permute-start.14 = (bf16[2,512,128]{2,1,0:T(8,128)(2,1)S(1)}, bf16[2,512,128]{2,1,0:T(8,128)(2,1)S(1)}, u32[]{:S(2)}, u32[]{:S(2)}) collective-permute-start(bf16[2,512,128]{2,1,0:T(8,128)(2,1)S(1)} %get-tuple-element.49), channel_id=1, source_target_pairs={{0,4},{1,5},{2,6},{3,7},{4,0},{5,1},{6,2},{7,3},{8,12},{9,13},{10,... | collective-permute-start | bytes 786440 | tf_op jit(solution)/shard_map/ppermute | solution.py:488
  48.6 22.5 %collective-permute-start.13 = (bf16[2,512,128]{2,1,0:T(8,128)(2,1)S(1)}, bf16[2,512,128]{2,1,0:T(8,128)(2,1)S(1)}, u32[]{:S(2)}, u32[]{:S(2)}) collective-permute-start(bf16[2,512,128]{2,1,0:T(8,128)(2,1)S(1)} %get-tuple-element.47), channel_id=1, source_target_pairs={{0,4},{1,5},{2,6},{3,7},{4,0},{5,1},{6,2},{7,3},{8,12},{9,13},{10,... | collective-permute-start | bytes 786440 | tf_op jit(solution)/shard_map/ppermute | solution.py:488
  48.7 13.5 %collective-permute-start.10 = (bf16[2,512,128]{2,1,0:T(8,128)(2,1)S(1)}, bf16[2,512,128]{2,1,0:T(8,128)(2,1)S(1)}, u32[]{:S(2)}, u32[]{:S(2)}) collective-permute-start(bf16[2,512,128]{2,1,0:T(8,128)(2,1)S(1)} %get-tuple-element.43), channel_id=1, source_target_pairs={{0,2},{1,3},{2,0},{3,1},{4,6},{5,7},{6,4},{7,5},{8,10},{9,11},{10,... | collective-permute-start | bytes 786440 | tf_op jit(solution)/shard_map/ppermute | solution.py:488
  49.2 23.6 %collective-permute-start.9 = (bf16[2,512,128]{2,1,0:T(8,128)(2,1)S(1)}, bf16[2,512,128]{2,1,0:T(8,128)(2,1)S(1)}, u32[]{:S(2)}, u32[]{:S(2)}) collective-permute-start(bf16[2,512,128]{2,1,0:T(8,128)(2,1)S(1)} %get-tuple-element.41), channel_id=1, source_target_pairs={{0,2},{1,3},{2,0},{3,1},{4,6},{5,7},{6,4},{7,5},{8,10},{9,11},{10,... | collective-permute-start | bytes 786440 | tf_op jit(solution)/shard_map/ppermute | solution.py:488
  61.6 9.5 %collective-permute-start.15 = (bf16[2,512,128]{2,1,0:T(8,128)(2,1)S(1)}, bf16[2,512,128]{2,1,0:T(8,128)(2,1)S(1)}, u32[]{:S(2)}, u32[]{:S(2)}) collective-permute-start(bf16[2,512,128]{2,1,0:T(8,128)(2,1)S(1)} %add_convert_fusion), channel_id=1, source_target_pairs={{0,2},{1,3},{2,0},{3,1},{4,6},{5,7},{6,4},{7,5},{8,10},{9,11},{10,... | collective-permute-start | bytes 786440 | tf_op jit(solution)/shard_map/ppermute | solution.py:488
  62.3 10.5 %collective-permute-start.11 = (bf16[2,512,128]{2,1,0:T(8,128)(2,1)S(1)}, bf16[2,512,128]{2,1,0:T(8,128)(2,1)S(1)}, u32[]{:S(2)}, u32[]{:S(2)}) collective-permute-start(bf16[2,512,128]{2,1,0:T(8,128)(2,1)S(1)} %add_convert_fusion.1), channel_id=1, source_target_pairs={{0,4},{1,5},{2,6},{3,7},{4,0},{5,1},{6,2},{7,3},{8,12},{9,13},{10,... | collective-permute-start | bytes 786440 | tf_op jit(solution)/shard_map/ppermute | solution.py:488
  69.5 6.7 %collective-permute-start.17 = (f32[512,128]{1,0:T(8,128)S(1)}, f32[512,128]{1,0:T(8,128)S(1)}, u32[]{:S(2)}, u32[]{:S(2)}) collective-permute-start(f32[512,128]{1,0:T(8,128)S(1)} %power.1.refs_4_), channel_id=1, source_target_pairs={{0,16},{16,0},{1,17},{17,1},{2,18},{18,2},{3,19},{19,3},{4,20},{20... | collective-permute-start | bytes 786440 | tf_op jit(solution)/shard_map/ppermute | solution.py:685
  71.2 11.2 %collective-permute-start.16 = (bf16[1,512,128]{2,1,0:T(8,128)(2,1)S(1)}, bf16[1,512,128]{2,1,0:T(8,128)(2,1)S(1)}, u32[]{:S(2)}, u32[]{:S(2)}) collective-permute-start(bf16[1,512,128]{2,1,0:T(8,128)(2,1)S(1)} %get-tuple-element.52), channel_id=1, source_target_pairs={{0,8},{1,9},{2,10},{3,11},{4,12},{5,13},{6,14},{7,15},{8,0},{9,1},... | collective-permute-start | bytes 393224 | tf_op jit(solution)/shard_map/ppermute | solution.py:488
  72.9 11.1 %collective-permute-start.12 = (bf16[1,512,128]{2,1,0:T(8,128)(2,1)S(1)}, bf16[1,512,128]{2,1,0:T(8,128)(2,1)S(1)}, u32[]{:S(2)}, u32[]{:S(2)}) collective-permute-start(bf16[1,512,128]{2,1,0:T(8,128)(2,1)S(1)} %get-tuple-element.46), channel_id=1, source_target_pairs={{0,8},{1,9},{2,10},{3,11},{4,12},{5,13},{6,14},{7,15},{8,0},{9,1},... | collective-permute-start | bytes 393224 | tf_op jit(solution)/shard_map/ppermute | solution.py:488
